TPU v7x, 256 devices: a whole 4x4x8 slice. The times are simulated.
256 devices in a mesh: rows: 64 (over x, z, core), cols: 4 (over y).
Axes of the slice: x: 4, y: 4, z: 8, core: 2. Of those that a mesh axis runs over, the one named last changes fastest.
Arguments:
- rhs: float32 [2, 32768, 512], P(None, 'rows', 'cols'), may hold values from -6 to 6
- diag_blocks: float32 [2, 512, 512], replicated, may hold values from -0.25 to 0.25
- multipliers: float32 [2, 2, 32768, 512], P(None, None, 'rows'), may hold values from -0.25 to 0.25
- pivots: int32 [1024], P('cols'), may hold values from 0 to 65535, as said below
Outputs:
- solved: float32 [2, 32768, 512], P(None, 'rows', 'cols')
Inputs may be any that keep to these rules, and one draw needn't show every extreme that they name: pivots[i] is i or a row at 1024 or beyond; the rows at 1024 or beyond that pivots names are all different, and at most 24 of them lie among the rows held by one index of rows, a number that some index reaches.
All inputs are finite; a program needn't handle non-finite values.
Results may differ from a plain program's by a relative error of at most 0.0001.
Values sent between devices are 32-bit elements; how exact they have to be, the bound alone decides.
No kernel may reach another device: no remote copies, remote signals or barrier semaphores. Data moves between devices by JAX's collectives and lax.ppermute only.
A program may use at most 64 MiB of HBM per device.

v0:
```python
import jax
import jax.numpy as jnp
from jax import lax
from jax.sharding import PartitionSpec as P


def sent_to_all(value, axis):
    copies = jnp.broadcast_to(value, (lax.axis_size(axis), *value.shape))
    return lax.all_to_all(copies, axis, split_axis=0, concat_axis=0, tiled=True)


def laid_out(parts, dim):
    parts = jnp.moveaxis(parts, 0, dim)
    lengths = parts.shape
    return parts.reshape(*lengths[:dim], lengths[dim] * lengths[dim + 1], *lengths[dim + 2 :])


def collect(value, axis, dim):
    parts = sent_to_all(value, axis)
    return laid_out(parts, dim)


def broadcast(block, axis, holder):
    block = jnp.where(lax.axis_index(axis) == holder, block, jnp.zeros_like(block))
    return lax.psum(block, axis)


def unit_lower_solve(factor, values):
    return lax.linalg.triangular_solve(
        factor, values, left_side=True, lower=True, unit_diagonal=True
    )


def product(left, right):
    return jnp.dot(left, right, precision=lax.Precision.HIGHEST, preferred_element_type=jnp.float32)


def shards(rhs, diag_blocks, multipliers, pivots):
    cycles, blk, columns = rhs.shape
    ranks = lax.axis_size("rows")
    mine = lax.axis_index("rows")
    stride = ranks * blk
    local_count = cycles * blk
    listed = collect(pivots, "cols", 0)
    count = listed.shape[0]
    places = jnp.arange(count, dtype=jnp.int32)
    fresh = listed >= count
    fresh_targets = jnp.where(fresh, listed, 0)
    flat = rhs.reshape(local_count, columns)

    def locate(global_row):
        inner = global_row % stride
        return (global_row // stride, inner // blk, inner % blk)

    def fetch(source_rows):
        src_cycle, src_owner, src_row = locate(source_rows)
        return (jnp.take(flat, src_cycle * blk + src_row, axis=0), src_owner)

    def landing_of(global_rows, keep):
        dst_cycle, dst_owner, dst_row = locate(global_rows)
        return jnp.where(keep & (dst_owner == mine), dst_cycle * blk + dst_row, local_count)

    panel_here, panel_src = fetch(listed)
    panel_contrib = jnp.where((panel_src == mine)[:, None], panel_here, 0.0)
    fresh_here, fresh_src = fetch(places)
    panel_landing = landing_of(places, places < count)
    fresh_landing = landing_of(fresh_targets, fresh)
    fresh_contrib = jnp.where((fresh & (fresh_src == mine))[:, None], fresh_here, 0.0)
    moved = lax.psum(jnp.concatenate([panel_contrib, fresh_contrib], axis=0), "rows")
    panel_moved = moved[:count]
    fresh_moved = moved[count:]
    permuted = (
        flat.at[panel_landing]
        .set(panel_moved, mode="drop")
        .at[fresh_landing]
        .set(fresh_moved, mode="drop")
    )
    lower = multipliers.reshape(multipliers.shape[0], local_count, blk)
    first_block = unit_lower_solve(diag_blocks[0], panel_moved[:blk])
    below = broadcast(lower[0, :blk], "rows", 1)
    started = panel_moved[blk : 2 * blk] - product(below, first_block)
    second_block = unit_lower_solve(diag_blocks[1], started)
    local_rows = jnp.arange(local_count, dtype=jnp.int32)
    global_rows = local_rows // blk * stride + mine * blk + local_rows % blk
    result = permuted
    result = jnp.where(
        (global_rows >= blk)[:, None], result - product(lower[0], first_block), result
    )
    result = jnp.where(
        (global_rows >= 2 * blk)[:, None], result - product(lower[1], second_block), result
    )
    padding = jnp.zeros(((cycles - 1) * blk, columns), jnp.float32)
    head_first = jnp.concatenate([first_block, padding], axis=0)
    head_second = jnp.concatenate([second_block, padding], axis=0)
    result = jnp.where((global_rows < blk)[:, None], head_first, result)
    result = jnp.where(
        ((global_rows >= blk) & (global_rows < 2 * blk))[:, None], head_second, result
    )
    return result.reshape(cycles, blk, columns)


def solution(mesh):
    placed = (P(None, "rows", "cols"), P(), P(None, None, "rows", None), P("cols"))
    return jax.shard_map(
        shards, mesh=mesh, in_specs=placed, out_specs=P(None, "rows", "cols"), check_vma=False
    )
```

profile of v0, /device:TPU:1, one launch (start us, length us, event | category | flops | bytes accessed | tf_op | source)
XLA Modules:
  0.0 261.4 jit_solution(636847592922003258)
XLA Ops:
  7.6 1.3 broadcast_in_dim.70
  8.9 5.0 %all-to-all-start = ((s32[4,1,256]{2,1,0:T(1,128)}), s32[4,1,256]{2,1,0:T(1,128)S(1)}, u32[]{:S(2)}, u32[]{:S(2)}) async-start(s32[4,1,256]{2,1,0:T(1,128)} %broadcast_in_dim.70), calls=%async_computation | async-start | bytes 8192 | tf_op jit(solution)/shard_map/all_to_all | solution.py:9
  13.9 1.7 convert_add_fusion.1
  15.7 7.6 %while.4 = (s32[]{:T(128)}, f32[512,512]{1,0:T(8,128)S(1)}, s32[4,2]{0,1:T(2,128)S(1)}, f32[4,128,128]{2,1,0:T(8,128)S(1)}, s32[]{:T(128)}) while((s32[]{:T(128)}, f32[512,512]{1,0:T(8,128)S(1)}, s32[4,2]{0,1:T(2,128)S(1)}, f32[4,128,128]{2,1,0:T(8,128)S(1)}, s32[]{:T(128)}) %tuple.45), condition=%wide.while_cond, body=%wide.while_body.sunk | while | flops 2 | bytes 131181 | solution.py:29
  16.3 1.3 bitcast_dynamic-update-slice_fusion.4
  18.2 1.3 bitcast_dynamic-update-slice_fusion.4
  23.4 2.7 %fusion.6 = f32[512,512]{1,0:T(8,128)} fusion(f32[2,1024,512]{2,1,0:T(8,128)} %bitcast.96, pred[]{:T(512)S(6)} %eq.57), kind=kLoop, calls=%fused_computation.26 | loop fusion | flops 262144 | bytes 2097153 | tf_op jit(solution)/shard_map/jit(_where)/select_n | solution.py:24
  26.1 2.8 %gather_fusion.1 = f32[1024,128]{1,0:T(8,128)S(1)} fusion(f32[1024,128]{1,0:T(8,128)S(1)} %bitcast.91, s32[1024]{0:T(1024)S(1)} %broadcast_clamp_fusion), kind=kCustom, calls=%fused_computation.1.clone | custom fusion | bytes 1052672 | tf_op jit(solution)/shard_map/jit(_take)/gather | solution.py:57
  28.9 4.0 %gather_fusion = f32[1024,128]{1,0:T(8,128)} fusion(f32[1024,128]{1,0:T(8,128)S(1)} %bitcast.92, s32[1024]{0:T(1024)S(1)} %broadcast_clamp_fusion.1), kind=kCustom, calls=%fused_computation.clone | custom fusion | bytes 1052672 | tf_op jit(solution)/shard_map/jit(_take)/gather | solution.py:57
  33.0 1.8 select_select_fusion
  35.9 8.0 %while.5 = (s32[]{:T(128)}, f32[512,512]{1,0:T(8,128)S(1)}, s32[4,2]{0,1:T(2,128)S(1)}, f32[4,128,128]{2,1,0:T(8,128)S(1)}, s32[]{:T(128)}) while((s32[]{:T(128)}, f32[512,512]{1,0:T(8,128)S(1)}, s32[4,2]{0,1:T(2,128)S(1)}, f32[4,128,128]{2,1,0:T(8,128)S(1)}, s32[]{:T(128)}) %tuple.54), condition=%wide.while_cond.clone, body=%wide.while_body.clone.sunk | while | flops 2 | bytes 131181 | solution.py:29
  36.6 1.4 bitcast_dynamic-update-slice_fusion.5
  38.6 1.4 bitcast_dynamic-update-slice_fusion.5
  40.6 1.4 bitcast_dynamic-update-slice_fusion.5
  42.6 1.4 bitcast_dynamic-update-slice_fusion.5
  44.0 39.3 %custom-call.4 = f32[4,128,128]{1,2,0:T(8,128)S(1)} custom-call(f32[4,128,128]{2,1,0:T(8,128)S(1)} %get-tuple-element.21), custom_call_target="InvertDiagBlocksLowerTriangular" | custom-call | tf_op jit(solution)/shard_map/triangular_solve/custom-call.1 | solution.py:29
  83.3 39.3 %custom-call.5 = f32[4,128,128]{1,2,0:T(8,128)S(1)} custom-call(f32[4,128,128]{2,1,0:T(8,128)S(1)} %get-tuple-element.22), custom_call_target="InvertDiagBlocksLowerTriangular" | custom-call | tf_op jit(solution)/shard_map/triangular_solve/custom-call.1 | solution.py:29
  122.7 4.2 %fusion.80 = (f32[1,2,512,512]{3,2,1,0:T(8,128)}, f32[1,2,512,512]{3,2,1,0:T(8,128)S(1)}) fusion(f32[2,2,512,512]{3,2,1,0:T(8,128)} %param.10), kind=kLoop, calls=%fused_computation.176 | loop fusion | bytes 8388608 | tf_op jit(solution)/shard_map/slice | solution.py:90
  127.0 102.8 %all-reduce.5.cloned.1.call-done = (f32[2048,128]{1,0:T(8,128)}, f32[512,512]{1,0:T(8,128)}) async-done(((f32[2048,128]{1,0:T(8,128)}, f32[512,512]{1,0:T(8,128)}), (f32[2048,128]{1,0:T(8,128)}, f32[512,512]{1,0:T(8,128)})) %all-reduce.5.cloned.1.call-update) | async-done | bytes 2097168 | tf_op jit(solution)/shard_map/psum | solution.py:69
  235.4 1.9 convolution_subtract_fusion
  242.1 3.9 %scatter_custom_fusion = f32[1024,128]{1,0:T(8,128)S(1)} fusion(f32[1024,128]{1,0:T(8,128)S(1)} %bitcast.93, s32[1024]{0:T(1024)S(1)} %bitcast.100, f32[2048,128]{1,0:T(8,128)} %get-tuple-element.39), kind=kCustom, calls=%fused_computation.34 | custom fusion | bytes 1048576 | tf_op jit(solution)/shard_map/scatter | solution.py:74
  246.0 3.7 %scatter_custom_fusion.1 = f32[1024,128]{1,0:T(8,128)S(1)} fusion(f32[1024,128]{1,0:T(8,128)S(1)} %scatter_custom_fusion, s32[1024]{0:T(1024)S(1)} %bitcast.99, f32[2048,128]{1,0:T(8,128)} %get-tuple-element.39), kind=kCustom, calls=%fused_computation.32 | custom fusion | bytes 1048576 | tf_op jit(solution)/shard_map/scatter | solution.py:76
  249.7 1.8 fusion.1
  251.6 3.0 %fusion.5 = f32[1024,128]{1,0:T(8,128)} fusion(f32[1024,128]{1,0:T(8,128)S(1)} %fusion.1, f32[512,128]{1,0:T(8,128)S(1)} %pad_maximum_fusion.2, f32[1024,512]{1,0:T(8,128)S(1)} %bitcast.95, f32[512,128]{1,0:T(8,128)S(1)} %pad_maximum_fusion.1, pred[1024]{0:T(1024)(128)(4,1)S(1)} %get-tuple-element.58, pred[1024]{0:T(1024)(128)(4,1)S(1)} %get-tuple-element.59, ...), kind=kOutput, calls=%fused_computation.17 | convolution fusion | flops 805830656 | bytes 3673088 | tf_op jit(solution)/shard_map/dot_general | solution.py:35
  (59 shorter events, 20.0 us)
Async XLA Ops:
  8.9 20.0 %all-to-all-start = ((s32[4,1,256]{2,1,0:T(1,128)}), s32[4,1,256]{2,1,0:T(1,128)S(1)}, u32[]{:S(2)}, u32[]{:S(2)}) async-start(s32[4,1,256]{2,1,0:T(1,128)} %broadcast_in_dim.70), calls=%async_computation | async-start | bytes 8192 | tf_op jit(solution)/shard_map/all_to_all | solution.py:9
  13.9 215.9 %all-reduce.5.cloned.1.call-start = ((), (), s32[]{:S(2)}) async-start(), calls=%async_computation.1 | async-start | bytes 4194304 | tf_op jit(solution)/shard_map/psum | solution.py:69
  23.3 11.5 %copy-start.2 = (f32[512,512]{1,0:T(8,128)}, f32[512,512]{1,0:T(8,128)S(1)}, u32[]{:S(2)}) copy-start(f32[512,512]{1,0:T(8,128)S(1)} %get-tuple-element.157) | copy-start | bytes 3145732
  44.0 78.7 %copy-start.1 = (f32[512,512]{1,0:T(8,128)}, f32[512,512]{1,0:T(8,128)S(1)}, u32[]{:S(2)}) copy-start(f32[512,512]{1,0:T(8,128)S(1)} %get-tuple-element.156) | copy-start | bytes 3145732
  229.8 5.7 %copy-start.3 = (f32[512,512]{1,0:T(8,128)S(1)}, f32[512,512]{1,0:T(8,128)}, u32[]{:S(2)}) copy-start(f32[512,512]{1,0:T(8,128)} %get-tuple-element.40) | copy-start | bytes 3145732
  249.7 1.8 copy-start
Sparse Core Ops, SparseCore 0:
  36.0 193.6 all-reduce.4
where the time goes:
time: 263 us; the launch traced here: 261 us
  waiting for transfers between devices  103 us (39%)
  other arithmetic  86.2 us (33%)
  local copies, waits for them, and re-layouts  36.6 us (14%)
  matrix products  16.9 us (6%)
  between operations  13.7 us (5%)
  starting transfers between devices  5 us (2%)
    psum x1, waiting for transfers between devices, shards(): lax.psum(jnp.concatenate([panel_contrib, fresh_contrib], axis=0), 'rows')  103 us
    another operation x7, other arithmetic, unit_lower_solve(): lax.linalg.triangular_solve(factor, values, left_side=True, lower=True, u...  80.4 us
    another operation x27, local copies, waits for them, and re-layouts, unit_lower_solve(): lax.linalg.triangular_solve(factor, values, left_side=True, lower=True, u...  15.5 us
    another operation x14, matrix products, unit_lower_solve(): lax.linalg.triangular_solve(factor, values, left_side=True, lower=True, u...  10.2 us
    scatter x2, local copies, waits for them, and re-layouts, shards(): permuted = flat.at[panel_landing].set(panel_moved, mode='drop').at[fresh_...  7.66 us
    gather x2, local copies, waits for them, and re-layouts, fetch(): return (jnp.take(flat, src_cycle * blk + src_row, axis=0), src_owner)  6.84 us
    dot_general x3, matrix products, product(): jnp.dot(left, right, precision=lax.Precision.HIGHEST, preferred_element_t...  6.77 us
  transfers between devices with their start and end apart: 2, of which 1 were waited for; matrix products, arithmetic and copies ran while one was open for 40% of the time, Pallas kernels for 0%

commit v1 on v0

v1 whole, which is shorter than its diff:
```python
import functools

import jax
import jax.numpy as jnp
from jax import lax
from jax.experimental import pallas as pl
from jax.experimental.pallas import tpu as pltpu
from jax.sharding import PartitionSpec as P

BLK = 512
COLS = 128
MOVE = 24
CHIPS = 32
PLANES = 4
HIGHEST = lax.Precision.HIGHEST
GROUPS = [[2 * chip + core for chip in range(CHIPS)] for core in range(2)]
SWAP = [(device, device ^ 1) for device in range(2 * CHIPS)]
NORTH_TO_SOUTH = [(2 * chip + 1, 2 * chip) for chip in range(CHIPS)]
VMEM = pl.BlockSpec(memory_space=pltpu.VMEM)
SMEM = pl.BlockSpec(memory_space=pltpu.SMEM)
HBM = pl.BlockSpec(memory_space=pl.ANY)


def across_planes(step):
    pairs = []
    for chip in range(CHIPS):
        for plane in range(PLANES):
            device = (2 * chip + 1) * PLANES
            pairs.append((device + plane, device + (plane + step) % PLANES))
    return pairs


def halves(value):
    high = value.astype(jnp.bfloat16)
    return high, (value - high.astype(jnp.float32)).astype(jnp.bfloat16)


def dot(left, right):
    return jnp.dot(left, right, preferred_element_type=jnp.float32)


def product(left_high, left_low, right):
    high, low = halves(right)
    width = right.shape[1]
    both = dot(left_high, jnp.concatenate([high, low], axis=1))
    return both[:, :width] + both[:, width:] + dot(left_low, high)


def stage_kernel(rhs, multipliers, out, sems):
    plane = lax.axis_index("cols")
    copies = [pltpu.make_async_copy(rhs.at[0], out.at[:, 0:16, :], sems.at[0])]
    for part in range(4):
        copies.append(
            pltpu.make_async_copy(
                multipliers.at[0, 0, plane, :, :, pl.ds(128 * part, 128)],
                out.at[pl.ds(8 * part, 8), 16:32, :],
                sems.at[1 + part],
            )
        )
    for copy in copies:
        copy.start()
    for copy in copies:
        copy.wait()


def stage(rhs, multipliers):
    return pl.pallas_call(
        stage_kernel,
        name="stage",
        out_shape=jax.ShapeDtypeStruct((CHIPS, 32, COLS), jnp.float32),
        in_specs=[HBM, HBM],
        out_specs=VMEM,
        scratch_shapes=[pltpu.SemaphoreType.DMA((5,))],
    )(
        rhs.reshape(2, CHIPS, 16, COLS),
        multipliers.reshape(2, 2, PLANES, 8, 16, BLK),
    )


def choose_kernel(pivots, rhs, sent, slots, lists):
    mine = lax.axis_index("rows")
    core = mine % 2
    lane = lax.broadcasted_iota(jnp.int32, (64, 128), 1)
    sub = lax.broadcasted_iota(jnp.int32, (64, 128), 0)
    row = lax.broadcasted_iota(jnp.int32, (128, 128), 0)
    col = lax.broadcasted_iota(jnp.int32, (128, 128), 1)
    earlier = jnp.where(row < col, 1.0, 0.0).astype(jnp.bfloat16)
    carry = jnp.zeros((64, 1), jnp.float32)
    source = jnp.zeros((64, 1), jnp.int32)
    place = jnp.zeros((64, 1), jnp.int32)
    for piece in range(8):
        target = pivots[piece : piece + 1, :]
        owner = lax.shift_right_logical(target, 9) & 63
        moved = target >= 2 * BLK
        hit = (sub == owner) & moved
        ones = jnp.where(hit, 1.0, 0.0)
        before = dot(ones.astype(jnp.bfloat16), earlier) + carry
        carry = carry + jnp.sum(ones, axis=1, keepdims=True)
        rank = jnp.sum(jnp.where(hit, before, 0.0), axis=0, keepdims=True).astype(jnp.int32)
        here = lane[:1] + 128 * piece
        far = jnp.where(owner % 2 == core, 0, CHIPS * MOVE) + (owner // 2) * MOVE + rank
        slots[piece : piece + 1, :] = jnp.where(moved, 2 * BLK + far, here)
        local = lax.shift_right_logical(target, 15) * BLK + (target & (BLK - 1))
        taken = (sub == rank) & moved & (owner == mine)
        source = source + jnp.sum(jnp.where(taken, local + 1, 0), axis=1, keepdims=True)
        place = place + jnp.sum(jnp.where(taken, here + 1, 0), axis=1, keepdims=True)
    source = source[:32] - 1
    place = place[:32] - 1
    lists[...] = jnp.where(lane[:32] == 0, source, place)
    wide = lax.broadcasted_iota(jnp.int32, (32, 2 * BLK), 1)
    pick = jnp.where(wide == source, 1.0, 0.0)
    rows = jnp.dot(pick, rhs[...], precision=HIGHEST, preferred_element_type=jnp.float32)
    sent[...] = jnp.broadcast_to(rows[None, :MOVE], (CHIPS, MOVE, COLS))


def choose(pivots, flat):
    return pl.pallas_call(
        choose_kernel,
        name="choose",
        out_shape=(
            jax.ShapeDtypeStruct((CHIPS, MOVE, COLS), jnp.float32),
            jax.ShapeDtypeStruct((8, 128), jnp.int32),
            jax.ShapeDtypeStruct((32, 128), jnp.int32),
        ),
        in_specs=[VMEM, VMEM],
        out_specs=(VMEM, VMEM, VMEM),
    )(pivots, flat)


def invert_kernel(diag, multipliers, inv_high, inv_low, low_high, low_low, work):
    row = lax.broadcasted_iota(jnp.int32, (128, 128), 0)
    col = lax.broadcasted_iota(jnp.int32, (128, 128), 1)

    def square(left, right):
        return jnp.dot(left, right, precision=HIGHEST, preferred_element_type=jnp.float32)

    def block(panel, i, j):
        return diag[panel, 128 * i : 128 * (i + 1), 128 * j : 128 * (j + 1)]

    for b in range(8):
        pair = (row // 2 == col // 2) & (row > col)
        unit = jnp.where(row == col, 1.0, 0.0)
        work[b] = unit - jnp.where(pair, block(b // 4, b % 4, b % 4), 0.0)

    def level(step, carry):
        shift = step + 1
        near = (lax.shift_right_logical(row, shift) % 2 == 1) & (
            lax.shift_right_logical(col, shift) == lax.shift_right_logical(row, shift) - 1
        )
        firsts = []
        for b in range(8):
            part = jnp.where(near, block(b // 4, b % 4, b % 4), 0.0)
            firsts.append(square(part, work[b]))
        for b in range(8):
            work[b] = work[b] - square(work[b], firsts[b])
        return carry

    lax.fori_loop(0, 6, level, 0)

    def put(panel, i, j, value):
        high, low = halves(value)
        rows = slice(i, i + value.shape[0])
        cols = slice(j, j + value.shape[1])
        inv_high[panel, rows, cols] = high
        inv_low[panel, rows, cols] = low

    zero = jnp.zeros((256, 256), jnp.bfloat16)
    for panel in range(2):
        tops = []
        for half in range(2):
            first = work[4 * panel + 2 * half]
            second = work[4 * panel + 2 * half + 1]
            below = -square(second, square(block(panel, 2 * half + 1, 2 * half), first))
            top = jnp.concatenate([first, jnp.zeros((128, 128), jnp.float32)], axis=1)
            bottom = jnp.concatenate([below, second], axis=1)
            whole = jnp.concatenate([top, bottom], axis=0)
            tops.append(whole)
            put(panel, 256 * half, 256 * half, whole)
        corner = -square(tops[1], square(diag[panel, 256:512, 0:256], tops[0]))
        put(panel, 256, 0, corner)
        inv_high[panel, 0:256, 256:512] = zero
        inv_low[panel, 0:256, 256:512] = zero
    for panel in range(2):
        for cycle in range(2):
            high, low = halves(multipliers[panel, cycle])
            rows = slice(BLK * cycle, BLK * (cycle + 1))
            cols = slice(BLK * panel, BLK * (panel + 1))
            low_high[rows, cols] = high
            low_low[rows, cols] = low


def invert(diag, multipliers):
    return pl.pallas_call(
        invert_kernel,
        name="invert",
        out_shape=(
            jax.ShapeDtypeStruct((2, BLK, BLK), jnp.bfloat16),
            jax.ShapeDtypeStruct((2, BLK, BLK), jnp.bfloat16),
            jax.ShapeDtypeStruct((2 * BLK, 2 * BLK), jnp.bfloat16),
            jax.ShapeDtypeStruct((2 * BLK, 2 * BLK), jnp.bfloat16),
        ),
        in_specs=[VMEM, VMEM],
        out_specs=(VMEM, VMEM, VMEM, VMEM),
        scratch_shapes=[pltpu.VMEM((8, 128, 128), jnp.float32)],
        cost_estimate=pl.CostEstimate(
            flops=4 * 10**9, bytes_accessed=12 * 2**20, transcendentals=0
        ),
    )(diag, multipliers)


def finish_kernel(
    slots, lists, rhs, near, near_other, far, far_other,
    p0, p1, p2, p3, inv_high, inv_low, low_high, low_low,
    out, pool, panel, l21_high, l21_low,
):
    mine = lax.axis_index("rows")
    plane = lax.axis_index("cols")
    core = mine % 2
    own = pl.multiple_of(core * BLK, BLK)
    other = pl.multiple_of(BLK - core * BLK, BLK)
    pool[pl.ds(own, BLK), :] = near[:, :16, :].reshape(BLK, COLS)
    pool[pl.ds(other, BLK), :] = near_other[...].reshape(BLK, COLS)
    pool[2 * BLK : 2 * BLK + CHIPS * MOVE, :] = far[...].reshape(CHIPS * MOVE, COLS)
    pool[2 * BLK + CHIPS * MOVE :, :] = far_other[...].reshape(CHIPS * MOVE, COLS)

    def gather(i, carry):
        for k in range(8):
            spot = i * 8 + k
            panel[pl.ds(spot, 1), :] = pool[pl.ds(slots[spot], 1), :]
        return carry

    lax.fori_loop(0, 2 * BLK // 8, gather, 0)
    for step, pieces in enumerate((p0, p1, p2, p3)):
        base = pl.multiple_of(((plane - step) % PLANES) * 128, 128)
        for part in range(4):
            value = pieces[8 * part : 8 * (part + 1)].reshape(128, 128)
            high, low = halves(value)
            l21_high[pl.ds(base, 128), 128 * part : 128 * (part + 1)] = high
            l21_low[pl.ds(base, 128), 128 * part : 128 * (part + 1)] = low
    first = product(inv_high[0], inv_low[0], panel[:BLK, :])
    rest = panel[BLK:, :] - product(l21_high[...], l21_low[...], first)
    second = product(inv_high[1], inv_low[1], rest)
    solved = jnp.concatenate([first, second], axis=0)
    source = lists[:, 0:1]
    place = lists[:, 1:2]
    wide = lax.broadcasted_iota(jnp.int32, (32, 2 * BLK), 1)
    at_source = jnp.where(wide == source, 1.0, 0.0)
    at_place = jnp.where(wide == place, 1.0, 0.0)
    fresh = jnp.dot(
        at_place, pool[: 2 * BLK, :], precision=HIGHEST, preferred_element_type=jnp.float32
    )
    spread = (((0,), (0,)), ((), ()))
    landed = lax.dot_general(
        at_source, fresh, spread, precision=HIGHEST, preferred_element_type=jnp.float32
    )
    hit = lax.dot_general(
        at_source, jnp.ones((32, COLS), jnp.float32), spread,
        preferred_element_type=jnp.float32,
    )
    base = jnp.where(hit > 0.5, landed, rhs[...])
    result = base - product(low_high[...], low_low[...], solved)
    out[...] = result

    @pl.when(mine == 0)
    def _():
        out[:BLK, :] = first

    @pl.when(mine == 1)
    def _():
        out[:BLK, :] = second


def finish(*operands):
    return pl.pallas_call(
        finish_kernel,
        name="finish",
        out_shape=jax.ShapeDtypeStruct((2 * BLK, COLS), jnp.float32),
        in_specs=[SMEM] + [VMEM] * 14,
        out_specs=VMEM,
        scratch_shapes=[
            pltpu.VMEM((2 * BLK + 2 * CHIPS * MOVE, COLS), jnp.float32),
            pltpu.VMEM((2 * BLK, COLS), jnp.float32),
            pltpu.VMEM((BLK, BLK), jnp.bfloat16),
            pltpu.VMEM((BLK, BLK), jnp.bfloat16),
        ],
    )(*operands)


def exchange(value):
    return lax.all_to_all(value, "rows", 0, 0, axis_index_groups=GROUPS, tiled=True)


def shards(rhs, diag_blocks, multipliers, pivots):
    cycles, blk, columns = rhs.shape
    flat = rhs.reshape(cycles * blk, columns)
    core = lax.axis_index("rows") % 2
    listed = lax.all_to_all(
        jnp.broadcast_to(pivots.reshape(1, 2, 128), (PLANES, 2, 128)),
        "cols", 0, 0, tiled=True,
    ).reshape(8, 128)
    piece = exchange(stage(rhs, multipliers))[0]
    near = exchange(jnp.broadcast_to(piece[None], (CHIPS, 32, COLS)))
    sent, slots, lists = choose(listed, flat)
    far = exchange(sent)
    inverses = invert(diag_blocks, multipliers)
    near_other = lax.ppermute(near[:, :16], "rows", SWAP)
    quarter = near[:, 16:]
    quarters = [quarter] + [
        lax.ppermute(quarter, ("rows", "cols"), across_planes(step)) for step in range(1, 4)
    ]
    down = [lax.ppermute(q, "rows", NORTH_TO_SOUTH) for q in quarters]
    pieces = [jnp.where(core == 1, q, d) for q, d in zip(quarters, down)]
    far_other = lax.ppermute(far, "rows", SWAP)
    solved = finish(
        slots.reshape(1024), lists, flat, near, near_other, far, far_other,
        *pieces, *inverses,
    )
    return solved.reshape(cycles, blk, columns)


def solution(mesh):
    placed = (P(None, "rows", "cols"), P(), P(None, None, "rows", None), P("cols"))
    return jax.shard_map(
        shards, mesh=mesh, in_specs=placed, out_specs=P(None, "rows", "cols"), check_vma=False
    )
```

time: 263 us -> 112 us (0.43)
  waiting for transfers between devices: 103 us -> 13.6 us
  other arithmetic: 86.2 us -> 3.01 us
  local copies, waits for them, and re-layouts: 36.6 us -> 2.34 us
  starting transfers between devices: 5 us -> 36.8 us
  Pallas kernels: 0 us -> 28.7 us
  blocking collectives: 0 us -> 26.4 us
  matrix products: 16.9 us -> 0 us
  between operations: 13.7 us -> 0.18 us
    psum x1 -> x0, waiting for transfers between devices: 103 us -> none  [shards(): lax.psum(jnp.concatenate([panel_contrib, fresh_contrib], axis=0), 'rows')]
    another operation x7 -> x0, other arithmetic: 80.4 us -> none  [unit_lower_solve(): lax.linalg.triangular_solve(factor, values, left_side=True, lower=True, u...]
    pallas_call x0 -> x4, Pallas kernels: none -> 28.7 us  [the longest x1 14.8 us: invert(): pl.pallas_call(invert_kernel, name='invert', out_shape=(jax.ShapeDtypeStr...]
    all_to_all x0 -> x1, blocking collectives: none -> 26.4 us  [exchange(): lax.all_to_all(value, 'rows', 0, 0, axis_index_groups=GROUPS, tiled=True)]
    ppermute x0 -> x9, starting transfers between devices: none -> 17.3 us  [the longest x3 9.69 us: shards(): lax.ppermute(quarter, ('rows', 'cols'), across_planes(step))]
    another operation x27 -> x0, local copies, waits for them, and re-layouts: 15.5 us -> none  [unit_lower_solve(): lax.linalg.triangular_solve(factor, values, left_side=True, lower=True, u...]
    all_to_all x1 -> x3, starting transfers between devices: 5 us -> 19.5 us  [the longest x2 15.3 us: exchange(): lax.all_to_all(value, 'rows', 0, 0, axis_index_groups=GROUPS, tiled=True)]
    all_to_all x1 -> x3, waiting for transfers between devices: 0.01 us -> 13.5 us  [the longest x2 9.38 us: exchange(): lax.all_to_all(value, 'rows', 0, 0, axis_index_groups=GROUPS, tiled=True)]
  transfers between devices with their start and end apart: 2 -> 12, of which waited for: 1 -> 2; matrix products, arithmetic and copies ran while one was open for 40% -> 3% of each run, Pallas kernels for 0% -> 16%
where the time goes in v1:
time: 112 us; the launch traced here: 111 us
  starting transfers between devices  36.8 us (33%)
  Pallas kernels  28.7 us (26%)
  blocking collectives  26.4 us (24%)
  waiting for transfers between devices  13.6 us (12%)
  other arithmetic  3.01 us (3%)
  local copies, waits for them, and re-layouts  2.34 us (2%)
    all_to_all x1, blocking collectives, exchange(): lax.all_to_all(value, 'rows', 0, 0, axis_index_groups=GROUPS, tiled=True)  26.4 us
    all_to_all x2, starting transfers between devices, exchange(): lax.all_to_all(value, 'rows', 0, 0, axis_index_groups=GROUPS, tiled=True)  15.3 us
    pallas_call x1, Pallas kernels, invert(): pl.pallas_call(invert_kernel, name='invert', out_shape=(jax.ShapeDtypeStr...  14.8 us
    ppermute x3, starting transfers between devices, shards(): lax.ppermute(quarter, ('rows', 'cols'), across_planes(step))  9.69 us
    pallas_call x1, Pallas kernels, finish(): pl.pallas_call(finish_kernel, name='finish', out_shape=jax.ShapeDtypeStru...  9.52 us
    all_to_all x2, waiting for transfers between devices, exchange(): lax.all_to_all(value, 'rows', 0, 0, axis_index_groups=GROUPS, tiled=True)  9.38 us
    ppermute x4, starting transfers between devices, shards(): down = [lax.ppermute(q, 'rows', NORTH_TO_SOUTH) for q in quarters]  7.61 us
    all_to_all x1, starting transfers between devices, shards(): lax.all_to_all(jnp.broadcast_to(pivots.reshape(1, 2, 128), (PLANES, 2, 12...  4.18 us
  transfers between devices with their start and end apart: 12, of which 2 were waited for; matrix products, arithmetic and copies ran while one was open for 3% of the time, Pallas kernels for 16%

profile of v1, /device:TPU:1, one launch (start us, length us, event | category | flops | bytes accessed | tf_op | source)
XLA Modules:
  0.0 111.0 jit_solution(15087963318331095350)
XLA Ops:
  0.0 1.9 %stage.1 = f32[32,32,128]{2,1,0:T(8,128)} custom-call(f32[2,32,16,128]{3,2,1,0:T(8,128)} %bitcast.9, f32[2,2,4,8,16,512]{5,4,3,2,1,0:T(8,128)} %bitcast.12), custom_call_target="tpu_custom_call" | custom-call | tf_op jit(solution)/shard_map/stage/pallas_call | solution.py:67
  1.9 26.4 %all_to_all.20 = f32[32,32,128]{2,1,0:T(8,128)S(1)} all-to-all(f32[32,32,128]{2,1,0:T(8,128)} %stage.1), channel_id=1, replica_groups={{0,8,16,24,32,40,48,56,64,72,80,88,96,104,112,120,128,136,144,152,160,1..., dimensions={0} | all-to-all | bytes 1048576 | tf_op jit(solution)/shard_map/all_to_all | solution.py:290
  28.3 0.6 broadcast_in_dim.15
  28.9 4.2 %all-to-all-start = ((s32[4,2,128]{2,1,0:T(2,128)}), s32[4,2,128]{2,1,0:T(2,128)S(1)}, u32[]{:S(2)}, u32[]{:S(2)}) async-start(s32[4,2,128]{2,1,0:T(2,128)} %broadcast_in_dim.15), calls=%async_computation | async-start | bytes 8192 | tf_op jit(solution)/shard_map/all_to_all | solution.py:297
  33.1 4.1 %all-to-all-done = s32[4,2,128]{2,1,0:T(2,128)S(1)} async-done(((s32[4,2,128]{2,1,0:T(2,128)}), s32[4,2,128]{2,1,0:T(2,128)S(1)}, u32[]{:S(2)}, u32[]{:S(2)}) %all-to-all-start) | async-done | bytes 4128 | tf_op jit(solution)/shard_map/all_to_all | solution.py:297
  37.2 0.9 broadcast_in_dim.17
  38.1 7.3 %all-to-all-start.2 = ((f32[32,32,128]{2,1,0:T(8,128)}), f32[32,32,128]{2,1,0:T(8,128)S(1)}, u32[]{:S(2)}, u32[]{:S(2)}) async-start(f32[32,32,128]{2,1,0:T(8,128)} %broadcast_in_dim.17), calls=%async_computation.2 | async-start | bytes 1048576 | tf_op jit(solution)/shard_map/all_to_all | solution.py:290
  45.3 2.5 %choose.1 = (f32[32,24,128]{2,1,0:T(8,128)}, s32[8,128]{1,0:T(8,128)}, s32[32,128]{1,0:T(8,128)}) custom-call(s32[8,128]{1,0:T(8,128)} %bitcast.13, f32[1024,128]{1,0:T(8,128)} %bitcast.10), custom_call_target="tpu_custom_call" | custom-call | tf_op jit(solution)/shard_map/choose/pallas_call | solution.py:117
  47.8 9.4 %all-to-all-done.2.near = f32[32,32,128]{2,1,0:T(8,128)S(1)} async-done(((f32[32,32,128]{2,1,0:T(8,128)}), f32[32,32,128]{2,1,0:T(8,128)S(1)}, u32[]{:S(2)}, u32[]{:S(2)}) %all-to-all-start.2) | async-done | bytes 524320 | tf_op jit(solution)/shard_map/all_to_all | solution.py:290
  57.2 8.1 %all-to-all-start.3 = ((f32[32,24,128]{2,1,0:T(8,128)}), f32[32,24,128]{2,1,0:T(8,128)S(1)}, u32[]{:S(2)}, u32[]{:S(2)}) async-start(f32[32,24,128]{2,1,0:T(8,128)} %get-tuple-element.14), calls=%async_computation.3 | async-start | bytes 786432 | tf_op jit(solution)/shard_map/all_to_all | solution.py:290
  65.3 3.2 %collective-permute-start.5 = (f32[32,16,128]{2,1,0:T(8,128)S(1)}, f32[32,16,128]{2,1,0:T(8,128)S(1)}, u32[]{:S(2)}, u32[]{:S(2)}) collective-permute-start(f32[32,16,128]{2,1,0:T(8,128)S(1)} %slice.14), channel_id=1, source_target_pairs={{4,6},{5,7},{6,4},{7,5},{12,14},{13,15},{14,12},{15,13},{20,22},{2... | collective-permute-start | bytes 786440 | tf_op jit(solution)/shard_map/ppermute | solution.py:309
  68.5 2.1 %collective-permute-start.3 = (f32[32,16,128]{2,1,0:T(8,128)S(1)}, f32[32,16,128]{2,1,0:T(8,128)S(1)}, u32[]{:S(2)}, u32[]{:S(2)}) collective-permute-start(f32[32,16,128]{2,1,0:T(8,128)S(1)} %slice.14), channel_id=1, source_target_pairs={{4,5},{5,6},{6,7},{7,4},{12,13},{13,14},{14,15},{15,12},{20,21},{2... | collective-permute-start | bytes 786440 | tf_op jit(solution)/shard_map/ppermute | solution.py:309
  70.6 4.4 %collective-permute-start.7 = (f32[32,16,128]{2,1,0:T(8,128)S(1)}, f32[32,16,128]{2,1,0:T(8,128)S(1)}, u32[]{:S(2)}, u32[]{:S(2)}) collective-permute-start(f32[32,16,128]{2,1,0:T(8,128)S(1)} %slice.14), channel_id=1, source_target_pairs={{4,7},{5,4},{6,5},{7,6},{12,15},{13,12},{14,13},{15,14},{20,23},{2... | collective-permute-start | bytes 786440 | tf_op jit(solution)/shard_map/ppermute | solution.py:309
  75.0 1.3 %collective-permute-start.2 = (f32[32,16,128]{2,1,0:T(8,128)S(1)}, f32[32,16,128]{2,1,0:T(8,128)S(1)}, u32[]{:S(2)}, u32[]{:S(2)}) collective-permute-start(f32[32,16,128]{2,1,0:T(8,128)S(1)} %slice.14), channel_id=1, source_target_pairs={{4,0},{12,8},{20,16},{28,24},{36,32},{44,40},{52,48},{60,56},{68,6... | collective-permute-start | bytes 786440 | tf_op jit(solution)/shard_map/ppermute | solution.py:311
  76.4 1.3 %collective-permute-start.6 = (f32[32,16,128]{2,1,0:T(8,128)S(1)}, f32[32,16,128]{2,1,0:T(8,128)S(1)}, u32[]{:S(2)}, u32[]{:S(2)}) collective-permute-start(f32[32,16,128]{2,1,0:T(8,128)S(1)} %collective-permute-done.5), channel_id=1, source_target_pairs={{4,0},{12,8},{20,16},{28,24},{36,32},{44,40},{52,48},{60,56},{68,6... | collective-permute-start | bytes 786440 | tf_op jit(solution)/shard_map/ppermute | solution.py:311
  77.7 14.8 %invert.1 = (bf16[2,512,512]{2,1,0:T(8,128)(2,1)}, bf16[2,512,512]{2,1,0:T(8,128)(2,1)}, bf16[1024,1024]{1,0:T(8,128)(2,1)}, bf16[1024,1024]{1,0:T(8,128)(2,1)}) custom-call(f32[2,512,512]{2,1,0:T(8,128)} %diag.1, f32[2,2,512,512]{3,2,1,0:T(8,128)} %multipliers.1), custom_call_target="tpu_custom_call" | custom-call | flops 4000000000 | bytes 12582912 | tf_op jit(solution)/shard_map/invert/pallas_call | solution.py:193
  92.5 2.4 %collective-permute-start.4 = (f32[32,16,128]{2,1,0:T(8,128)S(1)}, f32[32,16,128]{2,1,0:T(8,128)S(1)}, u32[]{:S(2)}, u32[]{:S(2)}) collective-permute-start(f32[32,16,128]{2,1,0:T(8,128)S(1)} %collective-permute-done.3), channel_id=1, source_target_pairs={{4,0},{12,8},{20,16},{28,24},{36,32},{44,40},{52,48},{60,56},{68,6... | collective-permute-start | bytes 786440 | tf_op jit(solution)/shard_map/ppermute | solution.py:311
  94.9 0.8 broadcast_select_fusion.3
  95.7 2.6 %collective-permute-start.8 = (f32[32,16,128]{2,1,0:T(8,128)S(1)}, f32[32,16,128]{2,1,0:T(8,128)S(1)}, u32[]{:S(2)}, u32[]{:S(2)}) collective-permute-start(f32[32,16,128]{2,1,0:T(8,128)S(1)} %collective-permute-done.7), channel_id=1, source_target_pairs={{4,0},{12,8},{20,16},{28,24},{36,32},{44,40},{52,48},{60,56},{68,6... | collective-permute-start | bytes 786440 | tf_op jit(solution)/shard_map/ppermute | solution.py:311
  98.3 0.7 broadcast_select_fusion.1.p2
  99.0 0.8 broadcast_select_fusion.2.p1
  99.8 0.8 broadcast_select_fusion.p3
  100.6 0.7 copy-done.2
  101.4 9.5 %finish.1 = f32[1024,128]{1,0:T(8,128)} custom-call(s32[1024]{0:T(1024)} %bitcast.14, s32[32,128]{1,0:T(8,128)} %get-tuple-element.13.lists, f32[1024,128]{1,0:T(8,128)} %bitcast.11, f32[32,32,128]{2,1,0:T(8,128)} %copy-done, f32[32,16,128]{2,1,0:T(8,128)} %copy-done.3, f32[32,24,128]{2,1,0:T(8,128)} %copy-done.1, f32[32,24,128]{2,1,0:T(8,128)} %copy-done.2, ...), custom_call_target="tpu_custom_call" | custom-call | tf_op jit(solution)/shard_map/finish/pallas_call | solution.py:274
  (25 shorter events, 0.2 us)
Async XLA Ops:
  0.0 28.3 %copy-start.5 = (s32[256]{0:T(256)S(1)}, s32[256]{0:T(256)}, u32[]{:S(2)}) copy-start(s32[256]{0:T(256)} %param.7) | copy-start | bytes 3076
  28.9 8.3 %all-to-all-start = ((s32[4,2,128]{2,1,0:T(2,128)}), s32[4,2,128]{2,1,0:T(2,128)S(1)}, u32[]{:S(2)}, u32[]{:S(2)}) async-start(s32[4,2,128]{2,1,0:T(2,128)} %broadcast_in_dim.15), calls=%async_computation | async-start | bytes 8192 | tf_op jit(solution)/shard_map/all_to_all | solution.py:297
  37.2 8.1 %copy-start.4 = (s32[4,2,128]{2,1,0:T(2,128)}, s32[4,2,128]{2,1,0:T(2,128)S(1)}, u32[]{:S(2)}) copy-start(s32[4,2,128]{2,1,0:T(2,128)S(1)} %all-to-all-done) | copy-start | bytes 12292
  38.1 19.2 %all-to-all-start.2 = ((f32[32,32,128]{2,1,0:T(8,128)}), f32[32,32,128]{2,1,0:T(8,128)S(1)}, u32[]{:S(2)}, u32[]{:S(2)}) async-start(f32[32,32,128]{2,1,0:T(8,128)} %broadcast_in_dim.17), calls=%async_computation.2 | async-start | bytes 1048576 | tf_op jit(solution)/shard_map/all_to_all | solution.py:290
  57.2 37.7 %copy-start = (f32[32,32,128]{2,1,0:T(8,128)}, f32[32,32,128]{2,1,0:T(8,128)S(1)}, u32[]{:S(2)}) copy-start(f32[32,32,128]{2,1,0:T(8,128)S(1)} %all-to-all-done.2.near) | copy-start | bytes 1572868
  57.2 35.3 %all-to-all-start.3 = ((f32[32,24,128]{2,1,0:T(8,128)}), f32[32,24,128]{2,1,0:T(8,128)S(1)}, u32[]{:S(2)}, u32[]{:S(2)}) async-start(f32[32,24,128]{2,1,0:T(8,128)} %get-tuple-element.14), calls=%async_computation.3 | async-start | bytes 786432 | tf_op jit(solution)/shard_map/all_to_all | solution.py:290
  65.3 11.0 %collective-permute-start.5 = (f32[32,16,128]{2,1,0:T(8,128)S(1)}, f32[32,16,128]{2,1,0:T(8,128)S(1)}, u32[]{:S(2)}, u32[]{:S(2)}) collective-permute-start(f32[32,16,128]{2,1,0:T(8,128)S(1)} %slice.14), channel_id=1, source_target_pairs={{4,6},{5,7},{6,4},{7,5},{12,14},{13,15},{14,12},{15,13},{20,22},{2... | collective-permute-start | bytes 786440 | tf_op jit(solution)/shard_map/ppermute | solution.py:309
  68.5 23.9 %collective-permute-start.3 = (f32[32,16,128]{2,1,0:T(8,128)S(1)}, f32[32,16,128]{2,1,0:T(8,128)S(1)}, u32[]{:S(2)}, u32[]{:S(2)}) collective-permute-start(f32[32,16,128]{2,1,0:T(8,128)S(1)} %slice.14), channel_id=1, source_target_pairs={{4,5},{5,6},{6,7},{7,4},{12,13},{13,14},{14,15},{15,12},{20,21},{2... | collective-permute-start | bytes 786440 | tf_op jit(solution)/shard_map/ppermute | solution.py:309
  70.6 25.1 %collective-permute-start.7 = (f32[32,16,128]{2,1,0:T(8,128)S(1)}, f32[32,16,128]{2,1,0:T(8,128)S(1)}, u32[]{:S(2)}, u32[]{:S(2)}) collective-permute-start(f32[32,16,128]{2,1,0:T(8,128)S(1)} %slice.14), channel_id=1, source_target_pairs={{4,7},{5,4},{6,5},{7,6},{12,15},{13,12},{14,13},{15,14},{20,23},{2... | collective-permute-start | bytes 786440 | tf_op jit(solution)/shard_map/ppermute | solution.py:309
  75.0 19.9 %collective-permute-start.2 = (f32[32,16,128]{2,1,0:T(8,128)S(1)}, f32[32,16,128]{2,1,0:T(8,128)S(1)}, u32[]{:S(2)}, u32[]{:S(2)}) collective-permute-start(f32[32,16,128]{2,1,0:T(8,128)S(1)} %slice.14), channel_id=1, source_target_pairs={{4,0},{12,8},{20,16},{28,24},{36,32},{44,40},{52,48},{60,56},{68,6... | collective-permute-start | bytes 786440 | tf_op jit(solution)/shard_map/ppermute | solution.py:311
  76.4 21.9 %collective-permute-start.6 = (f32[32,16,128]{2,1,0:T(8,128)S(1)}, f32[32,16,128]{2,1,0:T(8,128)S(1)}, u32[]{:S(2)}, u32[]{:S(2)}) collective-permute-start(f32[32,16,128]{2,1,0:T(8,128)S(1)} %collective-permute-done.5), channel_id=1, source_target_pairs={{4,0},{12,8},{20,16},{28,24},{36,32},{44,40},{52,48},{60,56},{68,6... | collective-permute-start | bytes 786440 | tf_op jit(solution)/shard_map/ppermute | solution.py:311
  92.5 8.1 %copy-start.1 = (f32[32,24,128]{2,1,0:T(8,128)}, f32[32,24,128]{2,1,0:T(8,128)S(1)}, u32[]{:S(2)}) copy-start(f32[32,24,128]{2,1,0:T(8,128)S(1)} %all-to-all-done.3.far) | copy-start | bytes 1179652
  92.5 8.1 %collective-permute-start.1 = (f32[32,24,128]{2,1,0:T(8,128)S(1)}, f32[32,24,128]{2,1,0:T(8,128)S(1)}, u32[]{:S(2)}, u32[]{:S(2)}) collective-permute-start(f32[32,24,128]{2,1,0:T(8,128)S(1)} %all-to-all-done.3.far), channel_id=1, source_target_pairs={{0,4},{4,0},{8,12},{12,8},{16,20},{20,16},{24,28},{28,24},{32,36},... | collective-permute-start | bytes 1179656 | tf_op jit(solution)/shard_map/ppermute | solution.py:313
  92.5 6.5 %collective-permute-start.4 = (f32[32,16,128]{2,1,0:T(8,128)S(1)}, f32[32,16,128]{2,1,0:T(8,128)S(1)}, u32[]{:S(2)}, u32[]{:S(2)}) collective-permute-start(f32[32,16,128]{2,1,0:T(8,128)S(1)} %collective-permute-done.3), channel_id=1, source_target_pairs={{4,0},{12,8},{20,16},{28,24},{36,32},{44,40},{52,48},{60,56},{68,6... | collective-permute-start | bytes 786440 | tf_op jit(solution)/shard_map/ppermute | solution.py:311
  95.7 4.9 %collective-permute-start = (f32[32,16,128]{2,1,0:T(8,128)S(1)}, f32[32,16,128]{2,1,0:T(8,128)S(1)}, u32[]{:S(2)}, u32[]{:S(2)}) collective-permute-start(f32[32,16,128]{2,1,0:T(8,128)S(1)} %get-tuple-element.20), channel_id=1, source_target_pairs={{0,4},{4,0},{8,12},{12,8},{16,20},{20,16},{24,28},{28,24},{32,36},... | collective-permute-start | bytes 786440 | tf_op jit(solution)/shard_map/ppermute | solution.py:306
  95.7 4.1 %collective-permute-start.8 = (f32[32,16,128]{2,1,0:T(8,128)S(1)}, f32[32,16,128]{2,1,0:T(8,128)S(1)}, u32[]{:S(2)}, u32[]{:S(2)}) collective-permute-start(f32[32,16,128]{2,1,0:T(8,128)S(1)} %collective-permute-done.7), channel_id=1, source_target_pairs={{4,0},{12,8},{20,16},{28,24},{36,32},{44,40},{52,48},{60,56},{68,6... | collective-permute-start | bytes 786440 | tf_op jit(solution)/shard_map/ppermute | solution.py:311
  100.6 0.7 copy-start.2
  100.6 0.9 copy-start.3

commit v2 on v1

v2 whole, which is shorter than its diff:
```python
import jax
import jax.numpy as jnp
from jax import lax
from jax.experimental import pallas as pl
from jax.experimental.pallas import tpu as pltpu
from jax.sharding import PartitionSpec as P

BLK = 512
COLS = 128
MOVE = 24
XS, ZS, PLANES = 4, 8, 4
HEAD = BLK // XS
FAR = ZS * MOVE
FACTOR = 64
HALF = XS * (HEAD + FAR)
HIGHEST = lax.Precision.HIGHEST
VMEM = pl.BlockSpec(memory_space=pltpu.VMEM)
SMEM = pl.BlockSpec(memory_space=pltpu.SMEM)
HBM = pl.BlockSpec(memory_space=pl.ANY)


def device(x, z, core):
    return (x % XS * ZS + z % ZS) * 2 + core


def places():
    return [(x, z, core) for x in range(XS) for z in range(ZS) for core in range(2)]


SWAP = [(device(x, z, c), device(x, z, 1 - c)) for x, z, c in places()]
DOWN = [(device(x, z, 1), device(x, z, 0)) for x, z, c in places() if c == 1]
LINES = [[device(x, z, c) for z in range(ZS)] for x in range(XS) for c in range(2)]


def along_x(step):
    return [(device(x, z, c), device(x + step, z, c)) for x, z, c in places()]


def along_y(step):
    return [(y, (y + step) % PLANES) for y in range(PLANES)]


def from_corner(step):
    return [(device(0, 0, c), device(step, 0, c)) for c in range(2)]


def along_z(*hops):
    return [
        (device(x, start, c), device(x, end, c))
        for start, end in hops
        for x in range(XS)
        for c in range(2)
    ]


def halves(value):
    high = value.astype(jnp.bfloat16)
    return high, (value - high.astype(jnp.float32)).astype(jnp.bfloat16)


def dot(left, right):
    return jnp.dot(left, right, preferred_element_type=jnp.float32)


def product(left_high, left_low, right):
    high, low = halves(right)
    width = right.shape[1]
    both = dot(left_high, jnp.concatenate([high, low], axis=1))
    return both[:, :width] + both[:, width:] + dot(left_low, high)


def times(left, right):
    return product(*halves(left), right)


def stage_kernel(rhs, factor, given, out0, out1, out2, out3, sems):
    core = lax.axis_index("rows") % 2
    plane = lax.axis_index("cols")
    outs = (out0, out1, out2, out3)

    def head(x):
        return pltpu.make_async_copy(
            rhs.at[0, pl.ds(HEAD * x, HEAD), :], outs[x].at[pl.ds(0, HEAD), :], sems.at[5 * x]
        )

    def part(x, col, source, first):
        return pltpu.make_async_copy(
            source.at[pl.ds(first + 16 * x, 16), pl.ds(128 * col, 128)],
            outs[x].at[pl.ds(HEAD + 16 * col, 16), :],
            sems.at[5 * x + 1 + col],
        )

    for x in range(XS):
        head(x).start()

    @pl.when(core == 1)
    def _():
        for x in range(XS):
            for col in range(4):
                part(x, col, factor.at[0, 0], 128 * plane + 64).start()

    @pl.when(core == 0)
    def _():
        for x in range(XS):
            for col in range(4):
                part(x, col, given, 0).start()

    for x in range(XS):
        head(x).wait()
        for col in range(4):
            part(x, col, given, 0).wait()


def stage(rhs, multipliers, given):
    return pl.pallas_call(
        stage_kernel,
        name="stage",
        out_shape=[jax.ShapeDtypeStruct((HEAD + FACTOR, COLS), jnp.float32)] * XS,
        in_specs=[HBM, HBM, HBM],
        out_specs=[VMEM] * XS,
        scratch_shapes=[pltpu.SemaphoreType.DMA((5 * XS,))],
    )(rhs, multipliers, given)


def choose_kernel(piv0, piv1, piv2, piv3, rhs, sent, table):
    mine = lax.axis_index("rows")
    plane = lax.axis_index("cols")
    core = mine % 2
    x_mine = mine // (2 * ZS)
    lane = lax.broadcasted_iota(jnp.int32, (64, 128), 1)
    sub = lax.broadcasted_iota(jnp.int32, (64, 128), 0)
    row = lax.broadcasted_iota(jnp.int32, (128, 128), 0)
    col = lax.broadcasted_iota(jnp.int32, (128, 128), 1)
    earlier = jnp.where(row < col, 1.0, 0.0).astype(jnp.bfloat16)
    carry = jnp.zeros((64, 1), jnp.float32)
    source = jnp.zeros((64, 1), jnp.int32)
    place = jnp.zeros((64, 1), jnp.int32)
    for step, pivots in enumerate((piv0, piv1, piv2, piv3)):
        first = ((plane - step) & 3) * 2
        for half in range(2):
            target = pivots[half : half + 1, :]
            owner = lax.shift_right_logical(target, 9) & 63
            moved = target >= 2 * BLK
            hit = (sub == owner) & moved
            ones = jnp.where(hit, 1.0, 0.0)
            before = dot(ones.astype(jnp.bfloat16), earlier) + carry
            carry = carry + jnp.sum(ones, axis=1, keepdims=True)
            rank = jnp.sum(jnp.where(hit, before, 0.0), axis=0, keepdims=True).astype(jnp.int32)
            here = lane[:1] + 128 * (first + half)
            top = jnp.where(lax.shift_right_logical(here, 9) == core, 0, HALF)
            top = top + ((x_mine - lax.shift_right_logical(here, 7)) & 3) * HEAD + (here & 127)
            far = jnp.where((owner & 1) == core, XS * HEAD, HALF + XS * HEAD)
            far = far + ((x_mine - lax.shift_right_logical(owner, 4)) & 3) * FAR
            far = far + (lax.shift_right_logical(owner, 1) & 7) * MOVE + rank
            table[pl.ds(first + half, 1), :] = jnp.where(moved, far, top)
            local = lax.shift_right_logical(target, 15) * BLK + (target & (BLK - 1))
            taken = (sub == rank) & moved & (owner == mine)
            source = source + jnp.sum(jnp.where(taken, local + 1, 0), axis=1, keepdims=True)
            place = place + jnp.sum(jnp.where(taken, top + 1, 0), axis=1, keepdims=True)
    table[8:9, :] = jnp.sum(jnp.where(lane == sub, source, 0), axis=0, keepdims=True) - 1
    table[9:10, :] = jnp.sum(jnp.where(lane == sub, place, 0), axis=0, keepdims=True) - 1
    wide = lax.broadcasted_iota(jnp.int32, (32, 2 * BLK), 1)
    pick = jnp.where(wide == source[:32] - 1, 1.0, 0.0)
    rows = jnp.dot(pick, rhs[...], precision=HIGHEST, preferred_element_type=jnp.float32)
    sent[...] = jnp.broadcast_to(rows[None, :MOVE], (ZS, MOVE, COLS))


def choose(lists, flat):
    return pl.pallas_call(
        choose_kernel,
        name="choose",
        out_shape=(
            jax.ShapeDtypeStruct((ZS, MOVE, COLS), jnp.float32),
            jax.ShapeDtypeStruct((16, 128), jnp.int32),
        ),
        in_specs=[VMEM] * 5,
        out_specs=(VMEM, VMEM),
    )(*lists, flat)


def small_kernel(diag, out):
    row = lax.broadcasted_iota(jnp.int32, (128, 128), 0)
    col = lax.broadcasted_iota(jnp.int32, (128, 128), 1)

    def block(b):
        first = 128 * (b % 4)
        return diag[b // 4, first : first + 128, first : first + 128]

    for b in range(8):
        pair = (row // 2 == col // 2) & (row > col)
        unit = jnp.where(row == col, 1.0, 0.0)
        out[b] = unit - jnp.where(pair, block(b), 0.0)

    def level(step, carry):
        shift = step + 1
        tile_row = lax.shift_right_logical(row, shift)
        near = (tile_row % 2 == 1) & (lax.shift_right_logical(col, shift) == tile_row - 1)
        firsts = []
        for b in range(8):
            firsts.append(times(jnp.where(near, block(b), 0.0), out[b]))
        for b in range(8):
            out[b] = out[b] - times(out[b], firsts[b])
        return carry

    lax.fori_loop(0, 6, level, 0)


def small_inverses(diag):
    return pl.pallas_call(
        small_kernel,
        name="small_inverses",
        out_shape=jax.ShapeDtypeStruct((8, 128, 128), jnp.float32),
        in_specs=[VMEM],
        out_specs=VMEM,
        cost_estimate=pl.CostEstimate(
            flops=2 * 10**9, bytes_accessed=4 * 2**20, transcendentals=0
        ),
    )(diag)


def grow_kernel(diag, work, multipliers, inv_high, inv_low, low_high, low_low):
    def put(panel, i, j, value):
        high, low = halves(value)
        rows = slice(i, i + value.shape[0])
        cols = slice(j, j + value.shape[1])
        inv_high[panel, rows, cols] = high
        inv_low[panel, rows, cols] = low

    zero = jnp.zeros((256, 256), jnp.bfloat16)
    for panel in range(2):
        tops = []
        for half in range(2):
            first = work[4 * panel + 2 * half]
            second = work[4 * panel + 2 * half + 1]
            at = 256 * half
            below = -times(second, times(diag[panel, at + 128 : at + 256, at : at + 128], first))
            top = jnp.concatenate([first, jnp.zeros((128, 128), jnp.float32)], axis=1)
            bottom = jnp.concatenate([below, second], axis=1)
            whole = jnp.concatenate([top, bottom], axis=0)
            tops.append(whole)
            put(panel, 256 * half, 256 * half, whole)
        corner = -times(tops[1], times(diag[panel, 256:512, 0:256], tops[0]))
        put(panel, 256, 0, corner)
        inv_high[panel, 0:256, 256:512] = zero
        inv_low[panel, 0:256, 256:512] = zero
    for panel in range(2):
        for cycle in range(2):
            high, low = halves(multipliers[panel, cycle])
            rows = slice(BLK * cycle, BLK * (cycle + 1))
            cols = slice(BLK * panel, BLK * (panel + 1))
            low_high[rows, cols] = high
            low_low[rows, cols] = low


def grow(diag, work, multipliers):
    return pl.pallas_call(
        grow_kernel,
        name="grow",
        out_shape=(
            jax.ShapeDtypeStruct((2, BLK, BLK), jnp.bfloat16),
            jax.ShapeDtypeStruct((2, BLK, BLK), jnp.bfloat16),
            jax.ShapeDtypeStruct((2 * BLK, 2 * BLK), jnp.bfloat16),
            jax.ShapeDtypeStruct((2 * BLK, 2 * BLK), jnp.bfloat16),
        ),
        in_specs=[VMEM] * 3,
        out_specs=(VMEM,) * 4,
        cost_estimate=pl.CostEstimate(
            flops=2 * 10**9, bytes_accessed=12 * 2**20, transcendentals=0
        ),
    )(diag, work, multipliers)


def finish_kernel(
    table, rhs, rows_own, rows_other, factor_own, factor_other,
    inv_high, inv_low, low_high, low_low,
    out, pool, panel, l21_high, l21_low,
):
    mine = lax.axis_index("rows")
    plane = lax.axis_index("cols")
    core = mine % 2
    x_mine = mine // (2 * ZS)
    pool[:HALF, :] = rows_own[...]
    pool[HALF:, :] = rows_other[...]
    out[...] = rhs[...]

    def gather(i, carry):
        for k in range(8):
            spot = i * 8 + k
            panel[pl.ds(spot, 1), :] = pool[pl.ds(table[lax.shift_right_logical(spot, 7), spot & 127], 1), :]
        return carry

    lax.fori_loop(0, 2 * BLK // 8, gather, 0)
    for k in range(MOVE):
        source = table[8, k]

        @pl.when(source >= 0)
        def _(source=source, k=k):
            out[pl.ds(source, 1), :] = pool[pl.ds(table[9, k], 1), :]

    for step_y in range(PLANES):
        for step_x in range(XS):
            at = (step_y * XS + step_x) * FACTOR
            for side, source in ((0, factor_own), (1, factor_other)):
                first = ((plane - step_y) & 3) * 128 + ((core + side) & 1) * 64
                first = pl.multiple_of(first + ((x_mine - step_x) & 3) * 16, 16)
                for col in range(4):
                    high, low = halves(source[at + 16 * col : at + 16 * (col + 1), :])
                    l21_high[pl.ds(first, 16), 128 * col : 128 * (col + 1)] = high
                    l21_low[pl.ds(first, 16), 128 * col : 128 * (col + 1)] = low
    first = product(inv_high[0], inv_low[0], panel[:BLK, :])
    rest = panel[BLK:, :] - product(l21_high[...], l21_low[...], first)
    second = product(inv_high[1], inv_low[1], rest)
    solved = jnp.concatenate([first, second], axis=0)
    out[...] = out[...] - product(low_high[...], low_low[...], solved)

    @pl.when(mine == 0)
    def _():
        out[:BLK, :] = first

    @pl.when(mine == 1)
    def _():
        out[:BLK, :] = second


def finish(*operands):
    return pl.pallas_call(
        finish_kernel,
        name="finish",
        out_shape=jax.ShapeDtypeStruct((2 * BLK, COLS), jnp.float32),
        in_specs=[SMEM] + [VMEM] * 9,
        out_specs=VMEM,
        scratch_shapes=[
            pltpu.VMEM((2 * HALF, COLS), jnp.float32),
            pltpu.VMEM((2 * BLK, COLS), jnp.float32),
            pltpu.VMEM((BLK, BLK), jnp.bfloat16),
            pltpu.VMEM((BLK, BLK), jnp.bfloat16),
        ],
    )(*operands)


def spread(value, axis, routes):
    return [value] + [lax.ppermute(value, axis, route) for route in routes]


def shards(rhs, diag_blocks, multipliers, pivots):
    cycles, blk, columns = rhs.shape
    flat = rhs.reshape(cycles * blk, columns)
    mine = lax.axis_index("rows")
    plane = lax.axis_index("cols")
    x_mine = mine // (2 * ZS)
    z_mine = mine // 2 % ZS
    half = lax.dynamic_slice(multipliers[0, 0], (128 * plane, 0), (64, BLK))
    given = lax.ppermute(half, "rows", DOWN)
    lists = spread(pivots.reshape(2, 128), "cols", [along_y(k) for k in (1, 2, 3)])
    staged = stage(rhs, multipliers, given)
    out = [lax.ppermute(staged[k], "rows", from_corner(k)) for k in (1, 2, 3)]
    piece = jnp.where(x_mine == 0, staged[0], out[0] + out[1] + out[2])
    piece = jnp.where(z_mine == 0, piece, 0.0)
    out = [lax.ppermute(piece, "rows", along_z((0, k))) for k in (3, 5)]
    piece = piece + out[0] + out[1]
    out = [
        lax.ppermute(piece, "rows", along_z(*hops))
        for hops in (((0, 1), (3, 2), (5, 6)), ((0, 7), (3, 4)))
    ]
    piece = piece + out[0] + out[1]
    sent, table = choose(lists, flat)
    far = lax.all_to_all(sent, "rows", 0, 0, axis_index_groups=LINES, tiled=True)
    far = far.reshape(FAR, COLS)
    x_routes = [along_x(k) for k in (1, 2, 3)]
    factor = jnp.concatenate(spread(piece[HEAD:], "rows", x_routes))
    tops = spread(jnp.concatenate([piece[:HEAD], far]), "rows", x_routes)
    rows = jnp.concatenate([t[:HEAD] for t in tops] + [t[HEAD:] for t in tops])
    factor = jnp.concatenate(spread(factor, "cols", [along_y(k) for k in (1, 2, 3)]))
    rows_other = lax.ppermute(rows, "rows", SWAP)
    factor_other = lax.ppermute(factor, "rows", SWAP)
    work = small_inverses(diag_blocks)
    inverses = grow(diag_blocks, work, multipliers)
    solved = finish(table, flat, rows, rows_other, factor, factor_other, *inverses)
    return solved.reshape(cycles, blk, columns)


def solution(mesh):
    placed = (P(None, "rows", "cols"), P(), P(None, None, "rows", None), P("cols"))
    return jax.shard_map(
        shards, mesh=mesh, in_specs=placed, out_specs=P(None, "rows", "cols"), check_vma=False
    )
```

time: 112 us -> 95.5 us (0.85)
  blocking collectives: 26.4 us -> 0 us
  starting transfers between devices: 36.8 us -> 45 us
  waiting for transfers between devices: 13.6 us -> 16.7 us
  other arithmetic: 3.01 us -> 0.97 us
  local copies, waits for them, and re-layouts: 2.34 us -> 3.68 us
    all_to_all x1 -> x0, blocking collectives: 26.4 us -> none  [exchange(): lax.all_to_all(value, 'rows', 0, 0, axis_index_groups=GROUPS, tiled=True)]
    ppermute x9 -> x22, starting transfers between devices: 17.3 us -> 39.7 us  [the longest x12 11.3 us: spread(): return [value] + [lax.ppermute(value, axis, route) for route in routes]]
    all_to_all x3 -> x1, starting transfers between devices: 19.5 us -> 5.31 us  [shards(): lax.all_to_all(sent, 'rows', 0, 0, axis_index_groups=LINES, tiled=True)]
    ppermute x9 -> x22, waiting for transfers between devices: 0.02 us -> 12.1 us  [the longest x12 7.46 us: spread(): return [value] + [lax.ppermute(value, axis, route) for route in routes]]
    all_to_all x3 -> x1, waiting for transfers between devices: 13.5 us -> 4.59 us  [shards(): lax.all_to_all(sent, 'rows', 0, 0, axis_index_groups=LINES, tiled=True)]
    select_n x4 -> x1, other arithmetic: 3.01 us -> 0.91 us  [shards(): piece = jnp.where(z_mine == 0, piece, 0.0)]
    unnamed x12 -> x29, local copies, waits for them, and re-layouts: 0.87 us -> 2.33 us
    broadcast_in_dim x3 -> x0, local copies, waits for them, and re-layouts: 1.45 us -> none  [the longest x2 0.85 us: shards(): near = exchange(jnp.broadcast_to(piece[None], (CHIPS, 32, COLS)))]
  transfers between devices with their start and end apart: 12 -> 23, of which waited for: 2 -> 9; matrix products, arithmetic and copies ran while one was open for 3% -> 0% of each run, Pallas kernels for 16% -> 17%
where the time goes in v2:
time: 95.5 us; the launch traced here: 95 us
  starting transfers between devices  45 us (47%)
  Pallas kernels  28.3 us (30%)
  waiting for transfers between devices  16.7 us (17%)
  local copies, waits for them, and re-layouts  3.68 us (4%)
  other arithmetic  0.97 us (1%)
    ppermute x12, starting transfers between devices, spread(): return [value] + [lax.ppermute(value, axis, route) for route in routes]  11.3 us
    pallas_call x1, Pallas kernels, finish(): pl.pallas_call(finish_kernel, name='finish', out_shape=jax.ShapeDtypeStru...  10.3 us
    pallas_call x1, Pallas kernels, grow(): pl.pallas_call(grow_kernel, name='grow', out_shape=(jax.ShapeDtypeStruct(...  7.63 us
    ppermute x12, waiting for transfers between devices, spread(): return [value] + [lax.ppermute(value, axis, route) for route in routes]  7.46 us
    ppermute x1, starting transfers between devices, shards(): rows_other = lax.ppermute(rows, 'rows', SWAP)  6.54 us
    ppermute x1, starting transfers between devices, shards(): factor_other = lax.ppermute(factor, 'rows', SWAP)  6.21 us
    pallas_call x1, Pallas kernels, small_inverses(): pl.pallas_call(small_kernel, name='small_inverses', out_shape=jax.ShapeDt...  6.03 us
    all_to_all x1, starting transfers between devices, shards(): lax.all_to_all(sent, 'rows', 0, 0, axis_index_groups=LINES, tiled=True)  5.31 us
  transfers between devices with their start and end apart: 23, of which 9 were waited for; matrix products, arithmetic and copies ran while one was open for 0% of the time, Pallas kernels for 17%

profile of v2, /device:TPU:1, one launch (start us, length us, event | category | flops | bytes accessed | tf_op | source)
XLA Modules:
  0.0 95.0 jit_solution(17452265646201209667)
XLA Ops:
  1.3 5.1 %collective-permute-start.3 = (f32[64,512]{1,0:T(8,128)S(1)}, f32[64,512]{1,0:T(8,128)S(1)}, u32[]{:S(2)}, u32[]{:S(2)}) collective-permute-start(f32[64,512]{1,0:T(8,128)S(1)} %dynamic-slice_bitcast_fusion), channel_id=1, source_target_pairs={{4,0},{12,8},{20,16},{28,24},{36,32},{44,40},{52,48},{60,56},{68,6... | collective-permute-start | bytes 393224 | tf_op jit(solution)/shard_map/ppermute | solution.py:353
  8.1 1.9 %stage.1 = (f32[192,128]{1,0:T(8,128)}, f32[192,128]{1,0:T(8,128)}, f32[192,128]{1,0:T(8,128)}, f32[192,128]{1,0:T(8,128)}) custom-call(f32[2,512,128]{2,1,0:T(8,128)} %rhs.1, f32[2,2,512,512]{3,2,1,0:T(8,128)} %multipliers.1, f32[64,512]{1,0:T(8,128)} %copy-done.4), custom_call_target="tpu_custom_call" | custom-call | tf_op jit(solution)/shard_map/stage/pallas_call | solution.py:115
  9.9 1.4 %collective-permute-start.4 = (f32[192,128]{1,0:T(8,128)}, f32[192,128]{1,0:T(8,128)S(1)}, u32[]{:S(2)}, u32[]{:S(2)}) collective-permute-start(f32[192,128]{1,0:T(8,128)} %get-tuple-element.17), channel_id=1, source_target_pairs={{0,64},{4,68},{1,65},{5,69},{2,66},{6,70},{3,67},{7,71}} | collective-permute-start | bytes 294920 | tf_op jit(solution)/shard_map/ppermute | solution.py:356
  11.4 2.2 %collective-permute-start.5 = (f32[192,128]{1,0:T(8,128)}, f32[192,128]{1,0:T(8,128)S(1)}, u32[]{:S(2)}, u32[]{:S(2)}) collective-permute-start(f32[192,128]{1,0:T(8,128)} %get-tuple-element.18), channel_id=1, source_target_pairs={{0,128},{4,132},{1,129},{5,133},{2,130},{6,134},{3,131},{7,135}} | collective-permute-start | bytes 294920 | tf_op jit(solution)/shard_map/ppermute | solution.py:356
  13.6 1.3 %collective-permute-start.6 = (f32[192,128]{1,0:T(8,128)}, f32[192,128]{1,0:T(8,128)S(1)}, u32[]{:S(2)}, u32[]{:S(2)}) collective-permute-start(f32[192,128]{1,0:T(8,128)} %get-tuple-element.19), channel_id=1, source_target_pairs={{0,192},{4,196},{1,193},{5,197},{2,194},{6,198},{3,195},{7,199}} | collective-permute-start | bytes 294920 | tf_op jit(solution)/shard_map/ppermute | solution.py:356
  15.7 1.3 %collective-permute-done.6 = f32[192,128]{1,0:T(8,128)S(1)} collective-permute-done((f32[192,128]{1,0:T(8,128)}, f32[192,128]{1,0:T(8,128)S(1)}, u32[]{:S(2)}, u32[]{:S(2)}) %collective-permute-start.6) | collective-permute-done | bytes 98336 | tf_op jit(solution)/shard_map/ppermute | solution.py:356
  17.9 1.8 %collective-permute-start.8 = (f32[192,128]{1,0:T(8,128)S(1)}, f32[192,128]{1,0:T(8,128)S(1)}, u32[]{:S(2)}, u32[]{:S(2)}) collective-permute-start(f32[192,128]{1,0:T(8,128)S(1)} %select_select_fusion), channel_id=1, source_target_pairs={{0,40},{4,44},{64,104},{68,108},{128,168},{132,172},{192,232},{196... | collective-permute-start | bytes 294920 | tf_op jit(solution)/shard_map/ppermute | solution.py:359
  19.6 1.3 %collective-permute-start.7 = (f32[192,128]{1,0:T(8,128)S(1)}, f32[192,128]{1,0:T(8,128)S(1)}, u32[]{:S(2)}, u32[]{:S(2)}) collective-permute-start(f32[192,128]{1,0:T(8,128)S(1)} %select_select_fusion), channel_id=1, source_target_pairs={{0,24},{4,28},{64,88},{68,92},{128,152},{132,156},{192,216},{196,2... | collective-permute-start | bytes 294920 | tf_op jit(solution)/shard_map/ppermute | solution.py:359
  21.2 1.3 %collective-permute-done.7 = f32[192,128]{1,0:T(8,128)S(1)} collective-permute-done((f32[192,128]{1,0:T(8,128)S(1)}, f32[192,128]{1,0:T(8,128)S(1)}, u32[]{:S(2)}, u32[]{:S(2)}) %collective-permute-start.7) | collective-permute-done | bytes 98336 | tf_op jit(solution)/shard_map/ppermute | solution.py:359
  22.6 1.3 %collective-permute-start.10 = (f32[192,128]{1,0:T(8,128)S(1)}, f32[192,128]{1,0:T(8,128)S(1)}, u32[]{:S(2)}, u32[]{:S(2)}) collective-permute-start(f32[192,128]{1,0:T(8,128)S(1)} %add_add_fusion.1), channel_id=1, source_target_pairs={{0,56},{4,60},{64,120},{68,124},{128,184},{132,188},{192,248},{196... | collective-permute-start | bytes 294920 | tf_op jit(solution)/shard_map/ppermute | solution.py:362
  23.9 1.3 %collective-permute-start.9 = (f32[192,128]{1,0:T(8,128)S(1)}, f32[192,128]{1,0:T(8,128)S(1)}, u32[]{:S(2)}, u32[]{:S(2)}) collective-permute-start(f32[192,128]{1,0:T(8,128)S(1)} %add_add_fusion.1), channel_id=1, source_target_pairs={{0,8},{4,12},{64,72},{68,76},{128,136},{132,140},{192,200},{196,20... | collective-permute-start | bytes 294920 | tf_op jit(solution)/shard_map/ppermute | solution.py:362
  25.2 2.8 %collective-permute-start.2 = (s32[2,128]{1,0:T(2,128)S(1)}, s32[2,128]{1,0:T(2,128)S(1)}, u32[]{:S(2)}, u32[]{:S(2)}) collective-permute-start(s32[2,128]{1,0:T(2,128)S(1)} %bitcast.11), channel_id=1, source_target_pairs={{0,3},{1,0},{2,1},{3,2},{4,7},{5,4},{6,5},{7,6},{8,11},{9,8},{10,9... | collective-permute-start | bytes 3080 | tf_op jit(solution)/shard_map/ppermute | solution.py:342
  29.0 2.9 %collective-permute-done.1.piv2 = s32[2,128]{1,0:T(2,128)S(1)} collective-permute-done((s32[2,128]{1,0:T(2,128)S(1)}, s32[2,128]{1,0:T(2,128)S(1)}, u32[]{:S(2)}, u32[]{:S(2)}) %collective-permute-start.1) | collective-permute-done | bytes 1056 | tf_op jit(solution)/shard_map/ppermute | solution.py:342
  32.6 2.5 %choose.1 = (f32[8,24,128]{2,1,0:T(8,128)}, s32[16,128]{1,0:T(8,128)}) custom-call(s32[2,128]{1,0:T(2,128)} %bitcast.10, s32[2,128]{1,0:T(2,128)} %copy-done.8, s32[2,128]{1,0:T(2,128)} %copy-done.7, s32[2,128]{1,0:T(2,128)} %copy-done.6, f32[1024,128]{1,0:T(8,128)} %bitcast.6), custom_call_target="tpu_custom_call" | custom-call | tf_op jit(solution)/shard_map/choose/pallas_call | solution.py:169
  35.0 5.3 %all-to-all-start = ((f32[8,24,128]{2,1,0:T(8,128)}), f32[8,24,128]{2,1,0:T(8,128)S(1)}, u32[]{:S(2)}, u32[]{:S(2)}) async-start(f32[8,24,128]{2,1,0:T(8,128)} %get-tuple-element.20), calls=%async_computation | async-start | bytes 196608 | tf_op jit(solution)/shard_map/all_to_all | solution.py:367
  40.4 1.6 %collective-permute-start.17 = (f32[64,128]{1,0:T(8,128)S(1)}, f32[64,128]{1,0:T(8,128)S(1)}, u32[]{:S(2)}, u32[]{:S(2)}) collective-permute-start(f32[64,128]{1,0:T(8,128)S(1)} %get-tuple-element.25), channel_id=1, source_target_pairs={{0,192},{4,196},{8,200},{12,204},{16,208},{20,212},{24,216},{28,22... | collective-permute-start | bytes 98312 | tf_op jit(solution)/shard_map/ppermute | solution.py:342
  43.3 4.6 %all-to-all-done = f32[8,24,128]{2,1,0:T(8,128)S(1)} async-done(((f32[8,24,128]{2,1,0:T(8,128)}), f32[8,24,128]{2,1,0:T(8,128)S(1)}, u32[]{:S(2)}, u32[]{:S(2)}) %all-to-all-start) | async-done | bytes 98336 | tf_op jit(solution)/shard_map/all_to_all | solution.py:367
  47.9 1.6 %collective-permute-start.13 = (f32[320,128]{1,0:T(8,128)S(1)}, f32[320,128]{1,0:T(8,128)S(1)}, u32[]{:S(2)}, u32[]{:S(2)}) collective-permute-start(f32[320,128]{1,0:T(8,128)S(1)} %pad_maximum_fusion), channel_id=1, source_target_pairs={{0,192},{4,196},{8,200},{12,204},{16,208},{20,212},{24,216},{28,22... | collective-permute-start | bytes 491528 | tf_op jit(solution)/shard_map/ppermute | solution.py:342
  52.5 4.5 %collective-permute-done.11 = f32[320,128]{1,0:T(8,128)S(1)} collective-permute-done((f32[320,128]{1,0:T(8,128)S(1)}, f32[320,128]{1,0:T(8,128)S(1)}, u32[]{:S(2)}, u32[]{:S(2)}) %collective-permute-start.11) | collective-permute-done | bytes 163872 | tf_op jit(solution)/shard_map/ppermute | solution.py:342
  57.1 6.5 %collective-permute-start.14 = (f32[1280,128]{1,0:T(8,128)S(1)}, f32[1280,128]{1,0:T(8,128)S(1)}, u32[]{:S(2)}, u32[]{:S(2)}) collective-permute-start(f32[1280,128]{1,0:T(8,128)S(1)} %slice_dynamic-update-slice_fusion.rows_own), channel_id=1, source_target_pairs={{0,4},{4,0},{8,12},{12,8},{16,20},{20,16},{24,28},{28,24},{32,36},... | collective-permute-start | bytes 1966088 | tf_op jit(solution)/shard_map/ppermute | solution.py:374
  63.8 6.2 %collective-permute-start.21 = (f32[1024,128]{1,0:T(8,128)S(1)}, f32[1024,128]{1,0:T(8,128)S(1)}, u32[]{:S(2)}, u32[]{:S(2)}) collective-permute-start(f32[1024,128]{1,0:T(8,128)S(1)} %constant_dynamic-update-slice_fusion.2.factor_own), channel_id=1, source_target_pairs={{0,4},{4,0},{8,12},{12,8},{16,20},{20,16},{24,28},{28,24},{32,36},... | collective-permute-start | bytes 1572872 | tf_op jit(solution)/shard_map/ppermute | solution.py:375
  70.0 6.0 %small_inverses.1.work = f32[8,128,128]{2,1,0:T(8,128)} custom-call(f32[2,512,512]{2,1,0:T(8,128)} %diag.3), custom_call_target="tpu_custom_call" | custom-call | flops 2000000000 | bytes 4194304 | tf_op jit(solution)/shard_map/small_inverses/pallas_call | solution.py:209
  76.0 7.6 %grow.1 = (bf16[2,512,512]{2,1,0:T(8,128)(2,1)}, bf16[2,512,512]{2,1,0:T(8,128)(2,1)}, bf16[1024,1024]{1,0:T(8,128)(2,1)}, bf16[1024,1024]{1,0:T(8,128)(2,1)}) custom-call(f32[2,512,512]{2,1,0:T(8,128)} %diag.3, f32[8,128,128]{2,1,0:T(8,128)} %small_inverses.1.work, f32[2,2,512,512]{3,2,1,0:T(8,128)} %multipliers.1), custom_call_target="tpu_custom_call" | custom-call | flops 2000000000 | bytes 12582912 | tf_op jit(solution)/shard_map/grow/pallas_call | solution.py:256
  84.7 10.3 %finish.1 = f32[1024,128]{1,0:T(8,128)} custom-call(s32[16,128]{1,0:T(8,128)} %get-tuple-element.15.table, f32[1024,128]{1,0:T(8,128)} %bitcast.7, f32[1280,128]{1,0:T(8,128)} %copy-done, f32[1280,128]{1,0:T(8,128)} %copy-done.1, f32[1024,128]{1,0:T(8,128)} %copy-done.2, f32[1024,128]{1,0:T(8,128)} %copy-done.3, ...), custom_call_target="tpu_custom_call" | custom-call | tf_op jit(solution)/shard_map/finish/pallas_call | solution.py:326
  (67 shorter events, 12.0 us)
Async XLA Ops:
  1.3 23.9 %copy-start.5 = (s32[256]{0:T(256)S(1)}, s32[256]{0:T(256)}, u32[]{:S(2)}) copy-start(s32[256]{0:T(256)} %param.7) | copy-start | bytes 3076
  1.3 6.1 %collective-permute-start.3 = (f32[64,512]{1,0:T(8,128)S(1)}, f32[64,512]{1,0:T(8,128)S(1)}, u32[]{:S(2)}, u32[]{:S(2)}) collective-permute-start(f32[64,512]{1,0:T(8,128)S(1)} %dynamic-slice_bitcast_fusion), channel_id=1, source_target_pairs={{4,0},{12,8},{20,16},{28,24},{36,32},{44,40},{52,48},{60,56},{68,6... | collective-permute-start | bytes 393224 | tf_op jit(solution)/shard_map/ppermute | solution.py:353
  9.9 5.0 %collective-permute-start.4 = (f32[192,128]{1,0:T(8,128)}, f32[192,128]{1,0:T(8,128)S(1)}, u32[]{:S(2)}, u32[]{:S(2)}) collective-permute-start(f32[192,128]{1,0:T(8,128)} %get-tuple-element.17), channel_id=1, source_target_pairs={{0,64},{4,68},{1,65},{5,69},{2,66},{6,70},{3,67},{7,71}} | collective-permute-start | bytes 294920 | tf_op jit(solution)/shard_map/ppermute | solution.py:356
  11.4 4.3 %collective-permute-start.5 = (f32[192,128]{1,0:T(8,128)}, f32[192,128]{1,0:T(8,128)S(1)}, u32[]{:S(2)}, u32[]{:S(2)}) collective-permute-start(f32[192,128]{1,0:T(8,128)} %get-tuple-element.18), channel_id=1, source_target_pairs={{0,128},{4,132},{1,129},{5,133},{2,130},{6,134},{3,131},{7,135}} | collective-permute-start | bytes 294920 | tf_op jit(solution)/shard_map/ppermute | solution.py:356
  13.6 3.4 %collective-permute-start.6 = (f32[192,128]{1,0:T(8,128)}, f32[192,128]{1,0:T(8,128)S(1)}, u32[]{:S(2)}, u32[]{:S(2)}) collective-permute-start(f32[192,128]{1,0:T(8,128)} %get-tuple-element.19), channel_id=1, source_target_pairs={{0,192},{4,196},{1,193},{5,197},{2,194},{6,198},{3,195},{7,199}} | collective-permute-start | bytes 294920 | tf_op jit(solution)/shard_map/ppermute | solution.py:356
  17.9 3.4 %collective-permute-start.8 = (f32[192,128]{1,0:T(8,128)S(1)}, f32[192,128]{1,0:T(8,128)S(1)}, u32[]{:S(2)}, u32[]{:S(2)}) collective-permute-start(f32[192,128]{1,0:T(8,128)S(1)} %select_select_fusion), channel_id=1, source_target_pairs={{0,40},{4,44},{64,104},{68,108},{128,168},{132,172},{192,232},{196... | collective-permute-start | bytes 294920 | tf_op jit(solution)/shard_map/ppermute | solution.py:359
  19.6 2.9 %collective-permute-start.7 = (f32[192,128]{1,0:T(8,128)S(1)}, f32[192,128]{1,0:T(8,128)S(1)}, u32[]{:S(2)}, u32[]{:S(2)}) collective-permute-start(f32[192,128]{1,0:T(8,128)S(1)} %select_select_fusion), channel_id=1, source_target_pairs={{0,24},{4,28},{64,88},{68,92},{128,152},{132,156},{192,216},{196,2... | collective-permute-start | bytes 294920 | tf_op jit(solution)/shard_map/ppermute | solution.py:359
  22.6 17.8 %collective-permute-start.10 = (f32[192,128]{1,0:T(8,128)S(1)}, f32[192,128]{1,0:T(8,128)S(1)}, u32[]{:S(2)}, u32[]{:S(2)}) collective-permute-start(f32[192,128]{1,0:T(8,128)S(1)} %add_add_fusion.1), channel_id=1, source_target_pairs={{0,56},{4,60},{64,120},{68,124},{128,184},{132,188},{192,248},{196... | collective-permute-start | bytes 294920 | tf_op jit(solution)/shard_map/ppermute | solution.py:362
  23.9 16.5 %collective-permute-start.9 = (f32[192,128]{1,0:T(8,128)S(1)}, f32[192,128]{1,0:T(8,128)S(1)}, u32[]{:S(2)}, u32[]{:S(2)}) collective-permute-start(f32[192,128]{1,0:T(8,128)S(1)} %add_add_fusion.1), channel_id=1, source_target_pairs={{0,8},{4,12},{64,72},{68,76},{128,136},{132,140},{192,200},{196,20... | collective-permute-start | bytes 294920 | tf_op jit(solution)/shard_map/ppermute | solution.py:362
  25.2 3.9 %collective-permute-start.2 = (s32[2,128]{1,0:T(2,128)S(1)}, s32[2,128]{1,0:T(2,128)S(1)}, u32[]{:S(2)}, u32[]{:S(2)}) collective-permute-start(s32[2,128]{1,0:T(2,128)S(1)} %bitcast.11), channel_id=1, source_target_pairs={{0,3},{1,0},{2,1},{3,2},{4,7},{5,4},{6,5},{7,6},{8,11},{9,8},{10,9... | collective-permute-start | bytes 3080 | tf_op jit(solution)/shard_map/ppermute | solution.py:342
  28.0 3.9 %collective-permute-start.1 = (s32[2,128]{1,0:T(2,128)S(1)}, s32[2,128]{1,0:T(2,128)S(1)}, u32[]{:S(2)}, u32[]{:S(2)}) collective-permute-start(s32[2,128]{1,0:T(2,128)S(1)} %bitcast.12), channel_id=1, source_target_pairs={{0,2},{1,3},{2,0},{3,1},{4,6},{5,7},{6,4},{7,5},{8,10},{9,11},{10,... | collective-permute-start | bytes 3080 | tf_op jit(solution)/shard_map/ppermute | solution.py:342
  28.4 3.6 %collective-permute-start = (s32[2,128]{1,0:T(2,128)S(1)}, s32[2,128]{1,0:T(2,128)S(1)}, u32[]{:S(2)}, u32[]{:S(2)}) collective-permute-start(s32[2,128]{1,0:T(2,128)S(1)} %bitcast.13), channel_id=1, source_target_pairs={{0,1},{1,2},{2,3},{3,0},{4,5},{5,6},{6,7},{7,4},{8,9},{9,10},{10,1... | collective-permute-start | bytes 3080 | tf_op jit(solution)/shard_map/ppermute | solution.py:342
  35.0 12.9 %all-to-all-start = ((f32[8,24,128]{2,1,0:T(8,128)}), f32[8,24,128]{2,1,0:T(8,128)S(1)}, u32[]{:S(2)}, u32[]{:S(2)}) async-start(f32[8,24,128]{2,1,0:T(8,128)} %get-tuple-element.20), calls=%async_computation | async-start | bytes 196608 | tf_op jit(solution)/shard_map/all_to_all | solution.py:367
  40.4 9.9 %collective-permute-start.17 = (f32[64,128]{1,0:T(8,128)S(1)}, f32[64,128]{1,0:T(8,128)S(1)}, u32[]{:S(2)}, u32[]{:S(2)}) collective-permute-start(f32[64,128]{1,0:T(8,128)S(1)} %get-tuple-element.25), channel_id=1, source_target_pairs={{0,192},{4,196},{8,200},{12,204},{16,208},{20,212},{24,216},{28,22... | collective-permute-start | bytes 98312 | tf_op jit(solution)/shard_map/ppermute | solution.py:342
  42.0 8.8 %collective-permute-start.16 = (f32[64,128]{1,0:T(8,128)S(1)}, f32[64,128]{1,0:T(8,128)S(1)}, u32[]{:S(2)}, u32[]{:S(2)}) collective-permute-start(f32[64,128]{1,0:T(8,128)S(1)} %get-tuple-element.25), channel_id=1, source_target_pairs={{0,128},{4,132},{8,136},{12,140},{16,144},{20,148},{24,152},{28,15... | collective-permute-start | bytes 98312 | tf_op jit(solution)/shard_map/ppermute | solution.py:342
  42.7 8.2 %collective-permute-start.15 = (f32[64,128]{1,0:T(8,128)S(1)}, f32[64,128]{1,0:T(8,128)S(1)}, u32[]{:S(2)}, u32[]{:S(2)}) collective-permute-start(f32[64,128]{1,0:T(8,128)S(1)} %get-tuple-element.25), channel_id=1, source_target_pairs={{0,64},{4,68},{8,72},{12,76},{16,80},{20,84},{24,88},{28,92},{32,9... | collective-permute-start | bytes 98312 | tf_op jit(solution)/shard_map/ppermute | solution.py:342
  47.9 9.1 %collective-permute-start.13 = (f32[320,128]{1,0:T(8,128)S(1)}, f32[320,128]{1,0:T(8,128)S(1)}, u32[]{:S(2)}, u32[]{:S(2)}) collective-permute-start(f32[320,128]{1,0:T(8,128)S(1)} %pad_maximum_fusion), channel_id=1, source_target_pairs={{0,192},{4,196},{8,200},{12,204},{16,208},{20,212},{24,216},{28,22... | collective-permute-start | bytes 491528 | tf_op jit(solution)/shard_map/ppermute | solution.py:342
  49.6 7.4 %collective-permute-start.12 = (f32[320,128]{1,0:T(8,128)S(1)}, f32[320,128]{1,0:T(8,128)S(1)}, u32[]{:S(2)}, u32[]{:S(2)}) collective-permute-start(f32[320,128]{1,0:T(8,128)S(1)} %pad_maximum_fusion), channel_id=1, source_target_pairs={{0,128},{4,132},{8,136},{12,140},{16,144},{20,148},{24,152},{28,15... | collective-permute-start | bytes 491528 | tf_op jit(solution)/shard_map/ppermute | solution.py:342
  50.2 6.7 %collective-permute-start.11 = (f32[320,128]{1,0:T(8,128)S(1)}, f32[320,128]{1,0:T(8,128)S(1)}, u32[]{:S(2)}, u32[]{:S(2)}) collective-permute-start(f32[320,128]{1,0:T(8,128)S(1)} %pad_maximum_fusion), channel_id=1, source_target_pairs={{0,64},{4,68},{8,72},{12,76},{16,80},{20,84},{24,88},{28,92},{32,9... | collective-permute-start | bytes 491528 | tf_op jit(solution)/shard_map/ppermute | solution.py:342
  50.9 12.9 %collective-permute-start.20 = (f32[256,128]{1,0:T(8,128)S(1)}, f32[256,128]{1,0:T(8,128)S(1)}, u32[]{:S(2)}, u32[]{:S(2)}) collective-permute-start(f32[256,128]{1,0:T(8,128)S(1)} %pad_maximum_fusion.1), channel_id=1, source_target_pairs={{0,3},{1,0},{2,1},{3,2},{4,7},{5,4},{6,5},{7,6},{8,11},{9,8},{10,9... | collective-permute-start | bytes 393224 | tf_op jit(solution)/shard_map/ppermute | solution.py:342
  51.5 12.2 %collective-permute-start.19 = (f32[256,128]{1,0:T(8,128)S(1)}, f32[256,128]{1,0:T(8,128)S(1)}, u32[]{:S(2)}, u32[]{:S(2)}) collective-permute-start(f32[256,128]{1,0:T(8,128)S(1)} %pad_maximum_fusion.1), channel_id=1, source_target_pairs={{0,2},{1,3},{2,0},{3,1},{4,6},{5,7},{6,4},{7,5},{8,10},{9,11},{10,... | collective-permute-start | bytes 393224 | tf_op jit(solution)/shard_map/ppermute | solution.py:342
  57.0 6.7 %collective-permute-start.18 = (f32[256,128]{1,0:T(8,128)S(1)}, f32[256,128]{1,0:T(8,128)S(1)}, u32[]{:S(2)}, u32[]{:S(2)}) collective-permute-start(f32[256,128]{1,0:T(8,128)S(1)} %pad_maximum_fusion.1), channel_id=1, source_target_pairs={{0,1},{1,2},{2,3},{3,0},{4,5},{5,6},{6,7},{7,4},{8,9},{9,10},{10,1... | collective-permute-start | bytes 393224 | tf_op jit(solution)/shard_map/ppermute | solution.py:342
  57.1 26.5 %collective-permute-start.14 = (f32[1280,128]{1,0:T(8,128)S(1)}, f32[1280,128]{1,0:T(8,128)S(1)}, u32[]{:S(2)}, u32[]{:S(2)}) collective-permute-start(f32[1280,128]{1,0:T(8,128)S(1)} %slice_dynamic-update-slice_fusion.rows_own), channel_id=1, source_target_pairs={{0,4},{4,0},{8,12},{12,8},{16,20},{20,16},{24,28},{28,24},{32,36},... | collective-permute-start | bytes 1966088 | tf_op jit(solution)/shard_map/ppermute | solution.py:374
  63.8 19.9 %collective-permute-start.21 = (f32[1024,128]{1,0:T(8,128)S(1)}, f32[1024,128]{1,0:T(8,128)S(1)}, u32[]{:S(2)}, u32[]{:S(2)}) collective-permute-start(f32[1024,128]{1,0:T(8,128)S(1)} %constant_dynamic-update-slice_fusion.2.factor_own), channel_id=1, source_target_pairs={{0,4},{4,0},{8,12},{12,8},{16,20},{20,16},{24,28},{28,24},{32,36},... | collective-permute-start | bytes 1572872 | tf_op jit(solution)/shard_map/ppermute | solution.py:375
  (8 other events, 37.8 us)

commit v3 on v2

--- a/solution.py
+++ b/solution.py
@@ -4,6 +4,7 @@
 from jax.experimental import pallas as pl
 from jax.experimental.pallas import tpu as pltpu
 from jax.sharding import PartitionSpec as P
+
 
 BLK = 512
 COLS = 128
@@ -16,7 +17,8 @@
 HIGHEST = lax.Precision.HIGHEST
 VMEM = pl.BlockSpec(memory_space=pltpu.VMEM)
 SMEM = pl.BlockSpec(memory_space=pltpu.SMEM)
-HBM = pl.BlockSpec(memory_space=pl.ANY)
+HBM = pl.BlockSpec(memory_space=pltpu.HBM)
+ROOM = pltpu.CompilerParams(vmem_limit_bytes=24 * 2**20)
 
 
 def device(x, z, core):
@@ -53,6 +55,14 @@
     ]
 
 
+def near(value):
+    return pltpu.with_memory_space_constraint(value, pltpu.VMEM)
+
+
+def away(value):
+    return pltpu.with_memory_space_constraint(value, pltpu.HBM)
+
+
 def halves(value):
     high = value.astype(jnp.bfloat16)
     return high, (value - high.astype(jnp.float32)).astype(jnp.bfloat16)
@@ -115,11 +125,12 @@
     return pl.pallas_call(
         stage_kernel,
         name="stage",
+        compiler_params=ROOM,
         out_shape=[jax.ShapeDtypeStruct((HEAD + FACTOR, COLS), jnp.float32)] * XS,
-        in_specs=[HBM, HBM, HBM],
+        in_specs=[HBM, HBM, VMEM],
         out_specs=[VMEM] * XS,
         scratch_shapes=[pltpu.SemaphoreType.DMA((5 * XS,))],
-    )(rhs, multipliers, given)
+    )(away(rhs), away(multipliers), near(given))
 
 
 def choose_kernel(piv0, piv1, piv2, piv3, rhs, sent, table):
@@ -169,127 +180,100 @@
     return pl.pallas_call(
         choose_kernel,
         name="choose",
+        compiler_params=ROOM,
         out_shape=(
             jax.ShapeDtypeStruct((ZS, MOVE, COLS), jnp.float32),
             jax.ShapeDtypeStruct((16, 128), jnp.int32),
         ),
         in_specs=[VMEM] * 5,
         out_specs=(VMEM, VMEM),
-    )(*lists, flat)
-
-
-def small_kernel(diag, out):
+    )(*map(near, lists), flat)
+
+
+def invert_kernel(diag, out, work, load):
+    core = lax.axis_index("rows") % 2
+    copy = pltpu.make_async_copy(diag.at[core], out, load)
+    copy.start()
+    copy.wait()
     row = lax.broadcasted_iota(jnp.int32, (128, 128), 0)
     col = lax.broadcasted_iota(jnp.int32, (128, 128), 1)
 
     def block(b):
-        first = 128 * (b % 4)
-        return diag[b // 4, first : first + 128, first : first + 128]
-
-    for b in range(8):
+        return out[128 * b : 128 * (b + 1), 128 * b : 128 * (b + 1)]
+
+    for b in range(4):
         pair = (row // 2 == col // 2) & (row > col)
         unit = jnp.where(row == col, 1.0, 0.0)
-        out[b] = unit - jnp.where(pair, block(b), 0.0)
+        work[b] = unit - jnp.where(pair, block(b), 0.0)
 
     def level(step, carry):
         shift = step + 1
         tile_row = lax.shift_right_logical(row, shift)
         near = (tile_row % 2 == 1) & (lax.shift_right_logical(col, shift) == tile_row - 1)
         firsts = []
-        for b in range(8):
-            firsts.append(times(jnp.where(near, block(b), 0.0), out[b]))
-        for b in range(8):
-            out[b] = out[b] - times(out[b], firsts[b])
+        for b in range(4):
+            firsts.append(times(jnp.where(near, block(b), 0.0), work[b]))
+        for b in range(4):
+            work[b] = work[b] - times(work[b], firsts[b])
         return carry
 
     lax.fori_loop(0, 6, level, 0)
-
-
-def small_inverses(diag):
+    tops = []
+    for half in range(2):
+        first = work[2 * half]
+        second = work[2 * half + 1]
+        at = 256 * half
+        below = -times(second, times(out[at + 128 : at + 256, at : at + 128], first))
+        top = jnp.concatenate([first, jnp.zeros((128, 128), jnp.float32)], axis=1)
+        bottom = jnp.concatenate([below, second], axis=1)
+        tops.append(jnp.concatenate([top, bottom], axis=0))
+    out[256:512, 0:256] = -times(tops[1], times(out[256:512, 0:256], tops[0]))
+    out[0:256, 0:256] = tops[0]
+    out[256:512, 256:512] = tops[1]
+    out[0:256, 256:512] = jnp.zeros((256, 256), jnp.float32)
+
+
+def invert(diag):
     return pl.pallas_call(
-        small_kernel,
-        name="small_inverses",
-        out_shape=jax.ShapeDtypeStruct((8, 128, 128), jnp.float32),
-        in_specs=[VMEM],
+        invert_kernel,
+        name="invert",
+        compiler_params=ROOM,
+        out_shape=jax.ShapeDtypeStruct((BLK, BLK), jnp.float32),
+        in_specs=[HBM],
         out_specs=VMEM,
+        scratch_shapes=[pltpu.VMEM((4, 128, 128), jnp.float32), pltpu.SemaphoreType.DMA],
         cost_estimate=pl.CostEstimate(
             flops=2 * 10**9, bytes_accessed=4 * 2**20, transcendentals=0
         ),
-    )(diag)
-
-
-def grow_kernel(diag, work, multipliers, inv_high, inv_low, low_high, low_low):
-    def put(panel, i, j, value):
-        high, low = halves(value)
-        rows = slice(i, i + value.shape[0])
-        cols = slice(j, j + value.shape[1])
-        inv_high[panel, rows, cols] = high
-        inv_low[panel, rows, cols] = low
-
-    zero = jnp.zeros((256, 256), jnp.bfloat16)
-    for panel in range(2):
-        tops = []
-        for half in range(2):
-            first = work[4 * panel + 2 * half]
-            second = work[4 * panel + 2 * half + 1]
-            at = 256 * half
-            below = -times(second, times(diag[panel, at + 128 : at + 256, at : at + 128], first))
-            top = jnp.concatenate([first, jnp.zeros((128, 128), jnp.float32)], axis=1)
-            bottom = jnp.concatenate([below, second], axis=1)
-            whole = jnp.concatenate([top, bottom], axis=0)
-            tops.append(whole)
-            put(panel, 256 * half, 256 * half, whole)
-        corner = -times(tops[1], times(diag[panel, 256:512, 0:256], tops[0]))
-        put(panel, 256, 0, corner)
-        inv_high[panel, 0:256, 256:512] = zero
-        inv_low[panel, 0:256, 256:512] = zero
-    for panel in range(2):
-        for cycle in range(2):
-            high, low = halves(multipliers[panel, cycle])
-            rows = slice(BLK * cycle, BLK * (cycle + 1))
-            cols = slice(BLK * panel, BLK * (panel + 1))
-            low_high[rows, cols] = high
-            low_low[rows, cols] = low
-
-
-def grow(diag, work, multipliers):
-    return pl.pallas_call(
-        grow_kernel,
-        name="grow",
-        out_shape=(
-            jax.ShapeDtypeStruct((2, BLK, BLK), jnp.bfloat16),
-            jax.ShapeDtypeStruct((2, BLK, BLK), jnp.bfloat16),
-            jax.ShapeDtypeStruct((2 * BLK, 2 * BLK), jnp.bfloat16),
-            jax.ShapeDtypeStruct((2 * BLK, 2 * BLK), jnp.bfloat16),
-        ),
-        in_specs=[VMEM] * 3,
-        out_specs=(VMEM,) * 4,
-        cost_estimate=pl.CostEstimate(
-            flops=2 * 10**9, bytes_accessed=12 * 2**20, transcendentals=0
-        ),
-    )(diag, work, multipliers)
+    )(away(diag))
 
 
 def finish_kernel(
-    table, rhs, rows_own, rows_other, factor_own, factor_other,
-    inv_high, inv_low, low_high, low_low,
-    out, pool, panel, l21_high, l21_low,
+    table, rhs, multipliers, rows_own, rows_other, factor_own, factor_other, inv_own, inv_other,
+    out, lower, pool, panel, l21_high, l21_low, inverse, sems,
 ):
     mine = lax.axis_index("rows")
     plane = lax.axis_index("cols")
     core = mine % 2
     x_mine = mine // (2 * ZS)
+    kept = pltpu.make_async_copy(rhs, out, sems.at[0])
+    kept.start()
+    loads = [pltpu.make_async_copy(multipliers.at[k], lower.at[k], sems.at[1 + k]) for k in range(2)]
+    for load in loads:
+        load.start()
     pool[:HALF, :] = rows_own[...]
     pool[HALF:, :] = rows_other[...]
-    out[...] = rhs[...]
-
-    def gather(i, carry):
-        for k in range(8):
-            spot = i * 8 + k
-            panel[pl.ds(spot, 1), :] = pool[pl.ds(table[lax.shift_right_logical(spot, 7), spot & 127], 1), :]
-        return carry
-
-    lax.fori_loop(0, 2 * BLK // 8, gather, 0)
+
+    for part in range(8):
+
+        def gather(i, carry, part=part):
+            for k in range(8):
+                spot = i * 8 + k
+                panel[pl.ds(128 * part + spot, 1), :] = pool[pl.ds(table[part, spot], 1), :]
+            return carry
+
+        lax.fori_loop(0, 16, gather, 0)
+    kept.wait()
     for k in range(MOVE):
         source = table[8, k]
 
@@ -307,11 +291,17 @@
                     high, low = halves(source[at + 16 * col : at + 16 * (col + 1), :])
                     l21_high[pl.ds(first, 16), 128 * col : 128 * (col + 1)] = high
                     l21_low[pl.ds(first, 16), 128 * col : 128 * (col + 1)] = low
-    first = product(inv_high[0], inv_low[0], panel[:BLK, :])
+    inverse[core] = inv_own[...]
+    inverse[1 - core] = inv_other[...]
+    first = times(inverse[0], panel[:BLK, :])
     rest = panel[BLK:, :] - product(l21_high[...], l21_low[...], first)
-    second = product(inv_high[1], inv_low[1], rest)
-    solved = jnp.concatenate([first, second], axis=0)
-    out[...] = out[...] - product(low_high[...], low_low[...], solved)
+    second = times(inverse[1], rest)
+    for load in loads:
+        load.wait()
+    for cycle in range(2):
+        rows = slice(BLK * cycle, BLK * (cycle + 1))
+        taken = times(lower[0, cycle], first) + times(lower[1, cycle], second)
+        out[rows, :] = out[rows, :] - taken
 
     @pl.when(mine == 0)
     def _():
@@ -322,20 +312,27 @@
         out[:BLK, :] = second
 
 
-def finish(*operands):
+def finish(table, flat, multipliers, rows, rows_other, factor, factor_other, inverse, inverse_other):
     return pl.pallas_call(
         finish_kernel,
         name="finish",
+        compiler_params=ROOM,
         out_shape=jax.ShapeDtypeStruct((2 * BLK, COLS), jnp.float32),
-        in_specs=[SMEM] + [VMEM] * 9,
+        in_specs=[SMEM, HBM, HBM] + [VMEM] * 6,
         out_specs=VMEM,
         scratch_shapes=[
+            pltpu.VMEM((2, 2, BLK, BLK), jnp.float32),
             pltpu.VMEM((2 * HALF, COLS), jnp.float32),
             pltpu.VMEM((2 * BLK, COLS), jnp.float32),
             pltpu.VMEM((BLK, BLK), jnp.bfloat16),
             pltpu.VMEM((BLK, BLK), jnp.bfloat16),
+            pltpu.VMEM((2, BLK, BLK), jnp.float32),
+            pltpu.SemaphoreType.DMA((3,)),
         ],
-    )(*operands)
+    )(
+        table, away(flat), away(multipliers), near(rows), near(rows_other),
+        near(factor), near(factor_other), near(inverse), near(inverse_other),
+    )
 
 
 def spread(value, axis, routes):
@@ -349,7 +346,7 @@
     plane = lax.axis_index("cols")
     x_mine = mine // (2 * ZS)
     z_mine = mine // 2 % ZS
-    half = lax.dynamic_slice(multipliers[0, 0], (128 * plane, 0), (64, BLK))
+    half = lax.dynamic_slice(multipliers, (0, 0, 128 * plane, 0), (1, 1, 64, BLK))[0, 0]
     given = lax.ppermute(half, "rows", DOWN)
     lists = spread(pivots.reshape(2, 128), "cols", [along_y(k) for k in (1, 2, 3)])
     staged = stage(rhs, multipliers, given)
@@ -373,9 +370,12 @@
     factor = jnp.concatenate(spread(factor, "cols", [along_y(k) for k in (1, 2, 3)]))
     rows_other = lax.ppermute(rows, "rows", SWAP)
     factor_other = lax.ppermute(factor, "rows", SWAP)
-    work = small_inverses(diag_blocks)
-    inverses = grow(diag_blocks, work, multipliers)
-    solved = finish(table, flat, rows, rows_other, factor, factor_other, *inverses)
+    inverse = invert(diag_blocks)
+    inverse_other = lax.ppermute(inverse, "rows", SWAP)
+    solved = finish(
+        table, flat, multipliers, rows, rows_other, factor, factor_other,
+        inverse, inverse_other,
+    )
     return solved.reshape(cycles, blk, columns)
 
 

time: 95.5 us -> 78.1 us (0.82)
  Pallas kernels: 28.3 us -> 14.8 us
  starting transfers between devices: 45 us -> 39.7 us
  waiting for transfers between devices: 16.7 us -> 20 us
  local copies, waits for them, and re-layouts: 3.68 us -> 1.81 us
    pallas_call x5 -> x4, Pallas kernels: 28.3 us -> 14.8 us  [the longest x1 7.13 us: finish(): pl.pallas_call(finish_kernel, name='finish', compiler_params=ROOM, out_sh...]
    ppermute x1, starting transfers between devices: 6.21 us -> 0.95 us  [shards(): factor_other = lax.ppermute(factor, 'rows', SWAP)]
    ppermute x1, starting transfers between devices: 6.54 us -> 2 us  [shards(): rows_other = lax.ppermute(rows, 'rows', SWAP)]
    ppermute x12, waiting for transfers between devices: 7.46 us -> 11.9 us  [spread(): return [value] + [lax.ppermute(value, axis, route) for route in routes]]
    ppermute x12, starting transfers between devices: 11.3 us -> 15.7 us  [spread(): return [value] + [lax.ppermute(value, axis, route) for route in routes]]
    all_to_all x1, starting transfers between devices: 5.31 us -> 3.36 us  [shards(): lax.all_to_all(sent, 'rows', 0, 0, axis_index_groups=LINES, tiled=True)]
    ppermute x2, waiting for transfers between devices: 1.62 us -> 0.01 us  [shards(): out = [lax.ppermute(piece, 'rows', along_z((0, k))) for k in (3, 5)]]
    ppermute x0 -> x1, starting transfers between devices: none -> 1.57 us  [shards(): inverse_other = lax.ppermute(inverse, 'rows', SWAP)]
  transfers between devices with their start and end apart: 23 -> 24, of which waited for: 9 -> 7; matrix products, arithmetic and copies ran while one was open for 0% -> 2% of each run, Pallas kernels for 17% -> 8%
where the time goes in v3:
time: 78.1 us; the launch traced here: 77.6 us
  starting transfers between devices  39.7 us (51%)
  waiting for transfers between devices  20 us (26%)
  Pallas kernels  14.8 us (19%)
  local copies, waits for them, and re-layouts  1.81 us (2%)
  other arithmetic  0.84 us (1%)
    ppermute x12, starting transfers between devices, spread(): return [value] + [lax.ppermute(value, axis, route) for route in routes]  15.7 us
    ppermute x12, waiting for transfers between devices, spread(): return [value] + [lax.ppermute(value, axis, route) for route in routes]  11.9 us
    pallas_call x1, Pallas kernels, finish(): pl.pallas_call(finish_kernel, name='finish', compiler_params=ROOM, out_sh...  7.13 us
    pallas_call x1, Pallas kernels, invert(): pl.pallas_call(invert_kernel, name='invert', compiler_params=ROOM, out_sh...  5.12 us
    ppermute x1, starting transfers between devices, shards(): given = lax.ppermute(half, 'rows', DOWN)  5.11 us
    ppermute x3, starting transfers between devices, shards(): out = [lax.ppermute(staged[k], 'rows', from_corner(k)) for k in (1, 2, 3)]  5.04 us
    all_to_all x1, waiting for transfers between devices, shards(): lax.all_to_all(sent, 'rows', 0, 0, axis_index_groups=LINES, tiled=True)  3.92 us
    ppermute x2, starting transfers between devices, shards(): out = [lax.ppermute(piece, 'rows', along_z((0, k))) for k in (3, 5)]  3.36 us
  transfers between devices with their start and end apart: 24, of which 7 were waited for; matrix products, arithmetic and copies ran while one was open for 2% of the time, Pallas kernels for 8%

profile of v3, /device:TPU:1, one launch (start us, length us, event | category | flops | bytes accessed | tf_op | source)
XLA Modules:
  0.0 77.6 jit_solution(15941953668733778861)
XLA Ops:
  0.9 5.1 %collective-permute-start.3 = (f32[64,512]{1,0:T(8,128)S(1)}, f32[64,512]{1,0:T(8,128)S(1)}, u32[]{:S(2)}, u32[]{:S(2)}) collective-permute-start(f32[64,512]{1,0:T(8,128)S(1)} %dynamic-slice_bitcast_fusion), channel_id=1, source_target_pairs={{4,0},{12,8},{20,16},{28,24},{36,32},{44,40},{52,48},{60,56},{68,6... | collective-permute-start | bytes 393224 | tf_op jit(solution)/shard_map/ppermute | solution.py:350
  8.2 1.5 %collective-permute-start.4 = (f32[192,128]{1,0:T(8,128)S(1)}, f32[192,128]{1,0:T(8,128)S(1)}, u32[]{:S(2)}, u32[]{:S(2)}) collective-permute-start(f32[192,128]{1,0:T(8,128)S(1)} %get-tuple-element.13), channel_id=1, source_target_pairs={{0,64},{4,68},{1,65},{5,69},{2,66},{6,70},{3,67},{7,71}} | collective-permute-start | bytes 294920 | tf_op jit(solution)/shard_map/ppermute | solution.py:353
  9.7 2.2 %collective-permute-start.5 = (f32[192,128]{1,0:T(8,128)S(1)}, f32[192,128]{1,0:T(8,128)S(1)}, u32[]{:S(2)}, u32[]{:S(2)}) collective-permute-start(f32[192,128]{1,0:T(8,128)S(1)} %get-tuple-element.14), channel_id=1, source_target_pairs={{0,128},{4,132},{1,129},{5,133},{2,130},{6,134},{3,131},{7,135}} | collective-permute-start | bytes 294920 | tf_op jit(solution)/shard_map/ppermute | solution.py:353
  11.9 1.3 %collective-permute-start.6 = (f32[192,128]{1,0:T(8,128)S(1)}, f32[192,128]{1,0:T(8,128)S(1)}, u32[]{:S(2)}, u32[]{:S(2)}) collective-permute-start(f32[192,128]{1,0:T(8,128)S(1)} %get-tuple-element.15), channel_id=1, source_target_pairs={{0,192},{4,196},{1,193},{5,197},{2,194},{6,198},{3,195},{7,199}} | collective-permute-start | bytes 294920 | tf_op jit(solution)/shard_map/ppermute | solution.py:353
  13.7 1.3 %collective-permute-done.6 = f32[192,128]{1,0:T(8,128)S(1)} collective-permute-done((f32[192,128]{1,0:T(8,128)S(1)}, f32[192,128]{1,0:T(8,128)S(1)}, u32[]{:S(2)}, u32[]{:S(2)}) %collective-permute-start.6) | collective-permute-done | bytes 98336 | tf_op jit(solution)/shard_map/ppermute | solution.py:353
  15.0 2.1 %collective-permute-start.8 = (f32[192,128]{1,0:T(8,128)S(1)}, f32[192,128]{1,0:T(8,128)S(1)}, u32[]{:S(2)}, u32[]{:S(2)}) collective-permute-start(f32[192,128]{1,0:T(8,128)S(1)} %select_select_fusion), channel_id=1, source_target_pairs={{0,40},{4,44},{64,104},{68,108},{128,168},{132,172},{192,232},{196... | collective-permute-start | bytes 294920 | tf_op jit(solution)/shard_map/ppermute | solution.py:356
  17.1 1.3 %collective-permute-start.7 = (f32[192,128]{1,0:T(8,128)S(1)}, f32[192,128]{1,0:T(8,128)S(1)}, u32[]{:S(2)}, u32[]{:S(2)}) collective-permute-start(f32[192,128]{1,0:T(8,128)S(1)} %select_select_fusion), channel_id=1, source_target_pairs={{0,24},{4,28},{64,88},{68,92},{128,152},{132,156},{192,216},{196,2... | collective-permute-start | bytes 294920 | tf_op jit(solution)/shard_map/ppermute | solution.py:356
  18.4 2.8 %collective-permute-start.2 = (s32[2,128]{1,0:T(2,128)S(1)}, s32[2,128]{1,0:T(2,128)S(1)}, u32[]{:S(2)}, u32[]{:S(2)}) collective-permute-start(s32[2,128]{1,0:T(2,128)S(1)} %bitcast.8), channel_id=1, source_target_pairs={{0,3},{1,0},{2,1},{3,2},{4,7},{5,4},{6,5},{7,6},{8,11},{9,8},{10,9... | collective-permute-start | bytes 3080 | tf_op jit(solution)/shard_map/ppermute | solution.py:339
  22.3 1.3 %collective-permute-start.10 = (f32[192,128]{1,0:T(8,128)S(1)}, f32[192,128]{1,0:T(8,128)S(1)}, u32[]{:S(2)}, u32[]{:S(2)}) collective-permute-start(f32[192,128]{1,0:T(8,128)S(1)} %add_add_fusion.1), channel_id=1, source_target_pairs={{0,56},{4,60},{64,120},{68,124},{128,184},{132,188},{192,248},{196... | collective-permute-start | bytes 294920 | tf_op jit(solution)/shard_map/ppermute | solution.py:359
  23.6 1.3 %collective-permute-start.9 = (f32[192,128]{1,0:T(8,128)S(1)}, f32[192,128]{1,0:T(8,128)S(1)}, u32[]{:S(2)}, u32[]{:S(2)}) collective-permute-start(f32[192,128]{1,0:T(8,128)S(1)} %add_add_fusion.1), channel_id=1, source_target_pairs={{0,8},{4,12},{64,72},{68,76},{128,136},{132,140},{192,200},{196,20... | collective-permute-start | bytes 294920 | tf_op jit(solution)/shard_map/ppermute | solution.py:359
  24.9 5.1 %invert.1.inv_own = f32[512,512]{1,0:T(8,128)S(1)} custom-call(f32[2,512,512]{2,1,0:T(8,128)} %diag.1), custom_call_target="tpu_custom_call" | custom-call | flops 2000000000 | bytes 4194304 | tf_op jit(solution)/shard_map/invert/pallas_call | solution.py:237
  30.0 1.6 %collective-permute-start.22 = (f32[512,512]{1,0:T(8,128)S(1)}, f32[512,512]{1,0:T(8,128)S(1)}, u32[]{:S(2)}, u32[]{:S(2)}) collective-permute-start(f32[512,512]{1,0:T(8,128)S(1)} %invert.1.inv_own), channel_id=1, source_target_pairs={{0,4},{4,0},{8,12},{12,8},{16,20},{20,16},{24,28},{28,24},{32,36},... | collective-permute-start | bytes 3145736 | tf_op jit(solution)/shard_map/ppermute | solution.py:374
  31.6 1.4 %choose.1 = (f32[8,24,128]{2,1,0:T(8,128)}, s32[16,128]{1,0:T(8,128)S(1)}) custom-call(s32[2,128]{1,0:T(2,128)S(1)} %bitcast.11, s32[2,128]{1,0:T(2,128)S(1)} %collective-permute-done.piv1, s32[2,128]{1,0:T(2,128)S(1)} %collective-permute-done.1.piv2, s32[2,128]{1,0:T(2,128)S(1)} %collective-permute-done.2.piv3, f32[1024,128]{1,0:T(8,128)S(1)} %bitcast.7), custom_call_target="tpu_custom_call" | custom-call | tf_op jit(solution)/shard_map/choose/pallas_call | solution.py:180
  33.0 3.4 %all-to-all-start = ((f32[8,24,128]{2,1,0:T(8,128)}), f32[8,24,128]{2,1,0:T(8,128)S(1)}, u32[]{:S(2)}, u32[]{:S(2)}) async-start(f32[8,24,128]{2,1,0:T(8,128)} %get-tuple-element.16), calls=%async_computation | async-start | bytes 196608 | tf_op jit(solution)/shard_map/all_to_all | solution.py:364
  36.4 3.3 %collective-permute-start.17 = (f32[64,128]{1,0:T(8,128)S(1)}, f32[64,128]{1,0:T(8,128)S(1)}, u32[]{:S(2)}, u32[]{:S(2)}) collective-permute-start(f32[64,128]{1,0:T(8,128)S(1)} %get-tuple-element.17), channel_id=1, source_target_pairs={{0,192},{4,196},{8,200},{12,204},{16,208},{20,212},{24,216},{28,22... | collective-permute-start | bytes 98312 | tf_op jit(solution)/shard_map/ppermute | solution.py:339
  40.4 3.9 %all-to-all-done = f32[8,24,128]{2,1,0:T(8,128)S(1)} async-done(((f32[8,24,128]{2,1,0:T(8,128)}), f32[8,24,128]{2,1,0:T(8,128)S(1)}, u32[]{:S(2)}, u32[]{:S(2)}) %all-to-all-start) | async-done | bytes 98336 | tf_op jit(solution)/shard_map/all_to_all | solution.py:364
  44.3 3.3 %collective-permute-start.13 = (f32[320,128]{1,0:T(8,128)S(1)}, f32[320,128]{1,0:T(8,128)S(1)}, u32[]{:S(2)}, u32[]{:S(2)}) collective-permute-start(f32[320,128]{1,0:T(8,128)S(1)} %pad_maximum_fusion), channel_id=1, source_target_pairs={{0,192},{4,196},{8,200},{12,204},{16,208},{20,212},{24,216},{28,22... | collective-permute-start | bytes 491528 | tf_op jit(solution)/shard_map/ppermute | solution.py:339
  49.1 1.9 %collective-permute-start.20 = (f32[256,128]{1,0:T(8,128)S(1)}, f32[256,128]{1,0:T(8,128)S(1)}, u32[]{:S(2)}, u32[]{:S(2)}) collective-permute-start(f32[256,128]{1,0:T(8,128)S(1)} %pad_maximum_fusion.1), channel_id=1, source_target_pairs={{0,3},{1,0},{2,1},{3,2},{4,7},{5,4},{6,5},{7,6},{8,11},{9,8},{10,9... | collective-permute-start | bytes 393224 | tf_op jit(solution)/shard_map/ppermute | solution.py:339
  51.8 6.6 %collective-permute-done.11 = f32[320,128]{1,0:T(8,128)S(1)} collective-permute-done((f32[320,128]{1,0:T(8,128)S(1)}, f32[320,128]{1,0:T(8,128)S(1)}, u32[]{:S(2)}, u32[]{:S(2)}) %collective-permute-start.11) | collective-permute-done | bytes 163872 | tf_op jit(solution)/shard_map/ppermute | solution.py:339
  58.4 1.5 %collective-permute-start.19 = (f32[256,128]{1,0:T(8,128)S(1)}, f32[256,128]{1,0:T(8,128)S(1)}, u32[]{:S(2)}, u32[]{:S(2)}) collective-permute-start(f32[256,128]{1,0:T(8,128)S(1)} %pad_maximum_fusion.1), channel_id=1, source_target_pairs={{0,2},{1,3},{2,0},{3,1},{4,6},{5,7},{6,4},{7,5},{8,10},{9,11},{10,... | collective-permute-start | bytes 393224 | tf_op jit(solution)/shard_map/ppermute | solution.py:339
  60.5 2.0 %collective-permute-start.14 = (f32[1280,128]{1,0:T(8,128)S(1)}, f32[1280,128]{1,0:T(8,128)S(1)}, u32[]{:S(2)}, u32[]{:S(2)}) collective-permute-start(f32[1280,128]{1,0:T(8,128)S(1)} %slice_dynamic-update-slice_fusion.rows_own), channel_id=1, source_target_pairs={{0,4},{4,0},{8,12},{12,8},{16,20},{20,16},{24,28},{28,24},{32,36},... | collective-permute-start | bytes 1966088 | tf_op jit(solution)/shard_map/ppermute | solution.py:371
  62.5 5.3 %collective-permute-done.18 = f32[256,128]{1,0:T(8,128)S(1)} collective-permute-done((f32[256,128]{1,0:T(8,128)S(1)}, f32[256,128]{1,0:T(8,128)S(1)}, u32[]{:S(2)}, u32[]{:S(2)}) %collective-permute-start.18) | collective-permute-done | bytes 131104 | tf_op jit(solution)/shard_map/ppermute | solution.py:339
  68.7 1.5 %collective-permute-done.21.factor_other = f32[1024,128]{1,0:T(8,128)S(1)} collective-permute-done((f32[1024,128]{1,0:T(8,128)S(1)}, f32[1024,128]{1,0:T(8,128)S(1)}, u32[]{:S(2)}, u32[]{:S(2)}) %collective-permute-start.21) | collective-permute-done | bytes 524320 | tf_op jit(solution)/shard_map/ppermute | solution.py:372
  70.3 7.1 %finish.1 = f32[1024,128]{1,0:T(8,128)} custom-call(s32[16,128]{1,0:T(8,128)S(1)} %get-tuple-element.11.table, f32[1024,128]{1,0:T(8,128)} %bitcast.6, f32[2,2,512,512]{3,2,1,0:T(8,128)} %multipliers.1, f32[1280,128]{1,0:T(8,128)S(1)} %slice_dynamic-update-slice_fusion.rows_own, f32[1280,128]{1,0:T(8,128)S(1)} %collective-permute-done.14.rows_other, ...), custom_call_target="tpu_custom_call" | custom-call | tf_op jit(solution)/shard_map/finish/pallas_call | solution.py:316
  (53 shorter events, 9.0 us)
Async XLA Ops:
  0.9 6.1 %collective-permute-start.3 = (f32[64,512]{1,0:T(8,128)S(1)}, f32[64,512]{1,0:T(8,128)S(1)}, u32[]{:S(2)}, u32[]{:S(2)}) collective-permute-start(f32[64,512]{1,0:T(8,128)S(1)} %dynamic-slice_bitcast_fusion), channel_id=1, source_target_pairs={{4,0},{12,8},{20,16},{28,24},{36,32},{44,40},{52,48},{60,56},{68,6... | collective-permute-start | bytes 393224 | tf_op jit(solution)/shard_map/ppermute | solution.py:350
  8.2 5.1 %collective-permute-start.4 = (f32[192,128]{1,0:T(8,128)S(1)}, f32[192,128]{1,0:T(8,128)S(1)}, u32[]{:S(2)}, u32[]{:S(2)}) collective-permute-start(f32[192,128]{1,0:T(8,128)S(1)} %get-tuple-element.13), channel_id=1, source_target_pairs={{0,64},{4,68},{1,65},{5,69},{2,66},{6,70},{3,67},{7,71}} | collective-permute-start | bytes 294920 | tf_op jit(solution)/shard_map/ppermute | solution.py:353
  9.7 4.0 %collective-permute-start.5 = (f32[192,128]{1,0:T(8,128)S(1)}, f32[192,128]{1,0:T(8,128)S(1)}, u32[]{:S(2)}, u32[]{:S(2)}) collective-permute-start(f32[192,128]{1,0:T(8,128)S(1)} %get-tuple-element.14), channel_id=1, source_target_pairs={{0,128},{4,132},{1,129},{5,133},{2,130},{6,134},{3,131},{7,135}} | collective-permute-start | bytes 294920 | tf_op jit(solution)/shard_map/ppermute | solution.py:353
  11.9 3.1 %collective-permute-start.6 = (f32[192,128]{1,0:T(8,128)S(1)}, f32[192,128]{1,0:T(8,128)S(1)}, u32[]{:S(2)}, u32[]{:S(2)}) collective-permute-start(f32[192,128]{1,0:T(8,128)S(1)} %get-tuple-element.15), channel_id=1, source_target_pairs={{0,192},{4,196},{1,193},{5,197},{2,194},{6,198},{3,195},{7,199}} | collective-permute-start | bytes 294920 | tf_op jit(solution)/shard_map/ppermute | solution.py:353
  15.0 7.2 %collective-permute-start.8 = (f32[192,128]{1,0:T(8,128)S(1)}, f32[192,128]{1,0:T(8,128)S(1)}, u32[]{:S(2)}, u32[]{:S(2)}) collective-permute-start(f32[192,128]{1,0:T(8,128)S(1)} %select_select_fusion), channel_id=1, source_target_pairs={{0,40},{4,44},{64,104},{68,108},{128,168},{132,172},{192,232},{196... | collective-permute-start | bytes 294920 | tf_op jit(solution)/shard_map/ppermute | solution.py:356
  17.1 5.2 %collective-permute-start.7 = (f32[192,128]{1,0:T(8,128)S(1)}, f32[192,128]{1,0:T(8,128)S(1)}, u32[]{:S(2)}, u32[]{:S(2)}) collective-permute-start(f32[192,128]{1,0:T(8,128)S(1)} %select_select_fusion), channel_id=1, source_target_pairs={{0,24},{4,28},{64,88},{68,92},{128,152},{132,156},{192,216},{196,2... | collective-permute-start | bytes 294920 | tf_op jit(solution)/shard_map/ppermute | solution.py:356
  18.4 11.6 %collective-permute-start.2 = (s32[2,128]{1,0:T(2,128)S(1)}, s32[2,128]{1,0:T(2,128)S(1)}, u32[]{:S(2)}, u32[]{:S(2)}) collective-permute-start(s32[2,128]{1,0:T(2,128)S(1)} %bitcast.8), channel_id=1, source_target_pairs={{0,3},{1,0},{2,1},{3,2},{4,7},{5,4},{6,5},{7,6},{8,11},{9,8},{10,9... | collective-permute-start | bytes 3080 | tf_op jit(solution)/shard_map/ppermute | solution.py:339
  21.2 10.4 %collective-permute-start.1 = (s32[2,128]{1,0:T(2,128)S(1)}, s32[2,128]{1,0:T(2,128)S(1)}, u32[]{:S(2)}, u32[]{:S(2)}) collective-permute-start(s32[2,128]{1,0:T(2,128)S(1)} %bitcast.9), channel_id=1, source_target_pairs={{0,2},{1,3},{2,0},{3,1},{4,6},{5,7},{6,4},{7,5},{8,10},{9,11},{10,... | collective-permute-start | bytes 3080 | tf_op jit(solution)/shard_map/ppermute | solution.py:339
  21.6 10.0 %collective-permute-start = (s32[2,128]{1,0:T(2,128)S(1)}, s32[2,128]{1,0:T(2,128)S(1)}, u32[]{:S(2)}, u32[]{:S(2)}) collective-permute-start(s32[2,128]{1,0:T(2,128)S(1)} %bitcast.10), channel_id=1, source_target_pairs={{0,1},{1,2},{2,3},{3,0},{4,5},{5,6},{6,7},{7,4},{8,9},{9,10},{10,1... | collective-permute-start | bytes 3080 | tf_op jit(solution)/shard_map/ppermute | solution.py:339
  22.3 14.1 %collective-permute-start.10 = (f32[192,128]{1,0:T(8,128)S(1)}, f32[192,128]{1,0:T(8,128)S(1)}, u32[]{:S(2)}, u32[]{:S(2)}) collective-permute-start(f32[192,128]{1,0:T(8,128)S(1)} %add_add_fusion.1), channel_id=1, source_target_pairs={{0,56},{4,60},{64,120},{68,124},{128,184},{132,188},{192,248},{196... | collective-permute-start | bytes 294920 | tf_op jit(solution)/shard_map/ppermute | solution.py:359
  23.6 12.8 %collective-permute-start.9 = (f32[192,128]{1,0:T(8,128)S(1)}, f32[192,128]{1,0:T(8,128)S(1)}, u32[]{:S(2)}, u32[]{:S(2)}) collective-permute-start(f32[192,128]{1,0:T(8,128)S(1)} %add_add_fusion.1), channel_id=1, source_target_pairs={{0,8},{4,12},{64,72},{68,76},{128,136},{132,140},{192,200},{196,20... | collective-permute-start | bytes 294920 | tf_op jit(solution)/shard_map/ppermute | solution.py:359
  30.0 38.7 %collective-permute-start.22 = (f32[512,512]{1,0:T(8,128)S(1)}, f32[512,512]{1,0:T(8,128)S(1)}, u32[]{:S(2)}, u32[]{:S(2)}) collective-permute-start(f32[512,512]{1,0:T(8,128)S(1)} %invert.1.inv_own), channel_id=1, source_target_pairs={{0,4},{4,0},{8,12},{12,8},{16,20},{20,16},{24,28},{28,24},{32,36},... | collective-permute-start | bytes 3145736 | tf_op jit(solution)/shard_map/ppermute | solution.py:374
  33.0 11.3 %all-to-all-start = ((f32[8,24,128]{2,1,0:T(8,128)}), f32[8,24,128]{2,1,0:T(8,128)S(1)}, u32[]{:S(2)}, u32[]{:S(2)}) async-start(f32[8,24,128]{2,1,0:T(8,128)} %get-tuple-element.16), calls=%async_computation | async-start | bytes 196608 | tf_op jit(solution)/shard_map/all_to_all | solution.py:364
  36.4 11.2 %collective-permute-start.17 = (f32[64,128]{1,0:T(8,128)S(1)}, f32[64,128]{1,0:T(8,128)S(1)}, u32[]{:S(2)}, u32[]{:S(2)}) collective-permute-start(f32[64,128]{1,0:T(8,128)S(1)} %get-tuple-element.17), channel_id=1, source_target_pairs={{0,192},{4,196},{8,200},{12,204},{16,208},{20,212},{24,216},{28,22... | collective-permute-start | bytes 98312 | tf_op jit(solution)/shard_map/ppermute | solution.py:339
  39.7 7.9 %collective-permute-start.16 = (f32[64,128]{1,0:T(8,128)S(1)}, f32[64,128]{1,0:T(8,128)S(1)}, u32[]{:S(2)}, u32[]{:S(2)}) collective-permute-start(f32[64,128]{1,0:T(8,128)S(1)} %get-tuple-element.17), channel_id=1, source_target_pairs={{0,128},{4,132},{8,136},{12,140},{16,144},{20,148},{24,152},{28,15... | collective-permute-start | bytes 98312 | tf_op jit(solution)/shard_map/ppermute | solution.py:339
  39.7 8.6 %collective-permute-start.15 = (f32[64,128]{1,0:T(8,128)S(1)}, f32[64,128]{1,0:T(8,128)}, u32[]{:S(2)}, u32[]{:S(2)}) collective-permute-start(f32[64,128]{1,0:T(8,128)S(1)} %get-tuple-element.17), channel_id=1, source_target_pairs={{0,64},{4,68},{8,72},{12,76},{16,80},{20,84},{24,88},{28,92},{32,9... | collective-permute-start | bytes 98312 | tf_op jit(solution)/shard_map/ppermute | solution.py:339
  44.3 16.0 %collective-permute-start.13 = (f32[320,128]{1,0:T(8,128)S(1)}, f32[320,128]{1,0:T(8,128)S(1)}, u32[]{:S(2)}, u32[]{:S(2)}) collective-permute-start(f32[320,128]{1,0:T(8,128)S(1)} %pad_maximum_fusion), channel_id=1, source_target_pairs={{0,192},{4,196},{8,200},{12,204},{16,208},{20,212},{24,216},{28,22... | collective-permute-start | bytes 491528 | tf_op jit(solution)/shard_map/ppermute | solution.py:339
  47.6 12.3 %collective-permute-start.12 = (f32[320,128]{1,0:T(8,128)S(1)}, f32[320,128]{1,0:T(8,128)S(1)}, u32[]{:S(2)}, u32[]{:S(2)}) collective-permute-start(f32[320,128]{1,0:T(8,128)S(1)} %pad_maximum_fusion), channel_id=1, source_target_pairs={{0,128},{4,132},{8,136},{12,140},{16,144},{20,148},{24,152},{28,15... | collective-permute-start | bytes 491528 | tf_op jit(solution)/shard_map/ppermute | solution.py:339
  47.6 10.7 %collective-permute-start.11 = (f32[320,128]{1,0:T(8,128)S(1)}, f32[320,128]{1,0:T(8,128)S(1)}, u32[]{:S(2)}, u32[]{:S(2)}) collective-permute-start(f32[320,128]{1,0:T(8,128)S(1)} %pad_maximum_fusion), channel_id=1, source_target_pairs={{0,64},{4,68},{8,72},{12,76},{16,80},{20,84},{24,88},{28,92},{32,9... | collective-permute-start | bytes 491528 | tf_op jit(solution)/shard_map/ppermute | solution.py:339
  49.1 18.7 %collective-permute-start.20 = (f32[256,128]{1,0:T(8,128)S(1)}, f32[256,128]{1,0:T(8,128)S(1)}, u32[]{:S(2)}, u32[]{:S(2)}) collective-permute-start(f32[256,128]{1,0:T(8,128)S(1)} %pad_maximum_fusion.1), channel_id=1, source_target_pairs={{0,3},{1,0},{2,1},{3,2},{4,7},{5,4},{6,5},{7,6},{8,11},{9,8},{10,9... | collective-permute-start | bytes 393224 | tf_op jit(solution)/shard_map/ppermute | solution.py:339
  58.4 9.4 %collective-permute-start.19 = (f32[256,128]{1,0:T(8,128)S(1)}, f32[256,128]{1,0:T(8,128)S(1)}, u32[]{:S(2)}, u32[]{:S(2)}) collective-permute-start(f32[256,128]{1,0:T(8,128)S(1)} %pad_maximum_fusion.1), channel_id=1, source_target_pairs={{0,2},{1,3},{2,0},{3,1},{4,6},{5,7},{6,4},{7,5},{8,10},{9,11},{10,... | collective-permute-start | bytes 393224 | tf_op jit(solution)/shard_map/ppermute | solution.py:339
  59.9 7.8 %collective-permute-start.18 = (f32[256,128]{1,0:T(8,128)S(1)}, f32[256,128]{1,0:T(8,128)S(1)}, u32[]{:S(2)}, u32[]{:S(2)}) collective-permute-start(f32[256,128]{1,0:T(8,128)S(1)} %pad_maximum_fusion.1), channel_id=1, source_target_pairs={{0,1},{1,2},{2,3},{3,0},{4,5},{5,6},{6,7},{7,4},{8,9},{9,10},{10,1... | collective-permute-start | bytes 393224 | tf_op jit(solution)/shard_map/ppermute | solution.py:339
  60.5 9.8 %collective-permute-start.14 = (f32[1280,128]{1,0:T(8,128)S(1)}, f32[1280,128]{1,0:T(8,128)S(1)}, u32[]{:S(2)}, u32[]{:S(2)}) collective-permute-start(f32[1280,128]{1,0:T(8,128)S(1)} %slice_dynamic-update-slice_fusion.rows_own), channel_id=1, source_target_pairs={{0,4},{4,0},{8,12},{12,8},{16,20},{20,16},{24,28},{28,24},{32,36},... | collective-permute-start | bytes 1966088 | tf_op jit(solution)/shard_map/ppermute | solution.py:371
  67.8 2.5 %collective-permute-start.21 = (f32[1024,128]{1,0:T(8,128)S(1)}, f32[1024,128]{1,0:T(8,128)S(1)}, u32[]{:S(2)}, u32[]{:S(2)}) collective-permute-start(f32[1024,128]{1,0:T(8,128)S(1)} %constant_dynamic-update-slice_fusion.2.factor_own), channel_id=1, source_target_pairs={{0,4},{4,0},{8,12},{12,8},{16,20},{20,16},{24,28},{28,24},{32,36},... | collective-permute-start | bytes 1572872 | tf_op jit(solution)/shard_map/ppermute | solution.py:372
  (2 other events, 41.8 us)

commit v4 on v3

--- a/solution.py
+++ b/solution.py
@@ -31,7 +31,6 @@
 
 SWAP = [(device(x, z, c), device(x, z, 1 - c)) for x, z, c in places()]
 DOWN = [(device(x, z, 1), device(x, z, 0)) for x, z, c in places() if c == 1]
-LINES = [[device(x, z, c) for z in range(ZS)] for x in range(XS) for c in range(2)]
 
 
 def along_x(step):
@@ -53,6 +52,19 @@
         for x in range(XS)
         for c in range(2)
     ]
+
+
+def across_z(bit):
+    return [(device(x, z, c), device(x, z ^ bit, c)) for x, z, c in places()]
+
+
+def pick(place, value, *others):
+    for spots, other in others:
+        here = place == spots[0]
+        for spot in spots[1:]:
+            here = here | (place == spot)
+        value = jnp.where(here, other, value)
+    return value
 
 
 def near(value):
@@ -138,6 +150,7 @@
     plane = lax.axis_index("cols")
     core = mine % 2
     x_mine = mine // (2 * ZS)
+    z_mine = mine // 2 % ZS
     lane = lax.broadcasted_iota(jnp.int32, (64, 128), 1)
     sub = lax.broadcasted_iota(jnp.int32, (64, 128), 0)
     row = lax.broadcasted_iota(jnp.int32, (128, 128), 0)
@@ -162,7 +175,7 @@
             top = top + ((x_mine - lax.shift_right_logical(here, 7)) & 3) * HEAD + (here & 127)
             far = jnp.where((owner & 1) == core, XS * HEAD, HALF + XS * HEAD)
             far = far + ((x_mine - lax.shift_right_logical(owner, 4)) & 3) * FAR
-            far = far + (lax.shift_right_logical(owner, 1) & 7) * MOVE + rank
+            far = far + ((lax.shift_right_logical(owner, 1) & 7) ^ z_mine) * MOVE + rank
             table[pl.ds(first + half, 1), :] = jnp.where(moved, far, top)
             local = lax.shift_right_logical(target, 15) * BLK + (target & (BLK - 1))
             taken = (sub == rank) & moved & (owner == mine)
@@ -173,7 +186,7 @@
     wide = lax.broadcasted_iota(jnp.int32, (32, 2 * BLK), 1)
     pick = jnp.where(wide == source[:32] - 1, 1.0, 0.0)
     rows = jnp.dot(pick, rhs[...], precision=HIGHEST, preferred_element_type=jnp.float32)
-    sent[...] = jnp.broadcast_to(rows[None, :MOVE], (ZS, MOVE, COLS))
+    sent[...] = rows[:MOVE]
 
 
 def choose(lists, flat):
@@ -182,7 +195,7 @@
         name="choose",
         compiler_params=ROOM,
         out_shape=(
-            jax.ShapeDtypeStruct((ZS, MOVE, COLS), jnp.float32),
+            jax.ShapeDtypeStruct((MOVE, COLS), jnp.float32),
             jax.ShapeDtypeStruct((16, 128), jnp.int32),
         ),
         in_specs=[VMEM] * 5,
@@ -351,18 +364,17 @@
     lists = spread(pivots.reshape(2, 128), "cols", [along_y(k) for k in (1, 2, 3)])
     staged = stage(rhs, multipliers, given)
     out = [lax.ppermute(staged[k], "rows", from_corner(k)) for k in (1, 2, 3)]
-    piece = jnp.where(x_mine == 0, staged[0], out[0] + out[1] + out[2])
-    piece = jnp.where(z_mine == 0, piece, 0.0)
+    piece = pick(x_mine, staged[0], ((1,), out[0]), ((2,), out[1]), ((3,), out[2]))
     out = [lax.ppermute(piece, "rows", along_z((0, k))) for k in (3, 5)]
-    piece = piece + out[0] + out[1]
+    piece = pick(z_mine, piece, ((3,), out[0]), ((5,), out[1]))
     out = [
         lax.ppermute(piece, "rows", along_z(*hops))
         for hops in (((0, 1), (3, 2), (5, 6)), ((0, 7), (3, 4)))
     ]
-    piece = piece + out[0] + out[1]
-    sent, table = choose(lists, flat)
-    far = lax.all_to_all(sent, "rows", 0, 0, axis_index_groups=LINES, tiled=True)
-    far = far.reshape(FAR, COLS)
+    piece = pick(z_mine, piece, ((1, 2, 6), out[0]), ((7, 4), out[1]))
+    far, table = choose(lists, flat)
+    for bit in (1, 2, 4):
+        far = jnp.concatenate([far, lax.ppermute(far, "rows", across_z(bit))])
     x_routes = [along_x(k) for k in (1, 2, 3)]
     factor = jnp.concatenate(spread(piece[HEAD:], "rows", x_routes))
     tops = spread(jnp.concatenate([piece[:HEAD], far]), "rows", x_routes)

time: 78.1 us -> 73.5 us (0.941)
  waiting for transfers between devices: 20 us -> 14.5 us
  starting transfers between devices: 39.7 us -> 42.9 us
    ppermute x1, starting transfers between devices: 0.95 us -> 6.02 us  [shards(): factor_other = lax.ppermute(factor, 'rows', SWAP)]
    ppermute x12, starting transfers between devices: 15.7 us -> 11.3 us  [spread(): return [value] + [lax.ppermute(value, axis, route) for route in routes]]
    all_to_all x1 -> x0, waiting for transfers between devices: 3.92 us -> none  [shards(): lax.all_to_all(sent, 'rows', 0, 0, axis_index_groups=LINES, tiled=True)]
    ppermute x12, waiting for transfers between devices: 11.9 us -> 8.39 us  [spread(): return [value] + [lax.ppermute(value, axis, route) for route in routes]]
    all_to_all x1 -> x0, starting transfers between devices: 3.36 us -> none  [shards(): lax.all_to_all(sent, 'rows', 0, 0, axis_index_groups=LINES, tiled=True)]
    ppermute x1, starting transfers between devices: 2 us -> 5.17 us  [shards(): rows_other = lax.ppermute(rows, 'rows', SWAP)]
    ppermute x3, starting transfers between devices: 5.04 us -> 7.11 us  [shards(): out = [lax.ppermute(staged[k], 'rows', from_corner(k)) for k in (1, 2, 3)]]
    ppermute x3, waiting for transfers between devices: 1.72 us -> 0.01 us  [shards(): out = [lax.ppermute(staged[k], 'rows', from_corner(k)) for k in (1, 2, 3)]]
  transfers between devices with their start and end apart: 24 -> 26, of which waited for: 7 -> 7; matrix products, arithmetic and copies ran while one was open for 2% -> 0% of each run, Pallas kernels for 8% -> 9%
where the time goes in v4:
time: 73.5 us; the launch traced here: 73.2 us
  starting transfers between devices  42.9 us (58%)
  waiting for transfers between devices  14.5 us (20%)
  Pallas kernels  14.1 us (19%)
  local copies, waits for them, and re-layouts  1.07 us (1%)
    ppermute x12, starting transfers between devices, spread(): return [value] + [lax.ppermute(value, axis, route) for route in routes]  11.3 us
    ppermute x12, waiting for transfers between devices, spread(): return [value] + [lax.ppermute(value, axis, route) for route in routes]  8.39 us
    pallas_call x1, Pallas kernels, finish(): pl.pallas_call(finish_kernel, name='finish', compiler_params=ROOM, out_sh...  7.13 us
    ppermute x3, starting transfers between devices, shards(): out = [lax.ppermute(staged[k], 'rows', from_corner(k)) for k in (1, 2, 3)]  7.11 us
    ppermute x1, starting transfers between devices, shards(): factor_other = lax.ppermute(factor, 'rows', SWAP)  6.02 us
    ppermute x1, starting transfers between devices, shards(): rows_other = lax.ppermute(rows, 'rows', SWAP)  5.17 us
    ppermute x1, starting transfers between devices, shards(): given = lax.ppermute(half, 'rows', DOWN)  5.11 us
    pallas_call x1, Pallas kernels, invert(): pl.pallas_call(invert_kernel, name='invert', compiler_params=ROOM, out_sh...  5.08 us
  transfers between devices with their start and end apart: 26, of which 7 were waited for; matrix products, arithmetic and copies ran while one was open for 0% of the time, Pallas kernels for 9%

profile of v4, /device:TPU:1, one launch (start us, length us, event | category | flops | bytes accessed | tf_op | source)
XLA Modules:
  0.0 73.2 jit_solution(4868646473680074561)
XLA Ops:
  0.0 0.9 %dynamic-slice_bitcast_fusion = f32[64,512]{1,0:T(8,128)S(1)} fusion(f32[2,2,512,512]{3,2,1,0:T(8,128)} %multipliers.1, s32[]{:T(128)S(6)} %select_n.67), kind=kLoop, calls=%fused_computation.1 | loop fusion | bytes 262148 | tf_op jit(solution)/shard_map/squeeze | solution.py:362
  0.9 5.1 %collective-permute-start.3 = (f32[64,512]{1,0:T(8,128)S(1)}, f32[64,512]{1,0:T(8,128)S(1)}, u32[]{:S(2)}, u32[]{:S(2)}) collective-permute-start(f32[64,512]{1,0:T(8,128)S(1)} %dynamic-slice_bitcast_fusion), channel_id=1, source_target_pairs={{4,0},{12,8},{20,16},{28,24},{36,32},{44,40},{52,48},{60,56},{68,6... | collective-permute-start | bytes 393224 | tf_op jit(solution)/shard_map/ppermute | solution.py:363
  6.0 1.1 %collective-permute-start.2 = (s32[2,128]{1,0:T(2,128)}, s32[2,128]{1,0:T(2,128)S(1)}, u32[]{:S(2)}, u32[]{:S(2)}) collective-permute-start(s32[2,128]{1,0:T(2,128)} %bitcast.7), channel_id=1, source_target_pairs={{0,3},{1,0},{2,1},{3,2},{4,7},{5,4},{6,5},{7,6},{8,11},{9,8},{10,9... | collective-permute-start | bytes 3080 | tf_op jit(solution)/shard_map/ppermute | solution.py:352
  7.5 1.1 %stage.1 = (f32[192,128]{1,0:T(8,128)S(1)}, f32[192,128]{1,0:T(8,128)S(1)}, f32[192,128]{1,0:T(8,128)S(1)}, f32[192,128]{1,0:T(8,128)S(1)}) custom-call(f32[2,512,128]{2,1,0:T(8,128)} %rhs.1, f32[2,2,512,512]{3,2,1,0:T(8,128)} %multipliers.1, f32[64,512]{1,0:T(8,128)S(1)} %collective-permute-done.3.given), custom_call_target="tpu_custom_call" | custom-call | tf_op jit(solution)/shard_map/stage/pallas_call | solution.py:137
  8.6 4.5 %collective-permute-start.4 = (f32[192,128]{1,0:T(8,128)S(1)}, f32[192,128]{1,0:T(8,128)S(1)}, u32[]{:S(2)}, u32[]{:S(2)}) collective-permute-start(f32[192,128]{1,0:T(8,128)S(1)} %get-tuple-element.12), channel_id=1, source_target_pairs={{0,192},{4,196},{1,193},{5,197},{2,194},{6,198},{3,195},{7,199}} | collective-permute-start | bytes 294920 | tf_op jit(solution)/shard_map/ppermute | solution.py:366
  13.2 1.3 %collective-permute-start.5 = (f32[192,128]{1,0:T(8,128)S(1)}, f32[192,128]{1,0:T(8,128)S(1)}, u32[]{:S(2)}, u32[]{:S(2)}) collective-permute-start(f32[192,128]{1,0:T(8,128)S(1)} %get-tuple-element.13), channel_id=1, source_target_pairs={{0,128},{4,132},{1,129},{5,133},{2,130},{6,134},{3,131},{7,135}} | collective-permute-start | bytes 294920 | tf_op jit(solution)/shard_map/ppermute | solution.py:366
  14.5 1.3 %collective-permute-start.6 = (f32[192,128]{1,0:T(8,128)S(1)}, f32[192,128]{1,0:T(8,128)S(1)}, u32[]{:S(2)}, u32[]{:S(2)}) collective-permute-start(f32[192,128]{1,0:T(8,128)S(1)} %get-tuple-element.14), channel_id=1, source_target_pairs={{0,64},{4,68},{1,65},{5,69},{2,66},{6,70},{3,67},{7,71}} | collective-permute-start | bytes 294920 | tf_op jit(solution)/shard_map/ppermute | solution.py:366
  15.8 5.1 %invert.1.inv_own = f32[512,512]{1,0:T(8,128)S(1)} custom-call(f32[2,512,512]{2,1,0:T(8,128)} %diag.1), custom_call_target="tpu_custom_call" | custom-call | flops 2000000000 | bytes 4194304 | tf_op jit(solution)/shard_map/invert/pallas_call | solution.py:250
  22.2 2.4 %collective-permute-done.piv1 = s32[2,128]{1,0:T(2,128)S(1)} collective-permute-done((s32[2,128]{1,0:T(2,128)S(1)}, s32[2,128]{1,0:T(2,128)S(1)}, u32[]{:S(2)}, u32[]{:S(2)}) %collective-permute-start) | collective-permute-done | bytes 1056 | tf_op jit(solution)/shard_map/ppermute | solution.py:352
  25.6 1.3 %collective-permute-start.8 = (f32[192,128]{1,0:T(8,128)S(1)}, f32[192,128]{1,0:T(8,128)S(1)}, u32[]{:S(2)}, u32[]{:S(2)}) collective-permute-start(f32[192,128]{1,0:T(8,128)S(1)} %select_select_fusion.2), channel_id=1, source_target_pairs={{0,24},{4,28},{64,88},{68,92},{128,152},{132,156},{192,216},{196,2... | collective-permute-start | bytes 294920 | tf_op jit(solution)/shard_map/ppermute | solution.py:368
  26.9 3.5 %collective-permute-start.7 = (f32[192,128]{1,0:T(8,128)S(1)}, f32[192,128]{1,0:T(8,128)S(1)}, u32[]{:S(2)}, u32[]{:S(2)}) collective-permute-start(f32[192,128]{1,0:T(8,128)S(1)} %select_select_fusion.2), channel_id=1, source_target_pairs={{0,40},{4,44},{64,104},{68,108},{128,168},{132,172},{192,232},{196... | collective-permute-start | bytes 294920 | tf_op jit(solution)/shard_map/ppermute | solution.py:368
  30.5 1.5 %collective-permute-done.7 = f32[192,128]{1,0:T(8,128)S(1)} collective-permute-done((f32[192,128]{1,0:T(8,128)S(1)}, f32[192,128]{1,0:T(8,128)S(1)}, u32[]{:S(2)}, u32[]{:S(2)}) %collective-permute-start.7) | collective-permute-done | bytes 98336 | tf_op jit(solution)/shard_map/ppermute | solution.py:368
  32.0 1.3 %collective-permute-start.10 = (f32[192,128]{1,0:T(8,128)S(1)}, f32[192,128]{1,0:T(8,128)S(1)}, u32[]{:S(2)}, u32[]{:S(2)}) collective-permute-start(f32[192,128]{1,0:T(8,128)S(1)} %select_select_fusion.1), channel_id=1, source_target_pairs={{0,8},{4,12},{64,72},{68,76},{128,136},{132,140},{192,200},{196,20... | collective-permute-start | bytes 294920 | tf_op jit(solution)/shard_map/ppermute | solution.py:371
  33.3 1.3 %collective-permute-start.9 = (f32[192,128]{1,0:T(8,128)S(1)}, f32[192,128]{1,0:T(8,128)S(1)}, u32[]{:S(2)}, u32[]{:S(2)}) collective-permute-start(f32[192,128]{1,0:T(8,128)S(1)} %select_select_fusion.1), channel_id=1, source_target_pairs={{0,56},{4,60},{64,120},{68,124},{128,184},{132,188},{192,248},{196... | collective-permute-start | bytes 294920 | tf_op jit(solution)/shard_map/ppermute | solution.py:371
  34.9 1.3 %collective-permute-done.9 = f32[192,128]{1,0:T(8,128)S(1)} collective-permute-done((f32[192,128]{1,0:T(8,128)S(1)}, f32[192,128]{1,0:T(8,128)S(1)}, u32[]{:S(2)}, u32[]{:S(2)}) %collective-permute-start.9) | collective-permute-done | bytes 98336 | tf_op jit(solution)/shard_map/ppermute | solution.py:371
  36.2 2.6 %collective-permute-start.20 = (f32[64,128]{1,0:T(8,128)S(1)}, f32[64,128]{1,0:T(8,128)S(1)}, u32[]{:S(2)}, u32[]{:S(2)}) collective-permute-start(f32[64,128]{1,0:T(8,128)S(1)} %get-tuple-element.17), channel_id=1, source_target_pairs={{0,192},{4,196},{8,200},{12,204},{16,208},{20,212},{24,216},{28,22... | collective-permute-start | bytes 98312 | tf_op jit(solution)/shard_map/ppermute | solution.py:352
  40.0 1.6 %collective-permute-done.13 = f32[96,128]{1,0:T(8,128)S(1)} collective-permute-done((f32[96,128]{1,0:T(8,128)S(1)}, f32[96,128]{1,0:T(8,128)S(1)}, u32[]{:S(2)}, u32[]{:S(2)}) %collective-permute-start.13) | collective-permute-done | bytes 49184 | tf_op jit(solution)/shard_map/ppermute | solution.py:377
  41.5 2.5 %collective-permute-start.16 = (f32[320,128]{1,0:T(8,128)S(1)}, f32[320,128]{1,0:T(8,128)S(1)}, u32[]{:S(2)}, u32[]{:S(2)}) collective-permute-start(f32[320,128]{1,0:T(8,128)S(1)} %constant_dynamic-update-slice_fusion), channel_id=1, source_target_pairs={{0,192},{4,196},{8,200},{12,204},{16,208},{20,212},{24,216},{28,22... | collective-permute-start | bytes 491528 | tf_op jit(solution)/shard_map/ppermute | solution.py:352
  45.5 5.9 %collective-permute-done.14 = f32[320,128]{1,0:T(8,128)S(1)} collective-permute-done((f32[320,128]{1,0:T(8,128)S(1)}, f32[320,128]{1,0:T(8,128)S(1)}, u32[]{:S(2)}, u32[]{:S(2)}) %collective-permute-start.14) | collective-permute-done | bytes 163872 | tf_op jit(solution)/shard_map/ppermute | solution.py:352
  51.5 1.4 %collective-permute-start.22 = (f32[256,128]{1,0:T(8,128)S(1)}, f32[256,128]{1,0:T(8,128)S(1)}, u32[]{:S(2)}, u32[]{:S(2)}) collective-permute-start(f32[256,128]{1,0:T(8,128)S(1)} %pad_maximum_fusion), channel_id=1, source_target_pairs={{0,2},{1,3},{2,0},{3,1},{4,6},{5,7},{6,4},{7,5},{8,10},{9,11},{10,... | collective-permute-start | bytes 393224 | tf_op jit(solution)/shard_map/ppermute | solution.py:352
  53.1 5.2 %collective-permute-start.17 = (f32[1280,128]{1,0:T(8,128)S(1)}, f32[1280,128]{1,0:T(8,128)S(1)}, u32[]{:S(2)}, u32[]{:S(2)}) collective-permute-start(f32[1280,128]{1,0:T(8,128)S(1)} %slice_dynamic-update-slice_fusion.rows_own), channel_id=1, source_target_pairs={{0,4},{4,0},{8,12},{12,8},{16,20},{20,16},{24,28},{28,24},{32,36},... | collective-permute-start | bytes 1966088 | tf_op jit(solution)/shard_map/ppermute | solution.py:383
  58.4 6.0 %collective-permute-start.24 = (f32[1024,128]{1,0:T(8,128)S(1)}, f32[1024,128]{1,0:T(8,128)S(1)}, u32[]{:S(2)}, u32[]{:S(2)}) collective-permute-start(f32[1024,128]{1,0:T(8,128)S(1)} %constant_dynamic-update-slice_fusion.8.factor_own), channel_id=1, source_target_pairs={{0,4},{4,0},{8,12},{12,8},{16,20},{20,16},{24,28},{28,24},{32,36},... | collective-permute-start | bytes 1572872 | tf_op jit(solution)/shard_map/ppermute | solution.py:384
  64.4 1.5 %collective-permute-done.24.factor_other = f32[1024,128]{1,0:T(8,128)S(1)} collective-permute-done((f32[1024,128]{1,0:T(8,128)S(1)}, f32[1024,128]{1,0:T(8,128)S(1)}, u32[]{:S(2)}, u32[]{:S(2)}) %collective-permute-start.24) | collective-permute-done | bytes 524320 | tf_op jit(solution)/shard_map/ppermute | solution.py:384
  65.9 7.1 %finish.1 = f32[1024,128]{1,0:T(8,128)} custom-call(s32[16,128]{1,0:T(8,128)S(1)} %get-tuple-element.11.table, f32[1024,128]{1,0:T(8,128)} %bitcast.5, f32[2,2,512,512]{3,2,1,0:T(8,128)} %multipliers.1, f32[1280,128]{1,0:T(8,128)S(1)} %slice_dynamic-update-slice_fusion.rows_own, f32[1280,128]{1,0:T(8,128)S(1)} %collective-permute-done.17.rows_other, ...), custom_call_target="tpu_custom_call" | custom-call | tf_op jit(solution)/shard_map/finish/pallas_call | solution.py:329
  (65 shorter events, 5.8 us)
Async XLA Ops:
  0.9 6.6 %collective-permute-start.3 = (f32[64,512]{1,0:T(8,128)S(1)}, f32[64,512]{1,0:T(8,128)S(1)}, u32[]{:S(2)}, u32[]{:S(2)}) collective-permute-start(f32[64,512]{1,0:T(8,128)S(1)} %dynamic-slice_bitcast_fusion), channel_id=1, source_target_pairs={{4,0},{12,8},{20,16},{28,24},{36,32},{44,40},{52,48},{60,56},{68,6... | collective-permute-start | bytes 393224 | tf_op jit(solution)/shard_map/ppermute | solution.py:363
  6.0 14.9 %collective-permute-start.2 = (s32[2,128]{1,0:T(2,128)}, s32[2,128]{1,0:T(2,128)S(1)}, u32[]{:S(2)}, u32[]{:S(2)}) collective-permute-start(s32[2,128]{1,0:T(2,128)} %bitcast.7), channel_id=1, source_target_pairs={{0,3},{1,0},{2,1},{3,2},{4,7},{5,4},{6,5},{7,6},{8,11},{9,8},{10,9... | collective-permute-start | bytes 3080 | tf_op jit(solution)/shard_map/ppermute | solution.py:352
  7.1 14.5 %collective-permute-start.1 = (s32[2,128]{1,0:T(2,128)}, s32[2,128]{1,0:T(2,128)S(1)}, u32[]{:S(2)}, u32[]{:S(2)}) collective-permute-start(s32[2,128]{1,0:T(2,128)} %bitcast.8), channel_id=1, source_target_pairs={{0,2},{1,3},{2,0},{3,1},{4,6},{5,7},{6,4},{7,5},{8,10},{9,11},{10,... | collective-permute-start | bytes 3080 | tf_op jit(solution)/shard_map/ppermute | solution.py:352
  8.6 16.9 %collective-permute-start.4 = (f32[192,128]{1,0:T(8,128)S(1)}, f32[192,128]{1,0:T(8,128)S(1)}, u32[]{:S(2)}, u32[]{:S(2)}) collective-permute-start(f32[192,128]{1,0:T(8,128)S(1)} %get-tuple-element.12), channel_id=1, source_target_pairs={{0,192},{4,196},{1,193},{5,197},{2,194},{6,198},{3,195},{7,199}} | collective-permute-start | bytes 294920 | tf_op jit(solution)/shard_map/ppermute | solution.py:366
  13.2 12.3 %collective-permute-start.5 = (f32[192,128]{1,0:T(8,128)S(1)}, f32[192,128]{1,0:T(8,128)S(1)}, u32[]{:S(2)}, u32[]{:S(2)}) collective-permute-start(f32[192,128]{1,0:T(8,128)S(1)} %get-tuple-element.13), channel_id=1, source_target_pairs={{0,128},{4,132},{1,129},{5,133},{2,130},{6,134},{3,131},{7,135}} | collective-permute-start | bytes 294920 | tf_op jit(solution)/shard_map/ppermute | solution.py:366
  14.5 11.0 %collective-permute-start.6 = (f32[192,128]{1,0:T(8,128)S(1)}, f32[192,128]{1,0:T(8,128)S(1)}, u32[]{:S(2)}, u32[]{:S(2)}) collective-permute-start(f32[192,128]{1,0:T(8,128)S(1)} %get-tuple-element.14), channel_id=1, source_target_pairs={{0,64},{4,68},{1,65},{5,69},{2,66},{6,70},{3,67},{7,71}} | collective-permute-start | bytes 294920 | tf_op jit(solution)/shard_map/ppermute | solution.py:366
  20.9 3.7 %collective-permute-start = (s32[2,128]{1,0:T(2,128)S(1)}, s32[2,128]{1,0:T(2,128)S(1)}, u32[]{:S(2)}, u32[]{:S(2)}) collective-permute-start(s32[2,128]{1,0:T(2,128)S(1)} %bitcast.9), channel_id=1, source_target_pairs={{0,1},{1,2},{2,3},{3,0},{4,5},{5,6},{6,7},{7,4},{8,9},{9,10},{10,1... | collective-permute-start | bytes 3080 | tf_op jit(solution)/shard_map/ppermute | solution.py:352
  21.7 42.7 %collective-permute-start.25 = (f32[512,512]{1,0:T(8,128)S(1)}, f32[512,512]{1,0:T(8,128)S(1)}, u32[]{:S(2)}, u32[]{:S(2)}) collective-permute-start(f32[512,512]{1,0:T(8,128)S(1)} %invert.1.inv_own), channel_id=1, source_target_pairs={{0,4},{4,0},{8,12},{12,8},{16,20},{20,16},{24,28},{28,24},{32,36},... | collective-permute-start | bytes 3145736 | tf_op jit(solution)/shard_map/ppermute | solution.py:386
  25.4 4.9 %collective-permute-start.11 = (f32[24,128]{1,0:T(8,128)S(1)}, f32[24,128]{1,0:T(8,128)S(1)}, u32[]{:S(2)}, u32[]{:S(2)}) collective-permute-start(f32[24,128]{1,0:T(8,128)S(1)} %get-tuple-element.16), channel_id=1, source_target_pairs={{0,8},{4,12},{8,0},{12,4},{16,24},{20,28},{24,16},{28,20},{32,40},... | collective-permute-start | bytes 36872 | tf_op jit(solution)/shard_map/ppermute | solution.py:377
  25.6 4.9 %collective-permute-start.8 = (f32[192,128]{1,0:T(8,128)S(1)}, f32[192,128]{1,0:T(8,128)S(1)}, u32[]{:S(2)}, u32[]{:S(2)}) collective-permute-start(f32[192,128]{1,0:T(8,128)S(1)} %select_select_fusion.2), channel_id=1, source_target_pairs={{0,24},{4,28},{64,88},{68,92},{128,152},{132,156},{192,216},{196,2... | collective-permute-start | bytes 294920 | tf_op jit(solution)/shard_map/ppermute | solution.py:368
  26.9 5.1 %collective-permute-start.7 = (f32[192,128]{1,0:T(8,128)S(1)}, f32[192,128]{1,0:T(8,128)S(1)}, u32[]{:S(2)}, u32[]{:S(2)}) collective-permute-start(f32[192,128]{1,0:T(8,128)S(1)} %select_select_fusion.2), channel_id=1, source_target_pairs={{0,40},{4,44},{64,104},{68,108},{128,168},{132,172},{192,232},{196... | collective-permute-start | bytes 294920 | tf_op jit(solution)/shard_map/ppermute | solution.py:368
  30.3 4.2 %collective-permute-start.12 = (f32[48,128]{1,0:T(8,128)S(1)}, f32[48,128]{1,0:T(8,128)S(1)}, u32[]{:S(2)}, u32[]{:S(2)}) collective-permute-start(f32[48,128]{1,0:T(8,128)S(1)} %pad_maximum_fusion.2), channel_id=1, source_target_pairs={{0,16},{4,20},{8,24},{12,28},{16,0},{20,4},{24,8},{28,12},{32,48},... | collective-permute-start | bytes 73736 | tf_op jit(solution)/shard_map/ppermute | solution.py:377
  34.6 6.9 %collective-permute-start.13 = (f32[96,128]{1,0:T(8,128)S(1)}, f32[96,128]{1,0:T(8,128)S(1)}, u32[]{:S(2)}, u32[]{:S(2)}) collective-permute-start(f32[96,128]{1,0:T(8,128)S(1)} %pad_maximum_fusion.1), channel_id=1, source_target_pairs={{0,32},{4,36},{8,40},{12,44},{16,48},{20,52},{24,56},{28,60},{32,0... | collective-permute-start | bytes 147464 | tf_op jit(solution)/shard_map/ppermute | solution.py:377
  36.2 7.8 %collective-permute-start.20 = (f32[64,128]{1,0:T(8,128)S(1)}, f32[64,128]{1,0:T(8,128)S(1)}, u32[]{:S(2)}, u32[]{:S(2)}) collective-permute-start(f32[64,128]{1,0:T(8,128)S(1)} %get-tuple-element.17), channel_id=1, source_target_pairs={{0,192},{4,196},{8,200},{12,204},{16,208},{20,212},{24,216},{28,22... | collective-permute-start | bytes 98312 | tf_op jit(solution)/shard_map/ppermute | solution.py:352
  38.8 5.8 %collective-permute-start.19 = (f32[64,128]{1,0:T(8,128)S(1)}, f32[64,128]{1,0:T(8,128)S(1)}, u32[]{:S(2)}, u32[]{:S(2)}) collective-permute-start(f32[64,128]{1,0:T(8,128)S(1)} %get-tuple-element.17), channel_id=1, source_target_pairs={{0,128},{4,132},{8,136},{12,140},{16,144},{20,148},{24,152},{28,15... | collective-permute-start | bytes 98312 | tf_op jit(solution)/shard_map/ppermute | solution.py:352
  39.3 5.9 %collective-permute-start.18 = (f32[64,128]{1,0:T(8,128)S(1)}, f32[64,128]{1,0:T(8,128)S(1)}, u32[]{:S(2)}, u32[]{:S(2)}) collective-permute-start(f32[64,128]{1,0:T(8,128)S(1)} %get-tuple-element.17), channel_id=1, source_target_pairs={{0,64},{4,68},{8,72},{12,76},{16,80},{20,84},{24,88},{28,92},{32,9... | collective-permute-start | bytes 98312 | tf_op jit(solution)/shard_map/ppermute | solution.py:352
  41.5 11.4 %collective-permute-start.16 = (f32[320,128]{1,0:T(8,128)S(1)}, f32[320,128]{1,0:T(8,128)S(1)}, u32[]{:S(2)}, u32[]{:S(2)}) collective-permute-start(f32[320,128]{1,0:T(8,128)S(1)} %constant_dynamic-update-slice_fusion), channel_id=1, source_target_pairs={{0,192},{4,196},{8,200},{12,204},{16,208},{20,212},{24,216},{28,22... | collective-permute-start | bytes 491528 | tf_op jit(solution)/shard_map/ppermute | solution.py:352
  44.0 8.9 %collective-permute-start.15 = (f32[320,128]{1,0:T(8,128)S(1)}, f32[320,128]{1,0:T(8,128)S(1)}, u32[]{:S(2)}, u32[]{:S(2)}) collective-permute-start(f32[320,128]{1,0:T(8,128)S(1)} %constant_dynamic-update-slice_fusion), channel_id=1, source_target_pairs={{0,128},{4,132},{8,136},{12,140},{16,144},{20,148},{24,152},{28,15... | collective-permute-start | bytes 491528 | tf_op jit(solution)/shard_map/ppermute | solution.py:352
  44.5 6.9 %collective-permute-start.14 = (f32[320,128]{1,0:T(8,128)S(1)}, f32[320,128]{1,0:T(8,128)S(1)}, u32[]{:S(2)}, u32[]{:S(2)}) collective-permute-start(f32[320,128]{1,0:T(8,128)S(1)} %constant_dynamic-update-slice_fusion), channel_id=1, source_target_pairs={{0,64},{4,68},{8,72},{12,76},{16,80},{20,84},{24,88},{28,92},{32,9... | collective-permute-start | bytes 491528 | tf_op jit(solution)/shard_map/ppermute | solution.py:352
  45.2 13.2 %collective-permute-start.23 = (f32[256,128]{1,0:T(8,128)S(1)}, f32[256,128]{1,0:T(8,128)S(1)}, u32[]{:S(2)}, u32[]{:S(2)}) collective-permute-start(f32[256,128]{1,0:T(8,128)S(1)} %pad_maximum_fusion), channel_id=1, source_target_pairs={{0,3},{1,0},{2,1},{3,2},{4,7},{5,4},{6,5},{7,6},{8,11},{9,8},{10,9... | collective-permute-start | bytes 393224 | tf_op jit(solution)/shard_map/ppermute | solution.py:352
  51.5 6.9 %collective-permute-start.22 = (f32[256,128]{1,0:T(8,128)S(1)}, f32[256,128]{1,0:T(8,128)S(1)}, u32[]{:S(2)}, u32[]{:S(2)}) collective-permute-start(f32[256,128]{1,0:T(8,128)S(1)} %pad_maximum_fusion), channel_id=1, source_target_pairs={{0,2},{1,3},{2,0},{3,1},{4,6},{5,7},{6,4},{7,5},{8,10},{9,11},{10,... | collective-permute-start | bytes 393224 | tf_op jit(solution)/shard_map/ppermute | solution.py:352
  52.9 5.4 %collective-permute-start.21 = (f32[256,128]{1,0:T(8,128)S(1)}, f32[256,128]{1,0:T(8,128)S(1)}, u32[]{:S(2)}, u32[]{:S(2)}) collective-permute-start(f32[256,128]{1,0:T(8,128)S(1)} %pad_maximum_fusion), channel_id=1, source_target_pairs={{0,1},{1,2},{2,3},{3,0},{4,5},{5,6},{6,7},{7,4},{8,9},{9,10},{10,1... | collective-permute-start | bytes 393224 | tf_op jit(solution)/shard_map/ppermute | solution.py:352
  53.1 12.8 %collective-permute-start.17 = (f32[1280,128]{1,0:T(8,128)S(1)}, f32[1280,128]{1,0:T(8,128)S(1)}, u32[]{:S(2)}, u32[]{:S(2)}) collective-permute-start(f32[1280,128]{1,0:T(8,128)S(1)} %slice_dynamic-update-slice_fusion.rows_own), channel_id=1, source_target_pairs={{0,4},{4,0},{8,12},{12,8},{16,20},{20,16},{24,28},{28,24},{32,36},... | collective-permute-start | bytes 1966088 | tf_op jit(solution)/shard_map/ppermute | solution.py:383
  58.4 7.6 %collective-permute-start.24 = (f32[1024,128]{1,0:T(8,128)S(1)}, f32[1024,128]{1,0:T(8,128)S(1)}, u32[]{:S(2)}, u32[]{:S(2)}) collective-permute-start(f32[1024,128]{1,0:T(8,128)S(1)} %constant_dynamic-update-slice_fusion.8.factor_own), channel_id=1, source_target_pairs={{0,4},{4,0},{8,12},{12,8},{16,20},{20,16},{24,28},{28,24},{32,36},... | collective-permute-start | bytes 1572872 | tf_op jit(solution)/shard_map/ppermute | solution.py:384
  (4 other events, 34.1 us)

commit v5 on v4

--- a/solution.py
+++ b/solution.py
@@ -203,29 +203,35 @@
     )(*map(near, lists), flat)
 
 
-def invert_kernel(diag, out, work, load):
+def invert_kernel(diag, rhs, multipliers, out, kept, lower, block, work, sems):
     core = lax.axis_index("rows") % 2
-    copy = pltpu.make_async_copy(diag.at[core], out, load)
+    copy = pltpu.make_async_copy(diag.at[core], block, sems.at[0])
     copy.start()
+    loads = [
+        pltpu.make_async_copy(multipliers, lower, sems.at[1]),
+        pltpu.make_async_copy(rhs, kept, sems.at[2]),
+    ]
+    for load in loads:
+        load.start()
     copy.wait()
     row = lax.broadcasted_iota(jnp.int32, (128, 128), 0)
     col = lax.broadcasted_iota(jnp.int32, (128, 128), 1)
 
-    def block(b):
-        return out[128 * b : 128 * (b + 1), 128 * b : 128 * (b + 1)]
+    def square(b):
+        return block[128 * b : 128 * (b + 1), 128 * b : 128 * (b + 1)]
 
     for b in range(4):
         pair = (row // 2 == col // 2) & (row > col)
         unit = jnp.where(row == col, 1.0, 0.0)
-        work[b] = unit - jnp.where(pair, block(b), 0.0)
+        work[b] = unit - jnp.where(pair, square(b), 0.0)
 
     def level(step, carry):
         shift = step + 1
         tile_row = lax.shift_right_logical(row, shift)
-        near = (tile_row % 2 == 1) & (lax.shift_right_logical(col, shift) == tile_row - 1)
+        below = (tile_row % 2 == 1) & (lax.shift_right_logical(col, shift) == tile_row - 1)
         firsts = []
         for b in range(4):
-            firsts.append(times(jnp.where(near, block(b), 0.0), work[b]))
+            firsts.append(times(jnp.where(below, square(b), 0.0), work[b]))
         for b in range(4):
             work[b] = work[b] - times(work[b], firsts[b])
         return carry
@@ -236,116 +242,123 @@
         first = work[2 * half]
         second = work[2 * half + 1]
         at = 256 * half
-        below = -times(second, times(out[at + 128 : at + 256, at : at + 128], first))
+        below = -times(second, times(block[at + 128 : at + 256, at : at + 128], first))
         top = jnp.concatenate([first, jnp.zeros((128, 128), jnp.float32)], axis=1)
         bottom = jnp.concatenate([below, second], axis=1)
         tops.append(jnp.concatenate([top, bottom], axis=0))
-    out[256:512, 0:256] = -times(tops[1], times(out[256:512, 0:256], tops[0]))
-    out[0:256, 0:256] = tops[0]
-    out[256:512, 256:512] = tops[1]
-    out[0:256, 256:512] = jnp.zeros((256, 256), jnp.float32)
-
-
-def invert(diag):
+    out[0] = tops[0]
+    out[1] = -times(tops[1], times(block[256:512, 0:256], tops[0]))
+    out[2] = tops[1]
+    for load in loads:
+        load.wait()
+
+
+def invert(diag, flat, multipliers):
     return pl.pallas_call(
         invert_kernel,
         name="invert",
         compiler_params=ROOM,
-        out_shape=jax.ShapeDtypeStruct((BLK, BLK), jnp.float32),
-        in_specs=[HBM],
-        out_specs=VMEM,
-        scratch_shapes=[pltpu.VMEM((4, 128, 128), jnp.float32), pltpu.SemaphoreType.DMA],
+        out_shape=(
+            jax.ShapeDtypeStruct((3, 256, 256), jnp.float32),
+            jax.ShapeDtypeStruct((2 * BLK, COLS), jnp.float32),
+            jax.ShapeDtypeStruct((2, 2, BLK, BLK), jnp.float32),
+        ),
+        in_specs=[HBM] * 3,
+        out_specs=(VMEM,) * 3,
+        scratch_shapes=[
+            pltpu.VMEM((BLK, BLK), jnp.float32),
+            pltpu.VMEM((4, 128, 128), jnp.float32),
+            pltpu.SemaphoreType.DMA((3,)),
+        ],
         cost_estimate=pl.CostEstimate(
             flops=2 * 10**9, bytes_accessed=4 * 2**20, transcendentals=0
         ),
-    )(away(diag))
+    )(away(diag), away(flat), away(multipliers))
 
 
 def finish_kernel(
-    table, rhs, multipliers, rows_own, rows_other, factor_own, factor_other, inv_own, inv_other,
-    out, lower, pool, panel, l21_high, l21_low, inverse, sems,
+    table, kept, lower, rows_own, rows_other, factor_own, factor_other, inv_own, inv_other,
+    out, base, pool, panel, l21_high, l21_low, sems,
 ):
     mine = lax.axis_index("rows")
     plane = lax.axis_index("cols")
     core = mine % 2
     x_mine = mine // (2 * ZS)
-    kept = pltpu.make_async_copy(rhs, out, sems.at[0])
-    kept.start()
-    loads = [pltpu.make_async_copy(multipliers.at[k], lower.at[k], sems.at[1 + k]) for k in range(2)]
-    for load in loads:
-        load.start()
+    base[...] = kept[...]
     pool[:HALF, :] = rows_own[...]
     pool[HALF:, :] = rows_other[...]
-
     for part in range(8):
-
-        def gather(i, carry, part=part):
-            for k in range(8):
-                spot = i * 8 + k
-                panel[pl.ds(128 * part + spot, 1), :] = pool[pl.ds(table[part, spot], 1), :]
-            return carry
-
-        lax.fori_loop(0, 16, gather, 0)
-    kept.wait()
-    for k in range(MOVE):
-        source = table[8, k]
-
-        @pl.when(source >= 0)
-        def _(source=source, k=k):
-            out[pl.ds(source, 1), :] = pool[pl.ds(table[9, k], 1), :]
-
+        for spot in range(128):
+            panel[pl.ds(128 * part + spot, 1), :] = pool[pl.ds(table[part, spot], 1), :]
+
+    def solve(which, high, low):
+        own = core == which
+        blocks = [halves(jnp.where(own, inv_own[k], inv_other[k])) for k in range(3)]
+        width = high.shape[1]
+
+        def part(block, rows):
+            both = dot(block[0], jnp.concatenate([high[rows], low[rows]], axis=1))
+            return both[:, :width] + both[:, width:] + dot(block[1], high[rows])
+
+        top, bottom = slice(0, 256), slice(256, 512)
+        return jnp.concatenate(
+            [part(blocks[0], top), part(blocks[1], top) + part(blocks[2], bottom)], axis=0
+        )
+
+    first = solve(0, *halves(panel[:BLK, :]))
     for step_y in range(PLANES):
         for step_x in range(XS):
             at = (step_y * XS + step_x) * FACTOR
             for side, source in ((0, factor_own), (1, factor_other)):
-                first = ((plane - step_y) & 3) * 128 + ((core + side) & 1) * 64
-                first = pl.multiple_of(first + ((x_mine - step_x) & 3) * 16, 16)
+                to = ((plane - step_y) & 3) * 128 + ((core + side) & 1) * 64
+                to = pl.multiple_of(to + ((x_mine - step_x) & 3) * 16, 16)
                 for col in range(4):
                     high, low = halves(source[at + 16 * col : at + 16 * (col + 1), :])
-                    l21_high[pl.ds(first, 16), 128 * col : 128 * (col + 1)] = high
-                    l21_low[pl.ds(first, 16), 128 * col : 128 * (col + 1)] = low
-    inverse[core] = inv_own[...]
-    inverse[1 - core] = inv_other[...]
-    first = times(inverse[0], panel[:BLK, :])
+                    l21_high[pl.ds(to, 16), 128 * col : 128 * (col + 1)] = high
+                    l21_low[pl.ds(to, 16), 128 * col : 128 * (col + 1)] = low
     rest = panel[BLK:, :] - product(l21_high[...], l21_low[...], first)
-    second = times(inverse[1], rest)
-    for load in loads:
-        load.wait()
+    second = solve(1, *halves(rest))
+    for k in range(MOVE):
+        source = table[8, k]
+
+        @pl.when(source >= 0)
+        def _(source=source, k=k):
+            base[pl.ds(source, 1), :] = pool[pl.ds(table[9, k], 1), :]
+
+    stores = []
     for cycle in range(2):
         rows = slice(BLK * cycle, BLK * (cycle + 1))
         taken = times(lower[0, cycle], first) + times(lower[1, cycle], second)
-        out[rows, :] = out[rows, :] - taken
-
-    @pl.when(mine == 0)
-    def _():
-        out[:BLK, :] = first
-
-    @pl.when(mine == 1)
-    def _():
-        out[:BLK, :] = second
-
-
-def finish(table, flat, multipliers, rows, rows_other, factor, factor_other, inverse, inverse_other):
+        value = base[rows, :] - taken
+        if cycle == 0:
+            value = jnp.where(mine == 0, first, jnp.where(mine == 1, second, value))
+        base[rows, :] = value
+        store = pltpu.make_async_copy(
+            base.at[pl.ds(BLK * cycle, BLK)], out.at[pl.ds(BLK * cycle, BLK)], sems.at[cycle]
+        )
+        store.start()
+        stores.append(store)
+    for store in stores:
+        store.wait()
+
+
+def finish(table, *operands):
     return pl.pallas_call(
         finish_kernel,
         name="finish",
         compiler_params=ROOM,
         out_shape=jax.ShapeDtypeStruct((2 * BLK, COLS), jnp.float32),
-        in_specs=[SMEM, HBM, HBM] + [VMEM] * 6,
-        out_specs=VMEM,
+        in_specs=[SMEM] + [VMEM] * 8,
+        out_specs=HBM,
         scratch_shapes=[
-            pltpu.VMEM((2, 2, BLK, BLK), jnp.float32),
+            pltpu.VMEM((2 * BLK, COLS), jnp.float32),
             pltpu.VMEM((2 * HALF, COLS), jnp.float32),
             pltpu.VMEM((2 * BLK, COLS), jnp.float32),
             pltpu.VMEM((BLK, BLK), jnp.bfloat16),
             pltpu.VMEM((BLK, BLK), jnp.bfloat16),
-            pltpu.VMEM((2, BLK, BLK), jnp.float32),
-            pltpu.SemaphoreType.DMA((3,)),
+            pltpu.SemaphoreType.DMA((2,)),
         ],
-    )(
-        table, away(flat), away(multipliers), near(rows), near(rows_other),
-        near(factor), near(factor_other), near(inverse), near(inverse_other),
-    )
+    )(table, *map(near, operands))
 
 
 def spread(value, axis, routes):
@@ -382,10 +395,10 @@
     factor = jnp.concatenate(spread(factor, "cols", [along_y(k) for k in (1, 2, 3)]))
     rows_other = lax.ppermute(rows, "rows", SWAP)
     factor_other = lax.ppermute(factor, "rows", SWAP)
-    inverse = invert(diag_blocks)
+    inverse, kept, lower = invert(diag_blocks, flat, multipliers)
     inverse_other = lax.ppermute(inverse, "rows", SWAP)
     solved = finish(
-        table, flat, multipliers, rows, rows_other, factor, factor_other,
+        table, kept, lower, rows, rows_other, factor, factor_other,
         inverse, inverse_other,
     )
     return solved.reshape(cycles, blk, columns)

time: 73.5 us -> 72.8 us (level)
  Pallas kernels: 14.1 us -> 11.5 us
  local copies, waits for them, and re-layouts: 1.07 us -> 3.03 us
    pallas_call x1, Pallas kernels: 7.13 us -> 4.5 us  [finish(): pl.pallas_call(finish_kernel, name='finish', compiler_params=ROOM, out_sh...]
    unnamed x22 -> x26, local copies, waits for them, and re-layouts: 0.13 us -> 2.08 us
  transfers between devices with their start and end apart: 26 -> 26, of which waited for: 7 -> 7; matrix products, arithmetic and copies ran while one was open for 0% -> 0% of each run, Pallas kernels for 9% -> 10%
where the time goes in v5:
time: 72.8 us; the launch traced here: 72.5 us
  starting transfers between devices  42.8 us (59%)
  waiting for transfers between devices  14.5 us (20%)
  Pallas kernels  11.5 us (16%)
  local copies, waits for them, and re-layouts  3.03 us (4%)
    ppermute x12, starting transfers between devices, spread(): return [value] + [lax.ppermute(value, axis, route) for route in routes]  11.3 us
    ppermute x12, waiting for transfers between devices, spread(): return [value] + [lax.ppermute(value, axis, route) for route in routes]  8.36 us
    ppermute x3, starting transfers between devices, shards(): out = [lax.ppermute(staged[k], 'rows', from_corner(k)) for k in (1, 2, 3)]  7.11 us
    ppermute x1, starting transfers between devices, shards(): factor_other = lax.ppermute(factor, 'rows', SWAP)  6.02 us
    ppermute x1, starting transfers between devices, shards(): rows_other = lax.ppermute(rows, 'rows', SWAP)  5.19 us
    pallas_call x1, Pallas kernels, invert(): pl.pallas_call(invert_kernel, name='invert', compiler_params=ROOM, out_sh...  5.12 us
    ppermute x1, starting transfers between devices, shards(): given = lax.ppermute(half, 'rows', DOWN)  5.11 us
    ppermute x2, starting transfers between devices, shards(): out = [lax.ppermute(piece, 'rows', along_z((0, k))) for k in (3, 5)]  4.75 us
  transfers between devices with their start and end apart: 26, of which 7 were waited for; matrix products, arithmetic and copies ran while one was open for 0% of the time, Pallas kernels for 10%

profile of v5, /device:TPU:1, one launch (start us, length us, event | category | flops | bytes accessed | tf_op | source)
XLA Modules:
  0.0 72.5 jit_solution(18140173514604059207)
XLA Ops:
  0.9 5.1 %collective-permute-start.3 = (f32[64,512]{1,0:T(8,128)S(1)}, f32[64,512]{1,0:T(8,128)S(1)}, u32[]{:S(2)}, u32[]{:S(2)}) collective-permute-start(f32[64,512]{1,0:T(8,128)S(1)} %dynamic-slice_bitcast_fusion), channel_id=1, source_target_pairs={{4,0},{12,8},{20,16},{28,24},{36,32},{44,40},{52,48},{60,56},{68,6... | collective-permute-start | bytes 393224 | tf_op jit(solution)/shard_map/ppermute | solution.py:376
  6.0 1.1 %collective-permute-start.2 = (s32[2,128]{1,0:T(2,128)}, s32[2,128]{1,0:T(2,128)S(1)}, u32[]{:S(2)}, u32[]{:S(2)}) collective-permute-start(s32[2,128]{1,0:T(2,128)} %bitcast.7), channel_id=1, source_target_pairs={{0,3},{1,0},{2,1},{3,2},{4,7},{5,4},{6,5},{7,6},{8,11},{9,8},{10,9... | collective-permute-start | bytes 3080 | tf_op jit(solution)/shard_map/ppermute | solution.py:365
  7.5 1.1 %stage.1 = (f32[192,128]{1,0:T(8,128)S(1)}, f32[192,128]{1,0:T(8,128)S(1)}, f32[192,128]{1,0:T(8,128)S(1)}, f32[192,128]{1,0:T(8,128)S(1)}) custom-call(f32[2,512,128]{2,1,0:T(8,128)} %rhs.1, f32[2,2,512,512]{3,2,1,0:T(8,128)} %factor.1, f32[64,512]{1,0:T(8,128)S(1)} %collective-permute-done.3.given), custom_call_target="tpu_custom_call" | custom-call | tf_op jit(solution)/shard_map/stage/pallas_call | solution.py:137
  8.6 4.5 %collective-permute-start.4 = (f32[192,128]{1,0:T(8,128)S(1)}, f32[192,128]{1,0:T(8,128)S(1)}, u32[]{:S(2)}, u32[]{:S(2)}) collective-permute-start(f32[192,128]{1,0:T(8,128)S(1)} %get-tuple-element.17), channel_id=1, source_target_pairs={{0,192},{4,196},{1,193},{5,197},{2,194},{6,198},{3,195},{7,199}} | collective-permute-start | bytes 294920 | tf_op jit(solution)/shard_map/ppermute | solution.py:379
  13.2 1.3 %collective-permute-start.5 = (f32[192,128]{1,0:T(8,128)S(1)}, f32[192,128]{1,0:T(8,128)S(1)}, u32[]{:S(2)}, u32[]{:S(2)}) collective-permute-start(f32[192,128]{1,0:T(8,128)S(1)} %get-tuple-element.18), channel_id=1, source_target_pairs={{0,128},{4,132},{1,129},{5,133},{2,130},{6,134},{3,131},{7,135}} | collective-permute-start | bytes 294920 | tf_op jit(solution)/shard_map/ppermute | solution.py:379
  14.5 1.3 %collective-permute-start.6 = (f32[192,128]{1,0:T(8,128)S(1)}, f32[192,128]{1,0:T(8,128)S(1)}, u32[]{:S(2)}, u32[]{:S(2)}) collective-permute-start(f32[192,128]{1,0:T(8,128)S(1)} %get-tuple-element.19), channel_id=1, source_target_pairs={{0,64},{4,68},{1,65},{5,69},{2,66},{6,70},{3,67},{7,71}} | collective-permute-start | bytes 294920 | tf_op jit(solution)/shard_map/ppermute | solution.py:379
  15.8 5.1 %invert.1 = (f32[3,256,256]{2,1,0:T(8,128)S(1)}, f32[1024,128]{1,0:T(8,128)S(1)}, f32[2,2,512,512]{3,2,1,0:T(8,128)S(1)}) custom-call(f32[2,512,512]{2,1,0:T(8,128)} %diag.1, f32[1024,128]{1,0:T(8,128)} %bitcast.5, f32[2,2,512,512]{3,2,1,0:T(8,128)} %factor.1), custom_call_target="tpu_custom_call" | custom-call | flops 2000000000 | bytes 4194304 | tf_op jit(solution)/shard_map/invert/pallas_call | solution.py:257
  20.9 1.9 %copy-done = f32[2,2,512,512]{3,2,1,0:T(8,128)} copy-done((f32[2,2,512,512]{3,2,1,0:T(8,128)}, f32[2,2,512,512]{3,2,1,0:T(8,128)S(1)}, u32[]{:S(2)}) %copy-start) | copy-done | bytes 4194328
  24.1 2.4 %collective-permute-done.piv1 = s32[2,128]{1,0:T(2,128)S(1)} collective-permute-done((s32[2,128]{1,0:T(2,128)S(1)}, s32[2,128]{1,0:T(2,128)S(1)}, u32[]{:S(2)}, u32[]{:S(2)}) %collective-permute-start) | collective-permute-done | bytes 1056 | tf_op jit(solution)/shard_map/ppermute | solution.py:365
  27.4 1.3 %collective-permute-start.8 = (f32[192,128]{1,0:T(8,128)S(1)}, f32[192,128]{1,0:T(8,128)S(1)}, u32[]{:S(2)}, u32[]{:S(2)}) collective-permute-start(f32[192,128]{1,0:T(8,128)S(1)} %select_select_fusion.2), channel_id=1, source_target_pairs={{0,24},{4,28},{64,88},{68,92},{128,152},{132,156},{192,216},{196,2... | collective-permute-start | bytes 294920 | tf_op jit(solution)/shard_map/ppermute | solution.py:381
  28.7 3.5 %collective-permute-start.7 = (f32[192,128]{1,0:T(8,128)S(1)}, f32[192,128]{1,0:T(8,128)S(1)}, u32[]{:S(2)}, u32[]{:S(2)}) collective-permute-start(f32[192,128]{1,0:T(8,128)S(1)} %select_select_fusion.2), channel_id=1, source_target_pairs={{0,40},{4,44},{64,104},{68,108},{128,168},{132,172},{192,232},{196... | collective-permute-start | bytes 294920 | tf_op jit(solution)/shard_map/ppermute | solution.py:381
  32.3 1.5 %collective-permute-done.7 = f32[192,128]{1,0:T(8,128)S(1)} collective-permute-done((f32[192,128]{1,0:T(8,128)S(1)}, f32[192,128]{1,0:T(8,128)S(1)}, u32[]{:S(2)}, u32[]{:S(2)}) %collective-permute-start.7) | collective-permute-done | bytes 98336 | tf_op jit(solution)/shard_map/ppermute | solution.py:381
  33.8 1.3 %collective-permute-start.10 = (f32[192,128]{1,0:T(8,128)S(1)}, f32[192,128]{1,0:T(8,128)S(1)}, u32[]{:S(2)}, u32[]{:S(2)}) collective-permute-start(f32[192,128]{1,0:T(8,128)S(1)} %select_select_fusion.1), channel_id=1, source_target_pairs={{0,8},{4,12},{64,72},{68,76},{128,136},{132,140},{192,200},{196,20... | collective-permute-start | bytes 294920 | tf_op jit(solution)/shard_map/ppermute | solution.py:384
  35.1 1.3 %collective-permute-start.9 = (f32[192,128]{1,0:T(8,128)S(1)}, f32[192,128]{1,0:T(8,128)S(1)}, u32[]{:S(2)}, u32[]{:S(2)}) collective-permute-start(f32[192,128]{1,0:T(8,128)S(1)} %select_select_fusion.1), channel_id=1, source_target_pairs={{0,56},{4,60},{64,120},{68,124},{128,184},{132,188},{192,248},{196... | collective-permute-start | bytes 294920 | tf_op jit(solution)/shard_map/ppermute | solution.py:384
  36.8 1.3 %collective-permute-done.9 = f32[192,128]{1,0:T(8,128)S(1)} collective-permute-done((f32[192,128]{1,0:T(8,128)S(1)}, f32[192,128]{1,0:T(8,128)S(1)}, u32[]{:S(2)}, u32[]{:S(2)}) %collective-permute-start.9) | collective-permute-done | bytes 98336 | tf_op jit(solution)/shard_map/ppermute | solution.py:384
  38.1 2.6 %collective-permute-start.20 = (f32[64,128]{1,0:T(8,128)S(1)}, f32[64,128]{1,0:T(8,128)S(1)}, u32[]{:S(2)}, u32[]{:S(2)}) collective-permute-start(f32[64,128]{1,0:T(8,128)S(1)} %get-tuple-element.23), channel_id=1, source_target_pairs={{0,192},{4,196},{8,200},{12,204},{16,208},{20,212},{24,216},{28,22... | collective-permute-start | bytes 98312 | tf_op jit(solution)/shard_map/ppermute | solution.py:365
  41.8 1.6 %collective-permute-done.13 = f32[96,128]{1,0:T(8,128)S(1)} collective-permute-done((f32[96,128]{1,0:T(8,128)S(1)}, f32[96,128]{1,0:T(8,128)S(1)}, u32[]{:S(2)}, u32[]{:S(2)}) %collective-permute-start.13) | collective-permute-done | bytes 49184 | tf_op jit(solution)/shard_map/ppermute | solution.py:390
  43.4 2.5 %collective-permute-start.16 = (f32[320,128]{1,0:T(8,128)S(1)}, f32[320,128]{1,0:T(8,128)S(1)}, u32[]{:S(2)}, u32[]{:S(2)}) collective-permute-start(f32[320,128]{1,0:T(8,128)S(1)} %constant_dynamic-update-slice_fusion), channel_id=1, source_target_pairs={{0,192},{4,196},{8,200},{12,204},{16,208},{20,212},{24,216},{28,22... | collective-permute-start | bytes 491528 | tf_op jit(solution)/shard_map/ppermute | solution.py:365
  47.4 5.9 %collective-permute-done.14 = f32[320,128]{1,0:T(8,128)S(1)} collective-permute-done((f32[320,128]{1,0:T(8,128)S(1)}, f32[320,128]{1,0:T(8,128)S(1)}, u32[]{:S(2)}, u32[]{:S(2)}) %collective-permute-start.14) | collective-permute-done | bytes 163872 | tf_op jit(solution)/shard_map/ppermute | solution.py:365
  53.4 1.4 %collective-permute-start.22 = (f32[256,128]{1,0:T(8,128)S(1)}, f32[256,128]{1,0:T(8,128)S(1)}, u32[]{:S(2)}, u32[]{:S(2)}) collective-permute-start(f32[256,128]{1,0:T(8,128)S(1)} %pad_maximum_fusion), channel_id=1, source_target_pairs={{0,2},{1,3},{2,0},{3,1},{4,6},{5,7},{6,4},{7,5},{8,10},{9,11},{10,... | collective-permute-start | bytes 393224 | tf_op jit(solution)/shard_map/ppermute | solution.py:365
  55.0 5.2 %collective-permute-start.17 = (f32[1280,128]{1,0:T(8,128)S(1)}, f32[1280,128]{1,0:T(8,128)S(1)}, u32[]{:S(2)}, u32[]{:S(2)}) collective-permute-start(f32[1280,128]{1,0:T(8,128)S(1)} %slice_dynamic-update-slice_fusion.rows_own), channel_id=1, source_target_pairs={{0,4},{4,0},{8,12},{12,8},{16,20},{20,16},{24,28},{28,24},{32,36},... | collective-permute-start | bytes 1966088 | tf_op jit(solution)/shard_map/ppermute | solution.py:396
  60.3 6.0 %collective-permute-start.24 = (f32[1024,128]{1,0:T(8,128)S(1)}, f32[1024,128]{1,0:T(8,128)S(1)}, u32[]{:S(2)}, u32[]{:S(2)}) collective-permute-start(f32[1024,128]{1,0:T(8,128)S(1)} %constant_dynamic-update-slice_fusion.8.factor_own), channel_id=1, source_target_pairs={{0,4},{4,0},{8,12},{12,8},{16,20},{20,16},{24,28},{28,24},{32,36},... | collective-permute-start | bytes 1572872 | tf_op jit(solution)/shard_map/ppermute | solution.py:397
  66.3 1.5 %collective-permute-done.24.factor_other = f32[1024,128]{1,0:T(8,128)S(1)} collective-permute-done((f32[1024,128]{1,0:T(8,128)S(1)}, f32[1024,128]{1,0:T(8,128)S(1)}, u32[]{:S(2)}, u32[]{:S(2)}) %collective-permute-start.24) | collective-permute-done | bytes 524320 | tf_op jit(solution)/shard_map/ppermute | solution.py:397
  67.8 4.5 %finish.1 = f32[1024,128]{1,0:T(8,128)} custom-call(s32[16,128]{1,0:T(8,128)S(1)} %get-tuple-element.14.table, f32[1024,128]{1,0:T(8,128)S(1)} %get-tuple-element.15.kept, f32[2,2,512,512]{3,2,1,0:T(8,128)S(1)} %copy-done.1, f32[1280,128]{1,0:T(8,128)S(1)} %slice_dynamic-update-slice_fusion.rows_own, f32[1280,128]{1,0:T(8,128)S(1)} %collective-permute-done.17.rows_other, ...), custom_call_target="tpu_custom_call" | custom-call | tf_op jit(solution)/shard_map/finish/pallas_call | solution.py:346
  (69 shorter events, 6.6 us)
Async XLA Ops:
  0.9 6.6 %collective-permute-start.3 = (f32[64,512]{1,0:T(8,128)S(1)}, f32[64,512]{1,0:T(8,128)S(1)}, u32[]{:S(2)}, u32[]{:S(2)}) collective-permute-start(f32[64,512]{1,0:T(8,128)S(1)} %dynamic-slice_bitcast_fusion), channel_id=1, source_target_pairs={{4,0},{12,8},{20,16},{28,24},{36,32},{44,40},{52,48},{60,56},{68,6... | collective-permute-start | bytes 393224 | tf_op jit(solution)/shard_map/ppermute | solution.py:376
  6.0 16.8 %collective-permute-start.2 = (s32[2,128]{1,0:T(2,128)}, s32[2,128]{1,0:T(2,128)S(1)}, u32[]{:S(2)}, u32[]{:S(2)}) collective-permute-start(s32[2,128]{1,0:T(2,128)} %bitcast.7), channel_id=1, source_target_pairs={{0,3},{1,0},{2,1},{3,2},{4,7},{5,4},{6,5},{7,6},{8,11},{9,8},{10,9... | collective-permute-start | bytes 3080 | tf_op jit(solution)/shard_map/ppermute | solution.py:365
  7.1 16.4 %collective-permute-start.1 = (s32[2,128]{1,0:T(2,128)}, s32[2,128]{1,0:T(2,128)S(1)}, u32[]{:S(2)}, u32[]{:S(2)}) collective-permute-start(s32[2,128]{1,0:T(2,128)} %bitcast.8), channel_id=1, source_target_pairs={{0,2},{1,3},{2,0},{3,1},{4,6},{5,7},{6,4},{7,5},{8,10},{9,11},{10,... | collective-permute-start | bytes 3080 | tf_op jit(solution)/shard_map/ppermute | solution.py:365
  8.6 18.7 %collective-permute-start.4 = (f32[192,128]{1,0:T(8,128)S(1)}, f32[192,128]{1,0:T(8,128)S(1)}, u32[]{:S(2)}, u32[]{:S(2)}) collective-permute-start(f32[192,128]{1,0:T(8,128)S(1)} %get-tuple-element.17), channel_id=1, source_target_pairs={{0,192},{4,196},{1,193},{5,197},{2,194},{6,198},{3,195},{7,199}} | collective-permute-start | bytes 294920 | tf_op jit(solution)/shard_map/ppermute | solution.py:379
  13.2 14.2 %collective-permute-start.5 = (f32[192,128]{1,0:T(8,128)S(1)}, f32[192,128]{1,0:T(8,128)S(1)}, u32[]{:S(2)}, u32[]{:S(2)}) collective-permute-start(f32[192,128]{1,0:T(8,128)S(1)} %get-tuple-element.18), channel_id=1, source_target_pairs={{0,128},{4,132},{1,129},{5,133},{2,130},{6,134},{3,131},{7,135}} | collective-permute-start | bytes 294920 | tf_op jit(solution)/shard_map/ppermute | solution.py:379
  14.5 12.9 %collective-permute-start.6 = (f32[192,128]{1,0:T(8,128)S(1)}, f32[192,128]{1,0:T(8,128)S(1)}, u32[]{:S(2)}, u32[]{:S(2)}) collective-permute-start(f32[192,128]{1,0:T(8,128)S(1)} %get-tuple-element.19), channel_id=1, source_target_pairs={{0,64},{4,68},{1,65},{5,69},{2,66},{6,70},{3,67},{7,71}} | collective-permute-start | bytes 294920 | tf_op jit(solution)/shard_map/ppermute | solution.py:379
  22.9 3.6 %collective-permute-start = (s32[2,128]{1,0:T(2,128)S(1)}, s32[2,128]{1,0:T(2,128)S(1)}, u32[]{:S(2)}, u32[]{:S(2)}) collective-permute-start(s32[2,128]{1,0:T(2,128)S(1)} %bitcast.9), channel_id=1, source_target_pairs={{0,1},{1,2},{2,3},{3,0},{4,5},{5,6},{6,7},{7,4},{8,9},{9,10},{10,1... | collective-permute-start | bytes 3080 | tf_op jit(solution)/shard_map/ppermute | solution.py:365
  23.6 42.7 %collective-permute-start.25 = (f32[3,256,256]{2,1,0:T(8,128)S(1)}, f32[3,256,256]{2,1,0:T(8,128)S(1)}, u32[]{:S(2)}, u32[]{:S(2)}) collective-permute-start(f32[3,256,256]{2,1,0:T(8,128)S(1)} %get-tuple-element.22.inv_own), channel_id=1, source_target_pairs={{0,4},{4,0},{8,12},{12,8},{16,20},{20,16},{24,28},{28,24},{32,36},... | collective-permute-start | bytes 2359304 | tf_op jit(solution)/shard_map/ppermute | solution.py:399
  27.3 4.9 %collective-permute-start.11 = (f32[24,128]{1,0:T(8,128)S(1)}, f32[24,128]{1,0:T(8,128)S(1)}, u32[]{:S(2)}, u32[]{:S(2)}) collective-permute-start(f32[24,128]{1,0:T(8,128)S(1)} %get-tuple-element.21), channel_id=1, source_target_pairs={{0,8},{4,12},{8,0},{12,4},{16,24},{20,28},{24,16},{28,20},{32,40},... | collective-permute-start | bytes 36872 | tf_op jit(solution)/shard_map/ppermute | solution.py:390
  27.4 4.9 %collective-permute-start.8 = (f32[192,128]{1,0:T(8,128)S(1)}, f32[192,128]{1,0:T(8,128)S(1)}, u32[]{:S(2)}, u32[]{:S(2)}) collective-permute-start(f32[192,128]{1,0:T(8,128)S(1)} %select_select_fusion.2), channel_id=1, source_target_pairs={{0,24},{4,28},{64,88},{68,92},{128,152},{132,156},{192,216},{196,2... | collective-permute-start | bytes 294920 | tf_op jit(solution)/shard_map/ppermute | solution.py:381
  28.7 5.1 %collective-permute-start.7 = (f32[192,128]{1,0:T(8,128)S(1)}, f32[192,128]{1,0:T(8,128)S(1)}, u32[]{:S(2)}, u32[]{:S(2)}) collective-permute-start(f32[192,128]{1,0:T(8,128)S(1)} %select_select_fusion.2), channel_id=1, source_target_pairs={{0,40},{4,44},{64,104},{68,108},{128,168},{132,172},{192,232},{196... | collective-permute-start | bytes 294920 | tf_op jit(solution)/shard_map/ppermute | solution.py:381
  32.2 4.2 %collective-permute-start.12 = (f32[48,128]{1,0:T(8,128)S(1)}, f32[48,128]{1,0:T(8,128)S(1)}, u32[]{:S(2)}, u32[]{:S(2)}) collective-permute-start(f32[48,128]{1,0:T(8,128)S(1)} %pad_maximum_fusion.2), channel_id=1, source_target_pairs={{0,16},{4,20},{8,24},{12,28},{16,0},{20,4},{24,8},{28,12},{32,48},... | collective-permute-start | bytes 73736 | tf_op jit(solution)/shard_map/ppermute | solution.py:390
  36.5 6.9 %collective-permute-start.13 = (f32[96,128]{1,0:T(8,128)S(1)}, f32[96,128]{1,0:T(8,128)S(1)}, u32[]{:S(2)}, u32[]{:S(2)}) collective-permute-start(f32[96,128]{1,0:T(8,128)S(1)} %pad_maximum_fusion.1), channel_id=1, source_target_pairs={{0,32},{4,36},{8,40},{12,44},{16,48},{20,52},{24,56},{28,60},{32,0... | collective-permute-start | bytes 147464 | tf_op jit(solution)/shard_map/ppermute | solution.py:390
  38.1 7.8 %collective-permute-start.20 = (f32[64,128]{1,0:T(8,128)S(1)}, f32[64,128]{1,0:T(8,128)S(1)}, u32[]{:S(2)}, u32[]{:S(2)}) collective-permute-start(f32[64,128]{1,0:T(8,128)S(1)} %get-tuple-element.23), channel_id=1, source_target_pairs={{0,192},{4,196},{8,200},{12,204},{16,208},{20,212},{24,216},{28,22... | collective-permute-start | bytes 98312 | tf_op jit(solution)/shard_map/ppermute | solution.py:365
  40.7 5.7 %collective-permute-start.19 = (f32[64,128]{1,0:T(8,128)S(1)}, f32[64,128]{1,0:T(8,128)S(1)}, u32[]{:S(2)}, u32[]{:S(2)}) collective-permute-start(f32[64,128]{1,0:T(8,128)S(1)} %get-tuple-element.23), channel_id=1, source_target_pairs={{0,128},{4,132},{8,136},{12,140},{16,144},{20,148},{24,152},{28,15... | collective-permute-start | bytes 98312 | tf_op jit(solution)/shard_map/ppermute | solution.py:365
  41.2 5.8 %collective-permute-start.18 = (f32[64,128]{1,0:T(8,128)S(1)}, f32[64,128]{1,0:T(8,128)S(1)}, u32[]{:S(2)}, u32[]{:S(2)}) collective-permute-start(f32[64,128]{1,0:T(8,128)S(1)} %get-tuple-element.23), channel_id=1, source_target_pairs={{0,64},{4,68},{8,72},{12,76},{16,80},{20,84},{24,88},{28,92},{32,9... | collective-permute-start | bytes 98312 | tf_op jit(solution)/shard_map/ppermute | solution.py:365
  43.4 11.5 %collective-permute-start.16 = (f32[320,128]{1,0:T(8,128)S(1)}, f32[320,128]{1,0:T(8,128)S(1)}, u32[]{:S(2)}, u32[]{:S(2)}) collective-permute-start(f32[320,128]{1,0:T(8,128)S(1)} %constant_dynamic-update-slice_fusion), channel_id=1, source_target_pairs={{0,192},{4,196},{8,200},{12,204},{16,208},{20,212},{24,216},{28,22... | collective-permute-start | bytes 491528 | tf_op jit(solution)/shard_map/ppermute | solution.py:365
  45.9 8.8 %collective-permute-start.15 = (f32[320,128]{1,0:T(8,128)S(1)}, f32[320,128]{1,0:T(8,128)S(1)}, u32[]{:S(2)}, u32[]{:S(2)}) collective-permute-start(f32[320,128]{1,0:T(8,128)S(1)} %constant_dynamic-update-slice_fusion), channel_id=1, source_target_pairs={{0,128},{4,132},{8,136},{12,140},{16,144},{20,148},{24,152},{28,15... | collective-permute-start | bytes 491528 | tf_op jit(solution)/shard_map/ppermute | solution.py:365
  46.4 6.9 %collective-permute-start.14 = (f32[320,128]{1,0:T(8,128)S(1)}, f32[320,128]{1,0:T(8,128)S(1)}, u32[]{:S(2)}, u32[]{:S(2)}) collective-permute-start(f32[320,128]{1,0:T(8,128)S(1)} %constant_dynamic-update-slice_fusion), channel_id=1, source_target_pairs={{0,64},{4,68},{8,72},{12,76},{16,80},{20,84},{24,88},{28,92},{32,9... | collective-permute-start | bytes 491528 | tf_op jit(solution)/shard_map/ppermute | solution.py:365
  47.0 13.2 %collective-permute-start.23 = (f32[256,128]{1,0:T(8,128)S(1)}, f32[256,128]{1,0:T(8,128)S(1)}, u32[]{:S(2)}, u32[]{:S(2)}) collective-permute-start(f32[256,128]{1,0:T(8,128)S(1)} %pad_maximum_fusion), channel_id=1, source_target_pairs={{0,3},{1,0},{2,1},{3,2},{4,7},{5,4},{6,5},{7,6},{8,11},{9,8},{10,9... | collective-permute-start | bytes 393224 | tf_op jit(solution)/shard_map/ppermute | solution.py:365
  53.4 6.8 %collective-permute-start.22 = (f32[256,128]{1,0:T(8,128)S(1)}, f32[256,128]{1,0:T(8,128)S(1)}, u32[]{:S(2)}, u32[]{:S(2)}) collective-permute-start(f32[256,128]{1,0:T(8,128)S(1)} %pad_maximum_fusion), channel_id=1, source_target_pairs={{0,2},{1,3},{2,0},{3,1},{4,6},{5,7},{6,4},{7,5},{8,10},{9,11},{10,... | collective-permute-start | bytes 393224 | tf_op jit(solution)/shard_map/ppermute | solution.py:365
  54.8 5.4 %collective-permute-start.21 = (f32[256,128]{1,0:T(8,128)S(1)}, f32[256,128]{1,0:T(8,128)S(1)}, u32[]{:S(2)}, u32[]{:S(2)}) collective-permute-start(f32[256,128]{1,0:T(8,128)S(1)} %pad_maximum_fusion), channel_id=1, source_target_pairs={{0,1},{1,2},{2,3},{3,0},{4,5},{5,6},{6,7},{7,4},{8,9},{9,10},{10,1... | collective-permute-start | bytes 393224 | tf_op jit(solution)/shard_map/ppermute | solution.py:365
  55.0 12.8 %collective-permute-start.17 = (f32[1280,128]{1,0:T(8,128)S(1)}, f32[1280,128]{1,0:T(8,128)S(1)}, u32[]{:S(2)}, u32[]{:S(2)}) collective-permute-start(f32[1280,128]{1,0:T(8,128)S(1)} %slice_dynamic-update-slice_fusion.rows_own), channel_id=1, source_target_pairs={{0,4},{4,0},{8,12},{12,8},{16,20},{20,16},{24,28},{28,24},{32,36},... | collective-permute-start | bytes 1966088 | tf_op jit(solution)/shard_map/ppermute | solution.py:396
  60.3 7.6 %collective-permute-start.24 = (f32[1024,128]{1,0:T(8,128)S(1)}, f32[1024,128]{1,0:T(8,128)S(1)}, u32[]{:S(2)}, u32[]{:S(2)}) collective-permute-start(f32[1024,128]{1,0:T(8,128)S(1)} %constant_dynamic-update-slice_fusion.8.factor_own), channel_id=1, source_target_pairs={{0,4},{4,0},{8,12},{12,8},{16,20},{20,16},{24,28},{28,24},{32,36},... | collective-permute-start | bytes 1572872 | tf_op jit(solution)/shard_map/ppermute | solution.py:397
  (6 other events, 84.2 us)
